TPU v7x, 32 devices: a whole 2x2x4 slice. The times are simulated.
32 devices in a mesh: groups: 2 (over y), dp: 8 (over z, core), expert: 2 (over x).
Axes of the slice: x: 2, y: 2, z: 4, core: 2. Of those that a mesh axis runs over, the one named last changes fastest.
Arguments:
- queries: bfloat16 [2, 256, 32, 128], P(None, ('groups', 'dp'), 'expert'), parts along dimension 1, may hold values from -6 to 6
- fresh_kv: bfloat16 [2, 256, 4, 256], P(None, ('groups', 'dp'), 'expert'), parts along dimension 1, may hold values from -6 to 6
- kv_pool: bfloat16 [5120, 16, 4, 256], P(('groups', 'dp'), None, 'expert'), parts along dimension 0, may hold values from -6 to 6
- page_table: int32 [256, 305], P(('groups', 'dp')), parts along dimension 0, may hold values from -1 to 319, as said below
- context_lengths: int32 [256], P(('groups', 'dp')), parts along dimension 0, may hold values from 1 to 4880, as said below
- residual: bfloat16 [2, 256, 4096], P(None, ('groups', 'dp'), 'expert'), parts along dimension 1, may hold values from -16 to 16
- out_weight: bfloat16 [4096, 4096], P('expert', 'dp'), may hold values from -0.09375 to 0.09375
- norm_gain: float32 [4096], P('expert'), may hold values from 0.1 to 1.9
- expert_ids: int32 [2, 256, 8], P(None, ('groups', 'dp')), parts along dimension 1, may hold values from 0 to 15, all different within a row; in each aligned block of 16 rows (0 to 15, 16 to 31, ..., all dimensions but the last counted through in order) at most 16 rows name the same one
- route_weights: float32 [2, 256, 8], P(None, ('groups', 'dp')), parts along dimension 1, may hold values from 0.1 to 1
- gate_up: bfloat16 [16, 2, 4096, 768], P('dp', None, 'expert'), may hold values from -0.09375 to 0.09375
- down_proj: bfloat16 [16, 768, 4096], P('dp', None, 'expert'), may hold values from -0.21875 to 0.21875
Outputs:
- layer_out: bfloat16 [2, 256, 4096], P(None, ('groups', 'dp'), 'expert'), parts along dimension 1
There are 2 independent parts, one for each index of `groups`. A program takes and returns all parts, laid end to end along the dimension named above; an argument that names none is the same for every part. Nothing has to cross between parts.
Inputs may be any that keep to these rules, and one draw needn't show every extreme that they name: `page_table`: entries 0 to ceil(context_lengths[i] / 16) - 1 of a row name distinct pages, no page is named twice within the 16 requests of one block, and later entries are -1. The requests of one block hold at most 320 pages together; in every draw some block holds exactly 320, and some request holds exactly 305 pages. `context_lengths`: every request holds at least one cached token; in every draw some request holds exactly 4880. `expert_ids`: within the rows of one device (16 requests of one step) no expert is named by more than 16 rows.
All inputs are finite; a program needn't handle non-finite values.
Results may differ from a plain program's by a relative error of at most 0.005.
Values may be sent and summed in bfloat16 or wider, within the bound.
No kernel may reach another device: no remote copies, remote signals or barrier semaphores. Data moves between devices by JAX's collectives and lax.ppermute only.
A program may use at most 64 MiB of HBM per device.

v0:
```python
import math

import jax
import jax.numpy as jnp
from jax import lax
from jax.sharding import PartitionSpec as P

NEG = -1e30
EPS = 1e-06
EXACT = lax.Precision.HIGHEST


def page_owners(table, lengths, pool_pages, page_len):
    pages = jnp.arange(pool_pages, dtype=jnp.int32)
    matches = table[:, :, None] == pages[None, None, :]
    ownership = jnp.any(matches, axis=1)
    slot_index = jnp.arange(table.shape[1], dtype=jnp.int32)
    position = jnp.sum(jnp.where(matches, slot_index[None, :, None], 0), axis=(0, 1))
    owner_length = jnp.sum(jnp.where(ownership, lengths[:, None], 0), axis=0)
    live_count = jnp.clip(owner_length - position * page_len, 0, page_len)
    return (ownership, live_count)


def attend(query_block, fresh_block, pool_block, table_block, length_block):
    step_count, req_count, head_count, head_width = query_block.shape
    pool_pages, page_len, kv_heads, _ = pool_block.shape
    group_size = head_count // kv_heads
    score_scale = 1.0 / math.sqrt(head_width)
    ownership, live_count = page_owners(table_block, length_block, pool_pages, page_len)
    owned_f = ownership.astype(jnp.float32)
    grouped = query_block.reshape(step_count, req_count, kv_heads, group_size, head_width)
    page_query = jnp.einsum(
        "rp,srkgd->pskgd",
        ownership.astype(jnp.bfloat16),
        grouped,
        preferred_element_type=jnp.float32,
    ).astype(jnp.bfloat16)
    key_rows = pool_block[..., :head_width]
    value_rows = pool_block[..., head_width:]
    page_scores = (
        jnp.einsum("pskgd,ptkd->pskgt", page_query, key_rows, preferred_element_type=jnp.float32)
        * score_scale
    )
    in_page = jnp.arange(page_len)[None, :] < live_count[:, None]
    page_scores = jnp.where(in_page[:, None, None, None, :], page_scores, NEG)
    fresh_keys = fresh_block[..., :head_width]
    fresh_values = fresh_block[..., head_width:]
    fresh_scores = (
        jnp.einsum("srkgd,urkd->srkgu", grouped, fresh_keys, preferred_element_type=jnp.float32)
        * score_scale
    )
    causal = jnp.arange(step_count)[:, None] >= jnp.arange(step_count)[None, :]
    fresh_scores = jnp.where(causal[:, None, None, None, :], fresh_scores, NEG)
    page_best = jnp.max(page_scores, axis=4)
    row_best = jnp.max(jnp.where(ownership[:, :, None, None, None], page_best[None], NEG), axis=1)
    row_best = jnp.maximum(row_best, jnp.moveaxis(jnp.max(fresh_scores, axis=4), 0, 1))
    owner_best = jnp.einsum("rp,rskg->pskg", owned_f, row_best, precision=EXACT)
    page_probs = jnp.exp(page_scores - owner_best[..., None])
    page_sum = jnp.sum(page_probs, axis=4)
    page_acc = jnp.einsum(
        "pskgt,ptkd->pskgd",
        page_probs.astype(jnp.bfloat16),
        value_rows,
        preferred_element_type=jnp.float32,
    )
    denominator = jnp.einsum("rp,pskg->rskg", owned_f, page_sum, precision=EXACT)
    numerator = jnp.einsum("rp,pskgd->rskgd", owned_f, page_acc, precision=EXACT)
    fresh_probs = jnp.exp(fresh_scores - jnp.moveaxis(row_best, 1, 0)[..., None])
    denominator = denominator + jnp.moveaxis(jnp.sum(fresh_probs, axis=4), 0, 1)
    numerator = numerator + jnp.einsum(
        "srkgu,urkd->rskgd",
        fresh_probs.astype(jnp.bfloat16),
        fresh_values,
        preferred_element_type=jnp.float32,
    )
    attended = jnp.moveaxis(numerator / denominator[..., None], 1, 0)
    return attended.reshape(step_count, req_count, head_count * head_width).astype(jnp.bfloat16)


def dispatch_keys(expert_ids, expert_total, local_experts, dp_count, capacity):
    step_count = expert_ids.shape[0]
    catalog = jnp.arange(expert_total, dtype=jnp.int32)
    named_mask = jnp.any(expert_ids[..., None] == catalog, axis=2).astype(jnp.int32)
    earlier = jnp.cumsum(named_mask, axis=1) - named_mask
    slot_rank = jnp.take_along_axis(earlier, expert_ids, axis=2)
    owner_index = expert_ids // local_experts
    local_index = expert_ids % local_experts
    step_index = jnp.arange(step_count, dtype=jnp.int32)[:, None, None]
    return ((local_index * dp_count + owner_index) * step_count + step_index) * capacity + slot_rank


def body(
    queries,
    fresh_kv,
    kv_pool,
    page_table,
    context_lengths,
    residual,
    out_weight,
    norm_gain,
    expert_ids,
    route_weights,
    gate_up,
    down_proj,
):
    attended = attend(queries, fresh_kv, kv_pool, page_table, context_lengths)
    step_count, req_count, head_cols = attended.shape
    every_request = lax.all_gather(attended, "dp", axis=1, tiled=True)
    local_columns = jnp.einsum(
        "srh,hc->src", every_request, out_weight, preferred_element_type=jnp.float32
    )
    regrouped = lax.all_to_all(
        local_columns.astype(jnp.bfloat16), "dp", split_axis=1, concat_axis=2, tiled=True
    ).astype(local_columns.dtype)
    partial_out = regrouped.reshape(step_count * req_count, regrouped.shape[2])
    projected = lax.psum_scatter(
        partial_out.astype(jnp.bfloat16), "expert", scatter_dimension=1, tiled=True
    ).astype(jnp.float32)
    quarter = projected.shape[1]
    stream = residual.astype(jnp.float32).reshape(step_count * req_count, quarter) + projected
    squares = lax.psum(jnp.sum(stream * stream, axis=1), "expert")
    model_width = quarter * lax.axis_size("expert")
    inverse = lax.rsqrt(squares / model_width + EPS)
    normed = (stream * inverse[:, None] * norm_gain[None, :]).astype(jnp.bfloat16)
    dp_count = lax.axis_size("dp")
    local_experts = gate_up.shape[0]
    expert_total = local_experts * dp_count
    top_count = expert_ids.shape[2]
    capacity = min(
        req_count, max(2, (5 * req_count * top_count + 2 * expert_total - 1) // (2 * expert_total))
    )
    slot_keys = dispatch_keys(expert_ids, expert_total, local_experts, dp_count, capacity)
    slot_total = local_experts * dp_count * step_count * capacity
    slot_ids = jnp.arange(slot_total, dtype=jnp.int32)
    chosen = slot_keys.reshape(step_count * req_count, top_count)[None] == slot_ids[:, None, None]
    selector = jnp.any(chosen, axis=2).astype(jnp.bfloat16)
    outgoing = jnp.dot(selector, normed, preferred_element_type=jnp.float32).astype(jnp.bfloat16)
    outgoing = outgoing.reshape(local_experts, dp_count, step_count * capacity, quarter)
    incoming = lax.all_to_all(outgoing, "dp", split_axis=1, concat_axis=1, tiled=True)
    expert_rows = incoming.reshape(local_experts, dp_count * step_count * capacity, quarter)
    gate_part = jnp.einsum(
        "jmd,jdh->jmh", expert_rows, gate_up[:, 0], preferred_element_type=jnp.float32
    )
    up_part = jnp.einsum(
        "jmd,jdh->jmh", expert_rows, gate_up[:, 1], preferred_element_type=jnp.float32
    )
    gate_share, up_share = (
        lax.psum_scatter(gate_part, "expert", scatter_dimension=2, tiled=True),
        lax.psum_scatter(up_part, "expert", scatter_dimension=2, tiled=True),
    )
    active_share = (jax.nn.silu(gate_share) * up_share).astype(jnp.bfloat16)
    activated = lax.all_gather(active_share, "expert", axis=2, tiled=True)
    expert_out = jnp.einsum(
        "jmh,jhd->jmd", activated, down_proj, preferred_element_type=jnp.float32
    ).astype(jnp.bfloat16)
    expert_out = expert_out.reshape(local_experts, dp_count, step_count * capacity, quarter)
    returned = lax.all_to_all(expert_out, "dp", split_axis=1, concat_axis=1, tiled=True)
    returned = returned.reshape(slot_total, quarter)
    picked = returned[slot_keys].astype(jnp.float32)
    share = route_weights / jnp.sum(route_weights, axis=2, keepdims=True)
    mixture = jnp.sum(share[..., None] * picked, axis=2)
    return (stream.reshape(step_count, req_count, quarter) + mixture).astype(jnp.bfloat16)


def solution(mesh):
    return jax.shard_map(
        body,
        mesh=mesh,
        in_specs=(
            P(None, ("groups", "dp"), "expert", None),
            P(None, ("groups", "dp"), "expert", None),
            P(("groups", "dp"), None, "expert", None),
            P(("groups", "dp"), None),
            P(("groups", "dp")),
            P(None, ("groups", "dp"), "expert"),
            P("expert", "dp"),
            P("expert"),
            P(None, ("groups", "dp"), None),
            P(None, ("groups", "dp"), None),
            P("dp", None, "expert", None),
            P("dp", None, "expert"),
        ),
        out_specs=P(None, ("groups", "dp"), "expert"),
        check_vma=False,
    )
```

profile of v0, /device:TPU:0, one launch (start us, length us, event | category | flops | bytes accessed | tf_op | source)
XLA Modules:
  0.0 309.8 jit_solution(3611511401167732488)
XLA Ops:
  6.5 1.0 copy.113
  7.5 1.2 fusion
  8.7 1.5 select_reduce_fusion
  10.2 0.7 select_reduce_fusion.2
  11.1 1.8 convolution_convert_fusion.2
  12.9 7.0 %fusion.69 = (bf16[320,16,2,128]{3,2,1,0:T(2,128)(2,1)S(1)}, bf16[320,16,2,128]{3,2,1,0:T(2,128)(2,1)}) fusion(bf16[320,16,2,256]{3,2,1,0:T(2,128)(2,1)} %param.14), kind=kLoop, calls=%fused_computation.98 | loop fusion | bytes 10485760 | tf_op jit(solution)/shard_map/slice | solution.py:38
  19.8 5.3 %bitcast_reduce_fusion = (f32[320,2,2,8]{3,1,2,0:T(2,128)S(1)}, f32[320,2,2,8,16]{4,3,2,1,0:T(8,128)}) fusion(pred[320,16]{1,0:T(8,128)(4,1)S(1)} %iota_compare_fusion.2, bf16[320,16,2,128]{3,2,1,0:T(2,128)(2,1)S(1)} %get-tuple-element.7, bf16[320,2,2,8,128]{4,0,3,2,1:T(8,128)(2,1)S(1)} %convolution_convert_fusion.2), kind=kOutput, calls=%fused_computation.12 | convolution fusion | flops 42424320 | bytes 5944320 | tf_op jit(solution)/shard_map/pskgd,ptkd->pskgt/dot_general | solution.py:41
  25.1 0.4 copy.117
  25.5 0.2 select_reduce_fusion.1
  25.7 0.6 fusion.70
  26.4 0.7 fusion.71
  27.5 0.4 copy.122
  27.8 8.9 %fusion.10 = f32[320,2,2,8]{3,1,2,0:T(2,128)S(1)} fusion(f32[320,2,2,8,16]{4,3,2,1,0:T(8,128)} %get-tuple-element.14, f32[320,2,2,8]{3,1,2,0:T(2,128)S(1)} %copy.122, pred[320,16]{1,0:T(8,128)(4,1)S(1)} %iota_compare_fusion.2), kind=kLoop, calls=%fused_computation.17 | loop fusion | flops 645120 | bytes 742400 | tf_op jit(solution)/shard_map/reduce_sum | solution.py:59
  36.8 1.0 copy.130
  37.8 0.9 fusion.73
  39.1 4.4 %fusion.20 = f32[320,2,2,8,128]{4,3,1,2,0:T(8,128)S(1)} fusion(bf16[320,16,2,128]{3,2,1,0:T(2,128)(2,1)} %get-tuple-element.8, f32[320,2,2,8,16]{4,3,2,1,0:T(8,128)} %get-tuple-element.14, f32[320,2,2,8]{3,1,2,0:T(2,128)S(1)} %copy.122, pred[320,16]{1,0:T(8,128)(4,1)S(1)} %iota_compare_fusion.2), kind=kOutput, calls=%fused_computation.30 | convolution fusion | flops 42598400 | bytes 8565760 | tf_op jit(solution)/shard_map/pskgt,ptkd->pskgd/dot_general | solution.py:60
  43.5 0.2 fusion.51
  43.8 4.9 %fusion.38 = bf16[2,16,2,8,128]{4,1,3,2,0:T(8,128)(2,1)S(1)} fusion(f32[320,2,2,8,128]{4,3,1,2,0:T(8,128)S(1)} %fusion.20, f32[16,2,2,8,128]{4,3,2,1,0:T(8,128)S(1)} %fusion.51, f32[2,16,2,8]{1,3,2,0:T(8,128)S(1)} %add.66, pred[16,320]{1,0:T(8,128)(4,1)S(1)} %fusion), kind=kOutput, calls=%fused_computation.40 | convolution fusion | flops 251854848 | bytes 5643264 | tf_op jit(solution)/shard_map/rp,pskgd->rskgd/dot_general | solution.py:67
  48.7 0.7 convert_element_type.53
  49.5 25.1 %all-gather.2.cloned.1.call-done = bf16[2,128,2048]{2,1,0:T(8,128)(2,1)} async-done(((bf16[2,16,2048]{2,1,0:T(8,128)(2,1)}), bf16[2,128,2048]{2,1,0:T(8,128)(2,1)}) %all-gather.2.cloned.1.call-update) | async-done | bytes 1048592 | tf_op jit(solution)/shard_map/all_gather | solution.py:108
  74.6 1.9 fusion.26
  76.5 1.0 copy.133
  77.5 3.4 %all-to-all-start = ((bf16[2,128,512]{2,0,1:T(2,128)(2,1)}), bf16[2,128,512]{2,0,1:T(2,128)(2,1)S(1)}, u32[]{:S(2)}, u32[]{:S(2)}) async-start(bf16[2,128,512]{2,0,1:T(2,128)(2,1)} %copy.133), calls=%async_computation | async-start | bytes 524288 | tf_op jit(solution)/shard_map/all_to_all | solution.py:112
  81.3 9.2 %all-to-all-done = bf16[2,128,512]{2,0,1:T(2,128)(2,1)S(1)} async-done(((bf16[2,128,512]{2,0,1:T(2,128)(2,1)}), bf16[2,128,512]{2,0,1:T(2,128)(2,1)S(1)}, u32[]{:S(2)}, u32[]{:S(2)}) %all-to-all-start) | async-done | bytes 262176 | tf_op jit(solution)/shard_map/all_to_all | solution.py:112
  90.7 0.8 copy.163
  91.6 2.4 gather_fusion.1
  94.2 0.2 fusion.43
  94.4 7.9 %reduce-scatter.4.cloned.1.call-done = bf16[32,2048]{1,0:T(8,128)(2,1)} async-done(((bf16[32,4096]{1,0:T(8,128)(2,1)}), bf16[32,2048]{1,0:T(8,128)(2,1)}) %reduce-scatter.4.cloned.1.call-update) | async-done | bytes 131088 | tf_op jit(solution)/shard_map/reduce_scatter | solution.py:116
  102.3 1.1 multiply_reduce_fusion
  103.3 4.9 %psum.7 = f32[32]{0:T(128)S(1)} all-reduce(f32[32]{0:T(128)S(1)} %get-tuple-element.9), channel_id=1, replica_groups=mesh['groups'=2,'dp'=8,'expert'=2] {'expert'}, use_global_device_ids=true, to_apply=%region_14.15 | all-reduce | flops 32 | bytes 256 | tf_op jit(solution)/shard_map/psum | solution.py:121
  108.3 0.8 convolution_convert_fusion
  109.2 53.4 %all_to_all.28 = bf16[2,8,32,2048]{3,2,0,1:T(8,128)(2,1)S(1)} all-to-all(bf16[2,8,32,2048]{3,2,0,1:T(8,128)(2,1)S(1)} %copy.145), channel_id=1, replica_groups=mesh['groups'=2,'dp'=8,'expert'=2] {'dp'}, dimensions={1} | all-to-all | bytes 4194304 | tf_op jit(solution)/shard_map/all_to_all | solution.py:139
  162.6 0.2 copy.146
  162.9 1.3 copy-done.2
  164.2 5.7 %fusion.3 = f32[2,256,768]{2,1,0:T(8,128)} fusion(bf16[2,256,2048]{2,1,0:T(8,128)(2,1)S(1)} %bitcast.130, bf16[2,2,2048,768]{3,2,1,0:T(8,128)(2,1)} %param.22), kind=kOutput, calls=%fused_computation.7 | convolution fusion | flops 1610612736 | bytes 9961472 | tf_op jit(solution)/shard_map/jmd,jdh->jmh/dot_general | solution.py:141
  170.0 6.4 %fusion.1 = f32[2,256,768]{2,1,0:T(8,128)} fusion(bf16[2,256,2048]{2,1,0:T(8,128)(2,1)} %bitcast.131, bf16[2,2,2048,768]{3,2,1,0:T(8,128)(2,1)} %param.22), kind=kOutput, calls=%fused_computation.5 | convolution fusion | flops 1610612736 | bytes 9961472 | tf_op jit(solution)/shard_map/jmd,jdh->jmh/dot_general | solution.py:144
  176.4 17.8 %reduce-scatter.6.cloned.1.call-done = f32[2,256,384]{2,1,0:T(8,128)} async-done(((f32[2,256,768]{2,1,0:T(8,128)}), f32[2,256,384]{2,1,0:T(8,128)}) %reduce-scatter.6.cloned.1.call-update) | async-done | bytes 786448 | tf_op jit(solution)/shard_map/reduce_scatter | solution.py:148
  194.3 28.2 %reduce-scatter.8.cloned.1.call-done = f32[2,256,384]{2,1,0:T(8,128)} async-done(((f32[2,256,768]{2,1,0:T(8,128)}), f32[2,256,384]{2,1,0:T(8,128)}) %reduce-scatter.8.cloned.1.call-update) | async-done | bytes 786448 | tf_op jit(solution)/shard_map/reduce_scatter | solution.py:149
  222.5 1.6 multiply_convert_fusion
  224.1 11.6 %all_gather.7 = bf16[2,256,768]{2,1,0:T(8,128)(2,1)S(1)} all-gather(bf16[2,256,384]{2,1,0:T(8,128)(2,1)S(1)} %multiply_convert_fusion), channel_id=1, replica_groups=mesh['groups'=2,'dp'=8,'expert'=2] {'expert'}, dimensions={2}, use_global_device_ids=true | all-gather | bytes 1179648 | tf_op jit(solution)/shard_map/all_gather | solution.py:152
  235.7 4.6 %convolution_convert_fusion.1 = bf16[2,256,2048]{2,1,0:T(8,128)(2,1)S(1)} fusion(bf16[2,256,768]{2,1,0:T(8,128)(2,1)S(1)} %all_gather.7, bf16[2,768,2048]{2,1,0:T(8,128)(2,1)} %param.23), kind=kOutput, calls=%fused_computation.20 | convolution fusion | flops 1611661312 | bytes 9175040 | tf_op jit(solution)/shard_map/jmh,jhd->jmd/dot_general | solution.py:153
  240.3 1.6 copy.149
  241.9 4.6 %all-to-all-start.2 = ((bf16[2,8,32,2048]{3,2,0,1:T(8,128)(2,1)}), bf16[2,8,32,2048]{3,2,0,1:T(8,128)(2,1)S(1)}, u32[]{:S(2)}, u32[]{:S(2)}) async-start(bf16[2,8,32,2048]{3,2,0,1:T(8,128)(2,1)} %copy.149), calls=%async_computation.5 | async-start | bytes 4194304 | tf_op jit(solution)/shard_map/all_to_all | solution.py:157
  246.7 48.8 %all-to-all-done.2 = bf16[2,8,32,2048]{3,2,0,1:T(8,128)(2,1)S(1)} async-done(((bf16[2,8,32,2048]{3,2,0,1:T(8,128)(2,1)}), bf16[2,8,32,2048]{3,2,0,1:T(8,128)(2,1)S(1)}, u32[]{:S(2)}, u32[]{:S(2)}) %all-to-all-start.2) | async-done | bytes 2097184 | tf_op jit(solution)/shard_map/all_to_all | solution.py:157
  295.5 1.6 copy.150
  297.1 4.4 %gather_fusion = bf16[256,2048]{1,0:T(8,128)(2,1)S(1)} fusion(bf16[512,2048]{1,0:T(8,128)(2,1)} %bitcast.127, s32[1024]{0:T(1024)S(1)} %pad_clamp_fusion), kind=kCustom, calls=%fused_computation | custom fusion | bytes 2098176 | tf_op jit(solution)/shard_map/gather | solution.py:159
  301.5 1.0 fusion.23
  302.5 0.7 add_convert_fusion
  (58 shorter events, 2.1 us)
Async XLA Ops:
  6.5 68.1 %copy-start = (bf16[2048,512]{1,0:T(8,128)(2,1)S(1)}, bf16[2048,512]{1,0:T(8,128)(2,1)}, u32[]{:S(2)}) copy-start(bf16[2048,512]{1,0:T(8,128)(2,1)} %param.18) | copy-start | bytes 6291460
  6.5 68.1 %all-gather.2.cloned.1.call-start = ((), (), s32[]{:S(2)}) async-start(), calls=%async_computation.6 | async-start | bytes 1179648 | tf_op jit(solution)/shard_map/all_gather | solution.py:108
  19.8 5.9 %copy-start.6 = (bf16[2,16,2,256]{3,2,1,0:T(2,128)(2,1)S(1)}, bf16[2,16,2,256]{3,2,1,0:T(2,128)(2,1)}, u32[]{:S(2)}) copy-start(bf16[2,16,2,256]{3,2,1,0:T(2,128)(2,1)} %param.13) | copy-start | bytes 98308
  19.8 6.6 %copy-start.3 = (bf16[2,16,16,128]{3,2,1,0:T(8,128)(2,1)S(1)}, bf16[2,16,16,128]{3,2,1,0:T(8,128)(2,1)}, u32[]{:S(2)}) copy-start(bf16[2,16,16,128]{3,2,1,0:T(8,128)(2,1)} %param.12) | copy-start | bytes 393220
  39.1 4.4 %copy-start.5 = (bf16[2,16,2,128]{3,2,1,0:T(2,128)(2,1)S(1)}, bf16[2,16,2,128]{3,2,1,0:T(2,128)(2,1)}, u32[]{:S(2)}) copy-start(bf16[2,16,2,128]{3,2,1,0:T(2,128)(2,1)} %get-tuple-element.11) | copy-start | bytes 49156
  43.8 37.2 %copy-start.9 = (s32[2,16,8]{1,2,0:T(8,128)S(1)}, s32[2,16,8]{1,2,0:T(8,128)}, u32[]{:S(2)}) copy-start(s32[2,16,8]{1,2,0:T(8,128)} %param.20) | copy-start | bytes 3076
  77.5 13.1 %all-to-all-start = ((bf16[2,128,512]{2,0,1:T(2,128)(2,1)}), bf16[2,128,512]{2,0,1:T(2,128)(2,1)S(1)}, u32[]{:S(2)}, u32[]{:S(2)}) async-start(bf16[2,128,512]{2,0,1:T(2,128)(2,1)} %copy.133), calls=%async_computation | async-start | bytes 524288 | tf_op jit(solution)/shard_map/all_to_all | solution.py:112
  80.9 21.4 %reduce-scatter.4.cloned.1.call-start = ((), (), s32[]{:S(2)}) async-start(), calls=%async_computation.7 | async-start | bytes 393216 | tf_op jit(solution)/shard_map/reduce_scatter | solution.py:116
  91.5 102.8 %reduce-scatter.6.cloned.1.call-start = ((), (), s32[]{:S(2)}) async-start(), calls=%async_computation.8 | async-start | bytes 2359296 | tf_op jit(solution)/shard_map/reduce_scatter | solution.py:148
  91.6 10.7 %copy-start.4 = (bf16[2,16,2048]{2,1,0:T(8,128)(2,1)S(1)}, bf16[2,16,2048]{2,1,0:T(8,128)(2,1)}, u32[]{:S(2)}) copy-start(bf16[2,16,2048]{2,1,0:T(8,128)(2,1)} %param.17) | copy-start | bytes 393220
  91.6 16.7 %copy-start.8 = (f32[2048]{0:T(1024)S(1)}, f32[2048]{0:T(1024)}, u32[]{:S(2)}) copy-start(f32[2048]{0:T(1024)} %param.19) | copy-start | bytes 24580
  162.9 1.4 copy-start.2
  170.0 52.6 %reduce-scatter.8.cloned.1.call-start = ((), (), s32[]{:S(2)}) async-start(), calls=%async_computation.9 | async-start | bytes 2359296 | tf_op jit(solution)/shard_map/reduce_scatter | solution.py:149
  240.3 6.3 %copy-start.7 = (f32[2,16,8]{1,2,0:T(8,128)S(1)}, f32[2,16,8]{1,2,0:T(8,128)}, u32[]{:S(2)}) copy-start(f32[2,16,8]{1,2,0:T(8,128)} %param.21) | copy-start | bytes 3076
  241.9 53.6 %all-to-all-start.2 = ((bf16[2,8,32,2048]{3,2,0,1:T(8,128)(2,1)}), bf16[2,8,32,2048]{3,2,0,1:T(8,128)(2,1)S(1)}, u32[]{:S(2)}, u32[]{:S(2)}) async-start(bf16[2,8,32,2048]{3,2,0,1:T(8,128)(2,1)} %copy.149), calls=%async_computation.5 | async-start | bytes 4194304 | tf_op jit(solution)/shard_map/all_to_all | solution.py:157
  297.1 6.1 %copy-start.1 = (bf16[2048,512]{1,0:T(8,128)(2,1)S(1)}, bf16[2048,512]{1,0:T(8,128)(2,1)}, u32[]{:S(2)}) copy-start(bf16[2048,512]{1,0:T(8,128)(2,1)} %param.18) | copy-start | bytes 6291460
Sparse Core Ops, SparseCore 0:
  49.6 24.9 all-gather.1
  91.6 10.5 reduce-scatter.3
  170.1 24.1 reduce-scatter.5
  196.4 26.1 reduce-scatter.7
where the time goes:
time: 310 us
  waiting for transfers between devices  137 us (44%)
  blocking collectives  69.9 us (23%)
  matrix products  37.8 us (12%)
  local copies, waits for them, and re-layouts  25.6 us (8%)
  other arithmetic  17.7 us (6%)
  between operations  13.5 us (4%)
  starting transfers between devices  8.15 us (3%)
    all_to_all x1, blocking collectives, body(): lax.all_to_all(outgoing, 'dp', split_axis=1, concat_axis=1, tiled=True)  53.4 us
    all_to_all x1, waiting for transfers between devices, body(): lax.all_to_all(expert_out, 'dp', split_axis=1, concat_axis=1, tiled=True)  48.8 us
    reduce_scatter x1, waiting for transfers between devices, body(): lax.psum_scatter(up_part, 'expert', scatter_dimension=2, tiled=True)  28.2 us
    all_gather x1, waiting for transfers between devices, body(): every_request = lax.all_gather(attended, 'dp', axis=1, tiled=True)  25.1 us
    reduce_scatter x1, waiting for transfers between devices, body(): lax.psum_scatter(gate_part, 'expert', scatter_dimension=2, tiled=True)  17.8 us
    all_gather x1, blocking collectives, body(): activated = lax.all_gather(active_share, 'expert', axis=2, tiled=True)  11.6 us
    all_to_all x1, waiting for transfers between devices, body(): lax.all_to_all(local_columns.astype(jnp.bfloat16), 'dp', split_axis=1, co...  9.25 us
    reduce_sum x1, other arithmetic, attend(): page_sum = jnp.sum(page_probs, axis=4)  8.93 us
  transfers between devices with their start and end apart: 6, of which 6 were waited for; matrix products, arithmetic and copies ran while one was open for 3% of the time, Pallas kernels for 0%

commit v1 on v0

--- a/solution.py
+++ b/solution.py
@@ -77,16 +77,28 @@
     return attended.reshape(step_count, req_count, head_count * head_width).astype(jnp.bfloat16)
 
 
-def dispatch_keys(expert_ids, expert_total, local_experts, dp_count, capacity):
-    step_count = expert_ids.shape[0]
-    catalog = jnp.arange(expert_total, dtype=jnp.int32)
-    named_mask = jnp.any(expert_ids[..., None] == catalog, axis=2).astype(jnp.int32)
-    earlier = jnp.cumsum(named_mask, axis=1) - named_mask
-    slot_rank = jnp.take_along_axis(earlier, expert_ids, axis=2)
-    owner_index = expert_ids // local_experts
-    local_index = expert_ids % local_experts
-    step_index = jnp.arange(step_count, dtype=jnp.int32)[:, None, None]
-    return ((local_index * dp_count + owner_index) * step_count + step_index) * capacity + slot_rank
+def exchange(value, axis, mask):
+    count = lax.axis_size(axis)
+    return lax.ppermute(value, axis, [(i, i ^ mask) for i in range(count)])
+
+
+def reorder(blocks, index):
+    blocks = list(blocks)
+    for bit in range(len(blocks).bit_length() - 1):
+        flip = (index >> bit) & 1 == 1
+        blocks = [jnp.where(flip, blocks[j ^ (1 << bit)], blocks[j]) for j in range(len(blocks))]
+    return blocks
+
+
+def split_pair(value):
+    high = lax.reduce_precision(value, 8, 7)
+    return high.astype(jnp.bfloat16), (value - high).astype(jnp.bfloat16)
+
+
+def gather_rows(rows):
+    chips = lax.axis_size("dp") // 2
+    mine = jnp.stack([rows] + [exchange(rows, "dp", 2 * k) for k in range(1, chips)])
+    return jnp.stack([mine, exchange(mine, "dp", 1)])
 
 
 def body(
@@ -103,63 +115,105 @@
     gate_up,
     down_proj,
 ):
+    bf16, f32 = jnp.bfloat16, jnp.float32
+    dp_count, x_count = lax.axis_size("dp"), lax.axis_size("expert")
+    dp_index, x_index = lax.axis_index("dp"), lax.axis_index("expert")
+    chips = dp_count // 2
+    local_experts, _, width, hidden = gate_up.shape
+    expert_total = local_experts * dp_count
+
+    share = route_weights / jnp.sum(route_weights, axis=2, keepdims=True)
+    catalog = jnp.arange(expert_total, dtype=jnp.int32)
+    named = expert_ids[..., None] == catalog
+    routed = jnp.sum(jnp.where(named, share[..., None], 0.0), axis=2)
+
     attended = attend(queries, fresh_kv, kv_pool, page_table, context_lengths)
-    step_count, req_count, head_cols = attended.shape
-    every_request = lax.all_gather(attended, "dp", axis=1, tiled=True)
-    local_columns = jnp.einsum(
-        "srh,hc->src", every_request, out_weight, preferred_element_type=jnp.float32
-    )
-    regrouped = lax.all_to_all(
-        local_columns.astype(jnp.bfloat16), "dp", split_axis=1, concat_axis=2, tiled=True
-    ).astype(local_columns.dtype)
-    partial_out = regrouped.reshape(step_count * req_count, regrouped.shape[2])
-    projected = lax.psum_scatter(
-        partial_out.astype(jnp.bfloat16), "expert", scatter_dimension=1, tiled=True
-    ).astype(jnp.float32)
-    quarter = projected.shape[1]
-    stream = residual.astype(jnp.float32).reshape(step_count * req_count, quarter) + projected
-    squares = lax.psum(jnp.sum(stream * stream, axis=1), "expert")
-    model_width = quarter * lax.axis_size("expert")
-    inverse = lax.rsqrt(squares / model_width + EPS)
-    normed = (stream * inverse[:, None] * norm_gain[None, :]).astype(jnp.bfloat16)
-    dp_count = lax.axis_size("dp")
-    local_experts = gate_up.shape[0]
-    expert_total = local_experts * dp_count
-    top_count = expert_ids.shape[2]
-    capacity = min(
-        req_count, max(2, (5 * req_count * top_count + 2 * expert_total - 1) // (2 * expert_total))
-    )
-    slot_keys = dispatch_keys(expert_ids, expert_total, local_experts, dp_count, capacity)
-    slot_total = local_experts * dp_count * step_count * capacity
-    slot_ids = jnp.arange(slot_total, dtype=jnp.int32)
-    chosen = slot_keys.reshape(step_count * req_count, top_count)[None] == slot_ids[:, None, None]
-    selector = jnp.any(chosen, axis=2).astype(jnp.bfloat16)
-    outgoing = jnp.dot(selector, normed, preferred_element_type=jnp.float32).astype(jnp.bfloat16)
-    outgoing = outgoing.reshape(local_experts, dp_count, step_count * capacity, quarter)
-    incoming = lax.all_to_all(outgoing, "dp", split_axis=1, concat_axis=1, tiled=True)
-    expert_rows = incoming.reshape(local_experts, dp_count * step_count * capacity, quarter)
-    gate_part = jnp.einsum(
-        "jmd,jdh->jmh", expert_rows, gate_up[:, 0], preferred_element_type=jnp.float32
-    )
-    up_part = jnp.einsum(
-        "jmd,jdh->jmh", expert_rows, gate_up[:, 1], preferred_element_type=jnp.float32
-    )
-    gate_share, up_share = (
-        lax.psum_scatter(gate_part, "expert", scatter_dimension=2, tiled=True),
-        lax.psum_scatter(up_part, "expert", scatter_dimension=2, tiled=True),
-    )
-    active_share = (jax.nn.silu(gate_share) * up_share).astype(jnp.bfloat16)
-    activated = lax.all_gather(active_share, "expert", axis=2, tiled=True)
-    expert_out = jnp.einsum(
-        "jmh,jhd->jmd", activated, down_proj, preferred_element_type=jnp.float32
-    ).astype(jnp.bfloat16)
-    expert_out = expert_out.reshape(local_experts, dp_count, step_count * capacity, quarter)
-    returned = lax.all_to_all(expert_out, "dp", split_axis=1, concat_axis=1, tiled=True)
-    returned = returned.reshape(slot_total, quarter)
-    picked = returned[slot_keys].astype(jnp.float32)
-    share = route_weights / jnp.sum(route_weights, axis=2, keepdims=True)
-    mixture = jnp.sum(share[..., None] * picked, axis=2)
-    return (stream.reshape(step_count, req_count, quarter) + mixture).astype(jnp.bfloat16)
+    steps, reqs, head_cols = attended.shape
+    own = steps * reqs
+    total = dp_count * own
+    extra = -(-2 * expert_total // 128) * 128
+    routed_high, routed_low = split_pair(routed.reshape(own, expert_total))
+    packed = jnp.concatenate(
+        [
+            attended.reshape(own, head_cols),
+            routed_high,
+            routed_low,
+            jnp.zeros((own, extra - 2 * expert_total), bf16),
+        ],
+        axis=1,
+    )
+    gathered = gather_rows(packed).reshape(total, head_cols + extra)
+    routes = gathered[:, head_cols : head_cols + 2 * expert_total].astype(f32)
+    routes = routes[:, :expert_total] + routes[:, expert_total:]
+
+    columns = jnp.dot(gathered[:, :head_cols], out_weight, preferred_element_type=f32).astype(bf16)
+    block = columns.shape[1]
+    columns = columns.reshape(2, chips, own, block)
+    paired = jnp.stack([columns[0], exchange(columns[1], "dp", 1)], axis=1)
+    arrived = [paired[0]] + [exchange(paired[k], "dp", 2 * k) for k in range(1, chips)]
+    blocks = [arrived[q // 2][q % 2] for q in range(dp_count)]
+    per_x = dp_count // x_count
+    groups = [jnp.concatenate(blocks[g * per_x : (g + 1) * per_x], axis=1) for g in range(x_count)]
+    groups = reorder(groups, (dp_index // per_x) ^ x_index)
+    summed = groups[0].astype(f32)
+    for k in range(1, x_count):
+        summed = summed + exchange(groups[k], "expert", k).astype(f32)
+    summed = [summed[:, q * block : (q + 1) * block] for q in range(per_x)]
+    summed = jnp.concatenate(reorder(summed, dp_index % per_x), axis=1)
+    stream = residual.astype(f32).reshape(own, width) + summed
+
+    square_high, square_low = split_pair(jnp.sum(stream * stream, axis=1, keepdims=True))
+    rows = jnp.concatenate(
+        [
+            (stream * norm_gain[None, :]).astype(bf16),
+            square_high,
+            square_low,
+            jnp.zeros((own, 126), bf16),
+        ],
+        axis=1,
+    )
+    rows = gather_rows(rows).reshape(total, width + 128)
+    squares = rows[:, width : width + 2]
+    rows = rows[:, :width]
+
+    local = dp_index * local_experts + jnp.arange(local_experts, dtype=jnp.int32)
+    local_share = jnp.sum(
+        jnp.where(local[None, :, None] == catalog[None, None, :], routes[:, None, :], 0.0), axis=2
+    )
+    part = hidden // x_count
+    inverse = None
+    acts = []
+    for e in range(local_experts):
+        gate = jnp.dot(rows, gate_up[e, 0], preferred_element_type=f32)
+        up = jnp.dot(rows, gate_up[e, 1], preferred_element_type=f32)
+        gates = reorder([gate[:, k * part : (k + 1) * part] for k in range(x_count)], x_index)
+        ups = reorder([up[:, k * part : (k + 1) * part] for k in range(x_count)], x_index)
+        gate, up = gates[0], ups[0]
+        square = jnp.sum(squares.astype(f32), axis=1)
+        for k in range(1, x_count):
+            sent = [gates[k].astype(bf16), ups[k].astype(bf16)]
+            if e == 0:
+                sent.append(squares)
+            got = exchange(jnp.concatenate(sent, axis=1), "expert", k).astype(f32)
+            gate = gate + got[:, :part]
+            up = up + got[:, part : 2 * part]
+            if e == 0:
+                square = square + jnp.sum(got[:, 2 * part :], axis=1)
+        if e == 0:
+            inverse = lax.rsqrt(square / (width * x_count) + EPS)[:, None]
+        act = jax.nn.silu(gate * inverse) * (up * inverse) * local_share[:, e : e + 1]
+        act = act.astype(bf16)
+        pieces = [act] + [exchange(act, "expert", k) for k in range(1, x_count)]
+        acts.extend(reorder(pieces, x_index))
+    activated = jnp.concatenate(acts, axis=1)
+    down = down_proj.reshape(local_experts * hidden, width)
+    mixed = jnp.dot(activated, down, preferred_element_type=f32)
+    mixed = mixed.reshape(2, chips, own, width)
+    mixed = mixed[0] + exchange(mixed[1].astype(bf16), "dp", 1).astype(f32)
+    result = stream + mixed[0]
+    for k in range(1, chips):
+        result = result + exchange(mixed[k].astype(bf16), "dp", 2 * k).astype(f32)
+    return result.reshape(steps, reqs, width).astype(bf16)
 
 
 def solution(mesh):

time: 310 us -> 160 us (0.52)
  blocking collectives: 69.9 us -> 0 us
  waiting for transfers between devices: 137 us -> 70.7 us
  starting transfers between devices: 8.15 us -> 25.6 us
  between operations: 13.5 us -> 0.61 us
  local copies, waits for them, and re-layouts: 25.6 us -> 13.2 us
  matrix products: 37.8 us -> 32.6 us
    ppermute x0 -> x21, waiting for transfers between devices: none -> 70.7 us  [exchange(): return lax.ppermute(value, axis, [(i, i ^ mask) for i in range(count)])]
    all_to_all x2 -> x0, waiting for transfers between devices: 58.1 us -> none  [the longest x1 48.8 us: body(): lax.all_to_all(expert_out, 'dp', split_axis=1, concat_axis=1, tiled=True)]
    reduce_scatter x3 -> x0, waiting for transfers between devices: 53.9 us -> none  [the longest x1 28.2 us: body(): lax.psum_scatter(up_part, 'expert', scatter_dimension=2, tiled=True)]
    all_to_all x1 -> x0, blocking collectives: 53.4 us -> none  [body(): lax.all_to_all(outgoing, 'dp', split_axis=1, concat_axis=1, tiled=True)]
    ppermute x0 -> x21, starting transfers between devices: none -> 25.6 us  [exchange(): return lax.ppermute(value, axis, [(i, i ^ mask) for i in range(count)])]
    all_gather x1 -> x0, waiting for transfers between devices: 25.1 us -> none  [body(): every_request = lax.all_gather(attended, 'dp', axis=1, tiled=True)]
    all_gather x1 -> x0, blocking collectives: 11.6 us -> none  [body(): activated = lax.all_gather(active_share, 'expert', axis=2, tiled=True)]
    all_to_all x2 -> x0, starting transfers between devices: 8.02 us -> none  [the longest x1 4.61 us: body(): lax.all_to_all(expert_out, 'dp', split_axis=1, concat_axis=1, tiled=True)]
  transfers between devices with their start and end apart: 6 -> 21, of which waited for: 6 -> 18; matrix products, arithmetic and copies ran while one was open for 3% -> 1% of each run, Pallas kernels for 0% -> 0%
where the time goes in v1:
time: 160 us
  waiting for transfers between devices  70.7 us (44%)
  matrix products  32.6 us (20%)
  starting transfers between devices  25.6 us (16%)
  other arithmetic  16.9 us (11%)
  local copies, waits for them, and re-layouts  13.2 us (8%)
    ppermute x21, waiting for transfers between devices, exchange(): return lax.ppermute(value, axis, [(i, i ^ mask) for i in range(count)])  70.7 us
    ppermute x21, starting transfers between devices, exchange(): return lax.ppermute(value, axis, [(i, i ^ mask) for i in range(count)])  25.6 us
    reduce_sum x1, other arithmetic, attend(): page_sum = jnp.sum(page_probs, axis=4)  8.93 us
    slice x1, local copies, waits for them, and re-layouts, attend(): key_rows = pool_block[..., :head_width]  6.98 us
    dot_general x2, matrix products, body(): gate = jnp.dot(rows, gate_up[e, 0], preferred_element_type=f32)  5.94 us
    dot_general x2, matrix products, body(): up = jnp.dot(rows, gate_up[e, 1], preferred_element_type=f32)  5.79 us
    dot_general x1, matrix products, attend(): jnp.einsum('pskgd,ptkd->pskgt', page_query, key_rows, preferred_element_t...  5.26 us
    dot_general x1, matrix products, attend(): jnp.einsum('rp,pskgd->rskgd', owned_f, page_acc, precision=EXACT)  4.88 us
  transfers between devices with their start and end apart: 21, of which 18 were waited for; matrix products, arithmetic and copies ran while one was open for 1% of the time, Pallas kernels for 0%

profile of v1, /device:TPU:0, one launch (start us, length us, event | category | flops | bytes accessed | tf_op | source)
XLA Modules:
  0.0 159.6 jit_solution(6000017939281655143)
XLA Ops:
  0.0 1.0 copy.79
  1.0 1.2 fusion
  2.2 1.5 select_reduce_fusion
  3.7 0.7 select_reduce_fusion.4
  4.5 1.8 %convolution_convert_fusion = bf16[320,2,2,8,128]{4,0,3,2,1:T(8,128)(2,1)S(1)} fusion(bf16[2,16,2,8,128]{4,3,2,1,0:T(8,128)(2,1)} %bitcast.199, pred[16,320]{1,0:T(8,128)(4,1)S(1)} %fusion), kind=kOutput, calls=%fused_computation.33 | convolution fusion | flops 43253760 | bytes 2757632 | tf_op jit(solution)/shard_map/rp,srkgd->pskgd/dot_general | solution.py:32
  6.3 7.0 %fusion.91 = (bf16[320,16,2,128]{3,2,1,0:T(2,128)(2,1)S(1)}, bf16[320,16,2,128]{3,2,1,0:T(2,128)(2,1)}) fusion(bf16[320,16,2,256]{3,2,1,0:T(2,128)(2,1)} %param.14), kind=kLoop, calls=%fused_computation.163 | loop fusion | bytes 10485760 | tf_op jit(solution)/shard_map/slice | solution.py:38
  13.3 5.3 %bitcast_reduce_fusion = (f32[320,2,2,8]{3,1,2,0:T(2,128)S(1)}, f32[320,2,2,8,16]{4,3,2,1,0:T(8,128)}) fusion(pred[320,16]{1,0:T(8,128)(4,1)S(1)} %iota_compare_fusion.1, bf16[320,16,2,128]{3,2,1,0:T(2,128)(2,1)S(1)} %get-tuple-element.7, bf16[320,2,2,8,128]{4,0,3,2,1:T(8,128)(2,1)S(1)} %convolution_convert_fusion), kind=kOutput, calls=%fused_computation.4 | convolution fusion | flops 42424320 | bytes 5944320 | tf_op jit(solution)/shard_map/pskgd,ptkd->pskgt/dot_general | solution.py:41
  19.9 1.3 fusion.95
  22.6 8.9 %fusion.4 = f32[320,2,2,8]{3,1,2,0:T(2,128)S(1)} fusion(f32[320,2,2,8,16]{4,3,2,1,0:T(8,128)} %get-tuple-element.46, f32[320,2,2,8]{3,1,2,0:T(2,128)S(1)} %copy.88, pred[320,16]{1,0:T(8,128)(4,1)S(1)} %iota_compare_fusion.1), kind=kLoop, calls=%fused_computation.9 | loop fusion | flops 645120 | bytes 742400 | tf_op jit(solution)/shard_map/reduce_sum | solution.py:59
  32.2 1.0 fusion.76
  33.2 4.5 %fusion.26 = f32[320,2,2,8,128]{4,3,1,2,0:T(8,128)S(1)} fusion(bf16[320,16,2,128]{3,2,1,0:T(2,128)(2,1)} %get-tuple-element.8, f32[320,2,2,8,16]{4,3,2,1,0:T(8,128)} %get-tuple-element.46, f32[320,2,2,8]{3,1,2,0:T(2,128)S(1)} %copy.88, pred[320,16]{1,0:T(8,128)(4,1)S(1)} %iota_compare_fusion.1), kind=kOutput, calls=%fused_computation.32 | convolution fusion | flops 42598400 | bytes 8565760 | tf_op jit(solution)/shard_map/pskgt,ptkd->pskgd/dot_general | solution.py:60
  38.0 4.9 %fusion.38 = bf16[2,16,2,8,128]{4,1,3,2,0:T(8,128)(2,1)S(1)} fusion(f32[320,2,2,8,128]{4,3,1,2,0:T(8,128)S(1)} %fusion.26, f32[16,2,2,8,128]{4,3,2,1,0:T(8,128)S(1)} %fusion.78, f32[2,16,2,8]{1,3,2,0:T(8,128)S(1)} %add.88, pred[16,320]{1,0:T(8,128)(4,1)S(1)} %fusion), kind=kOutput, calls=%fused_computation.38 | convolution fusion | flops 251854848 | bytes 5643264 | tf_op jit(solution)/shard_map/rp,pskgd->rskgd/dot_general | solution.py:67
  43.5 3.1 %collective-permute-start = (bf16[32,2176]{1,0:T(8,128)(2,1)S(1)}, bf16[32,2176]{1,0:T(8,128)(2,1)S(1)}, u32[]{:S(2)}, u32[]{:S(2)}) collective-permute-start(bf16[32,2176]{1,0:T(8,128)(2,1)S(1)} %concatenate.35), channel_id=1, source_target_pairs={{0,4},{2,6},{4,0},{6,2},{8,12},{10,14},{12,8},{14,10},{1,5},{3,7},... | collective-permute-start | bytes 417800 | tf_op jit(solution)/shard_map/ppermute | solution.py:82
  46.6 2.6 %collective-permute-start.1 = (bf16[32,2176]{1,0:T(8,128)(2,1)S(1)}, bf16[32,2176]{1,0:T(8,128)(2,1)S(1)}, u32[]{:S(2)}, u32[]{:S(2)}) collective-permute-start(bf16[32,2176]{1,0:T(8,128)(2,1)S(1)} %concatenate.35), channel_id=1, source_target_pairs={{0,8},{2,10},{4,12},{6,14},{8,0},{10,2},{12,4},{14,6},{1,9},{3,11}... | collective-permute-start | bytes 417800 | tf_op jit(solution)/shard_map/ppermute | solution.py:82
  49.2 2.9 %collective-permute-done = bf16[32,2176]{1,0:T(8,128)(2,1)S(1)} collective-permute-done((bf16[32,2176]{1,0:T(8,128)(2,1)S(1)}, bf16[32,2176]{1,0:T(8,128)(2,1)S(1)}, u32[]{:S(2)}, u32[]{:S(2)}) %collective-permute-start) | collective-permute-done | bytes 139296 | tf_op jit(solution)/shard_map/ppermute | solution.py:82
  52.1 7.9 %collective-permute-done.1 = bf16[32,2176]{1,0:T(8,128)(2,1)S(1)} collective-permute-done((bf16[32,2176]{1,0:T(8,128)(2,1)S(1)}, bf16[32,2176]{1,0:T(8,128)(2,1)S(1)}, u32[]{:S(2)}, u32[]{:S(2)}) %collective-permute-start.1) | collective-permute-done | bytes 139296 | tf_op jit(solution)/shard_map/ppermute | solution.py:82
  60.2 1.9 %collective-permute-done.3 = bf16[4,32,2176]{2,1,0:T(8,128)(2,1)S(1)} collective-permute-done((bf16[4,32,2176]{2,1,0:T(8,128)(2,1)S(1)}, bf16[4,32,2176]{2,1,0:T(8,128)(2,1)S(1)}, u32[]{:S(2)}, u32[]{:S(2)}) %collective-permute-start.3) | collective-permute-done | bytes 557088 | tf_op jit(solution)/shard_map/ppermute | solution.py:82
  62.3 0.7 convolution_convert_fusion.1
  63.9 0.8 slice.233
  65.1 3.3 %collective-permute-start.5 = (bf16[2,32,512]{2,1,0:T(8,128)(2,1)S(1)}, bf16[2,32,512]{2,1,0:T(8,128)(2,1)S(1)}, u32[]{:S(2)}, u32[]{:S(2)}) collective-permute-start(bf16[2,32,512]{2,1,0:T(8,128)(2,1)S(1)} %get-tuple-element.24), channel_id=1, source_target_pairs={{0,8},{2,10},{4,12},{6,14},{8,0},{10,2},{12,4},{14,6},{1,9},{3,11}... | collective-permute-start | bytes 196616 | tf_op jit(solution)/shard_map/ppermute | solution.py:82
  68.4 1.4 collective-permute-start.6
  69.8 3.1 %collective-permute-done.5 = bf16[2,32,512]{2,1,0:T(8,128)(2,1)S(1)} collective-permute-done((bf16[2,32,512]{2,1,0:T(8,128)(2,1)S(1)}, bf16[2,32,512]{2,1,0:T(8,128)(2,1)S(1)}, u32[]{:S(2)}, u32[]{:S(2)}) %collective-permute-start.5) | collective-permute-done | bytes 65568 | tf_op jit(solution)/shard_map/ppermute | solution.py:82
  72.8 1.9 %collective-permute-done.6 = bf16[2,32,512]{2,1,0:T(8,128)(2,1)S(1)} collective-permute-done((bf16[2,32,512]{2,1,0:T(8,128)(2,1)S(1)}, bf16[2,32,512]{2,1,0:T(8,128)(2,1)S(1)}, u32[]{:S(2)}, u32[]{:S(2)}) %collective-permute-start.6) | collective-permute-done | bytes 65568 | tf_op jit(solution)/shard_map/ppermute | solution.py:82
  75.2 1.6 collective-permute-start.8
  76.7 3.5 %collective-permute-done.8 = bf16[32,2048]{1,0:T(8,128)(2,1)S(1)} collective-permute-done((bf16[32,2048]{1,0:T(8,128)(2,1)S(1)}, bf16[32,2048]{1,0:T(8,128)(2,1)S(1)}, u32[]{:S(2)}, u32[]{:S(2)}) %collective-permute-start.8) | collective-permute-done | bytes 131104 | tf_op jit(solution)/shard_map/ppermute | solution.py:82
  81.4 2.1 %collective-permute-start.10 = (bf16[32,2176]{1,0:T(8,128)(2,1)S(1)}, bf16[32,2176]{1,0:T(8,128)(2,1)S(1)}, u32[]{:S(2)}, u32[]{:S(2)}) collective-permute-start(bf16[32,2176]{1,0:T(8,128)(2,1)S(1)} %concatenate.44), channel_id=1, source_target_pairs={{0,8},{2,10},{4,12},{6,14},{8,0},{10,2},{12,4},{14,6},{1,9},{3,11}... | collective-permute-start | bytes 417800 | tf_op jit(solution)/shard_map/ppermute | solution.py:82
  83.5 1.8 %collective-permute-start.11 = (bf16[32,2176]{1,0:T(8,128)(2,1)S(1)}, bf16[32,2176]{1,0:T(8,128)(2,1)S(1)}, u32[]{:S(2)}, u32[]{:S(2)}) collective-permute-start(bf16[32,2176]{1,0:T(8,128)(2,1)S(1)} %concatenate.44), channel_id=1, source_target_pairs={{0,12},{2,14},{4,8},{6,10},{8,4},{10,6},{12,0},{14,2},{1,13},{3,15... | collective-permute-start | bytes 417800 | tf_op jit(solution)/shard_map/ppermute | solution.py:82
  85.3 1.0 collective-permute-done.9
  86.3 7.0 %collective-permute-done.10 = bf16[32,2176]{1,0:T(8,128)(2,1)S(1)} collective-permute-done((bf16[32,2176]{1,0:T(8,128)(2,1)S(1)}, bf16[32,2176]{1,0:T(8,128)(2,1)S(1)}, u32[]{:S(2)}, u32[]{:S(2)}) %collective-permute-start.10) | collective-permute-done | bytes 139296 | tf_op jit(solution)/shard_map/ppermute | solution.py:82
  93.8 1.7 %collective-permute-done.12 = bf16[4,32,2176]{2,1,0:T(8,128)(2,1)S(1)} collective-permute-done((bf16[4,32,2176]{2,1,0:T(8,128)(2,1)S(1)}, bf16[4,32,2176]{2,1,0:T(8,128)(2,1)S(1)}, u32[]{:S(2)}, u32[]{:S(2)}) %collective-permute-start.12) | collective-permute-done | bytes 557088 | tf_op jit(solution)/shard_map/ppermute | solution.py:82
  95.6 2.9 %fusion.6 = f32[256,768]{1,0:T(8,128)S(1)} fusion(bf16[2,2,2048,768]{3,2,1,0:T(8,128)(2,1)} %param.22, bf16[256,2176]{1,0:T(8,128)(2,1)S(1)} %bitcast.172), kind=kOutput, calls=%fused_computation.11 | convolution fusion | flops 805306368 | bytes 4980736 | tf_op jit(solution)/shard_map/dot_general | solution.py:188
  98.5 2.9 %fusion.8 = f32[256,768]{1,0:T(8,128)S(1)} fusion(bf16[2,2,2048,768]{3,2,1,0:T(8,128)(2,1)} %param.22, bf16[256,2176]{1,0:T(8,128)(2,1)S(1)} %bitcast.173), kind=kOutput, calls=%fused_computation.13 | convolution fusion | flops 805306368 | bytes 4980736 | tf_op jit(solution)/shard_map/dot_general | solution.py:187
  101.4 2.9 %fusion.10 = f32[256,768]{1,0:T(8,128)S(1)} fusion(bf16[2,2,2048,768]{3,2,1,0:T(8,128)(2,1)} %param.22, bf16[256,2176]{1,0:T(8,128)(2,1)S(1)} %bitcast.174), kind=kOutput, calls=%fused_computation.15 | convolution fusion | flops 805306368 | bytes 4980736 | tf_op jit(solution)/shard_map/dot_general | solution.py:188
  104.3 3.0 %fusion.12 = f32[256,768]{1,0:T(8,128)S(1)} fusion(bf16[2,2,2048,768]{3,2,1,0:T(8,128)(2,1)} %param.22, bf16[256,2176]{1,0:T(8,128)(2,1)S(1)} %bitcast.175), kind=kOutput, calls=%fused_computation.17 | convolution fusion | flops 805306368 | bytes 4980736 | tf_op jit(solution)/shard_map/dot_general | solution.py:187
  107.5 1.5 collective-permute-start.15
  110.0 9.5 %collective-permute-done.15 = bf16[256,768]{1,0:T(8,128)(2,1)S(1)} collective-permute-done((bf16[256,768]{1,0:T(8,128)(2,1)S(1)}, bf16[256,768]{1,0:T(8,128)(2,1)S(1)}, u32[]{:S(2)}, u32[]{:S(2)}) %collective-permute-start.15) | collective-permute-done | bytes 393248 | tf_op jit(solution)/shard_map/ppermute | solution.py:82
  119.6 8.9 %collective-permute-done.13 = bf16[256,770]{1,0:T(8,128)(2,1)S(1)} collective-permute-done((bf16[256,770]{1,0:T(8,128)(2,1)S(1)}, bf16[256,770]{1,0:T(8,128)(2,1)S(1)}, u32[]{:S(2)}, u32[]{:S(2)}) %collective-permute-start.13) | collective-permute-done | bytes 394272 | tf_op jit(solution)/shard_map/ppermute | solution.py:82
  129.2 1.5 collective-permute-start.14
  131.3 5.7 %collective-permute-done.14 = bf16[256,384]{1,0:T(8,128)(2,1)S(1)} collective-permute-done((bf16[256,384]{1,0:T(8,128)(2,1)S(1)}, bf16[256,384]{1,0:T(8,128)(2,1)S(1)}, u32[]{:S(2)}, u32[]{:S(2)}) %collective-permute-start.14) | collective-permute-done | bytes 196640 | tf_op jit(solution)/shard_map/ppermute | solution.py:82
  137.1 2.5 %collective-permute-done.16 = bf16[256,384]{1,0:T(8,128)(2,1)S(1)} collective-permute-done((bf16[256,384]{1,0:T(8,128)(2,1)S(1)}, bf16[256,384]{1,0:T(8,128)(2,1)S(1)}, u32[]{:S(2)}, u32[]{:S(2)}) %collective-permute-start.16) | collective-permute-done | bytes 196640 | tf_op jit(solution)/shard_map/ppermute | solution.py:82
  139.6 1.9 %fusion.44 = f32[256,2048]{1,0:T(8,128)S(1)} fusion(bf16[1536,2048]{1,0:T(8,128)(2,1)S(1)} %bitcast.207, bf16[256,384]{1,0:T(8,128)(2,1)S(1)} %get-tuple-element.19, bf16[256,384]{1,0:T(8,128)(2,1)S(1)} %get-tuple-element.18, bf16[256,384]{1,0:T(8,128)(2,1)S(1)} %get-tuple-element.17, bf16[256,384]{1,0:T(8,128)(2,1)S(1)} %get-tuple-element.16), kind=kOutput, calls=%fused_computation.47 | convolution fusion | flops 1613758464 | bytes 9175040 | tf_op jit(solution)/shard_map/dot_general | solution.py:210
  141.8 1.8 %collective-permute-done.17 = bf16[4,32,2048]{2,1,0:T(8,128)(2,1)S(1)} collective-permute-done((bf16[4,32,2048]{2,1,0:T(8,128)(2,1)S(1)}, bf16[4,32,2048]{2,1,0:T(8,128)(2,1)S(1)}, u32[]{:S(2)}, u32[]{:S(2)}) %collective-permute-start.17) | collective-permute-done | bytes 524320 | tf_op jit(solution)/shard_map/ppermute | solution.py:82
  143.8 2.1 %collective-permute-start.18 = (bf16[32,2048]{1,0:T(8,128)(2,1)S(1)}, bf16[32,2048]{1,0:T(8,128)(2,1)S(1)}, u32[]{:S(2)}, u32[]{:S(2)}) collective-permute-start(bf16[32,2048]{1,0:T(8,128)(2,1)S(1)} %get-tuple-element.13), channel_id=1, source_target_pairs={{0,4},{2,6},{4,0},{6,2},{8,12},{10,14},{12,8},{14,10},{1,5},{3,7},... | collective-permute-start | bytes 393224 | tf_op jit(solution)/shard_map/ppermute | solution.py:82
  145.9 1.1 collective-permute-start.19
  147.0 1.4 collective-permute-start.20
  148.4 3.2 %collective-permute-done.18 = bf16[32,2048]{1,0:T(8,128)(2,1)S(1)} collective-permute-done((bf16[32,2048]{1,0:T(8,128)(2,1)S(1)}, bf16[32,2048]{1,0:T(8,128)(2,1)S(1)}, u32[]{:S(2)}, u32[]{:S(2)}) %collective-permute-start.18) | collective-permute-done | bytes 131104 | tf_op jit(solution)/shard_map/ppermute | solution.py:82
  151.6 7.2 %collective-permute-done.19 = bf16[32,2048]{1,0:T(8,128)(2,1)S(1)} collective-permute-done((bf16[32,2048]{1,0:T(8,128)(2,1)S(1)}, bf16[32,2048]{1,0:T(8,128)(2,1)S(1)}, u32[]{:S(2)}, u32[]{:S(2)}) %collective-permute-start.19) | collective-permute-done | bytes 131104 | tf_op jit(solution)/shard_map/ppermute | solution.py:82
  158.8 0.7 fusion.70
  (121 shorter events, 10.9 us)
Async XLA Ops:
  0.0 62.2 %copy-start = (bf16[2048,512]{1,0:T(8,128)(2,1)S(1)}, bf16[2048,512]{1,0:T(8,128)(2,1)}, u32[]{:S(2)}) copy-start(bf16[2048,512]{1,0:T(8,128)(2,1)} %param.18) | copy-start | bytes 6291460
  13.3 5.9 %copy-start.10 = (bf16[2,16,2,256]{3,2,1,0:T(2,128)(2,1)S(1)}, bf16[2,16,2,256]{3,2,1,0:T(2,128)(2,1)}, u32[]{:S(2)}) copy-start(bf16[2,16,2,256]{3,2,1,0:T(2,128)(2,1)} %param.13) | copy-start | bytes 98308
  13.3 6.6 %copy-start.7 = (bf16[2,16,16,128]{3,2,1,0:T(8,128)(2,1)S(1)}, bf16[2,16,16,128]{3,2,1,0:T(8,128)(2,1)}, u32[]{:S(2)}) copy-start(bf16[2,16,16,128]{3,2,1,0:T(8,128)(2,1)} %param.12) | copy-start | bytes 393220
  22.5 9.5 %copy-start.8 = (f32[2,16,2,8]{1,3,2,0:T(8,128)S(1)}, f32[2,16,2,8]{1,3,2,0:T(8,128)}, u32[]{:S(2)}) copy-start(f32[2,16,2,8]{1,3,2,0:T(8,128)} %copy.92) | copy-start | bytes 6148
  33.2 4.5 %copy-start.6 = (f32[2,16,2,8,2]{3,4,0,2,1:T(2,128)S(1)}, f32[2,16,2,8,2]{3,4,0,2,1:T(2,128)}, u32[]{:S(2)}) copy-start(f32[2,16,2,8,2]{3,4,0,2,1:T(2,128)} %get-tuple-element.48) | copy-start | bytes 12292
  33.2 4.5 %copy-start.9 = (bf16[2,16,2,128]{3,2,1,0:T(2,128)(2,1)S(1)}, bf16[2,16,2,128]{3,2,1,0:T(2,128)(2,1)}, u32[]{:S(2)}) copy-start(bf16[2,16,2,128]{3,2,1,0:T(2,128)(2,1)} %get-tuple-element.35) | copy-start | bytes 49156
  38.0 5.0 %copy-start.11 = (f32[2,16,8]{1,2,0:T(8,128)S(1)}, f32[2,16,8]{1,2,0:T(8,128)}, u32[]{:S(2)}) copy-start(f32[2,16,8]{1,2,0:T(8,128)} %param.21) | copy-start | bytes 3076
  38.0 5.1 %copy-start.13 = (s32[2,16,8]{1,2,0:T(8,128)S(1)}, s32[2,16,8]{1,2,0:T(8,128)}, u32[]{:S(2)}) copy-start(s32[2,16,8]{1,2,0:T(8,128)} %param.20) | copy-start | bytes 3076
  43.5 8.6 %collective-permute-start = (bf16[32,2176]{1,0:T(8,128)(2,1)S(1)}, bf16[32,2176]{1,0:T(8,128)(2,1)S(1)}, u32[]{:S(2)}, u32[]{:S(2)}) collective-permute-start(bf16[32,2176]{1,0:T(8,128)(2,1)S(1)} %concatenate.35), channel_id=1, source_target_pairs={{0,4},{2,6},{4,0},{6,2},{8,12},{10,14},{12,8},{14,10},{1,5},{3,7},... | collective-permute-start | bytes 417800 | tf_op jit(solution)/shard_map/ppermute | solution.py:82
  46.6 13.4 %collective-permute-start.1 = (bf16[32,2176]{1,0:T(8,128)(2,1)S(1)}, bf16[32,2176]{1,0:T(8,128)(2,1)S(1)}, u32[]{:S(2)}, u32[]{:S(2)}) collective-permute-start(bf16[32,2176]{1,0:T(8,128)(2,1)S(1)} %concatenate.35), channel_id=1, source_target_pairs={{0,8},{2,10},{4,12},{6,14},{8,0},{10,2},{12,4},{14,6},{1,9},{3,11}... | collective-permute-start | bytes 417800 | tf_op jit(solution)/shard_map/ppermute | solution.py:82
  49.2 10.8 %collective-permute-start.2 = (bf16[32,2176]{1,0:T(8,128)(2,1)S(1)}, bf16[32,2176]{1,0:T(8,128)(2,1)S(1)}, u32[]{:S(2)}, u32[]{:S(2)}) collective-permute-start(bf16[32,2176]{1,0:T(8,128)(2,1)S(1)} %concatenate.35), channel_id=1, source_target_pairs={{0,12},{2,14},{4,8},{6,10},{8,4},{10,6},{12,0},{14,2},{1,13},{3,15... | collective-permute-start | bytes 417800 | tf_op jit(solution)/shard_map/ppermute | solution.py:82
  60.1 2.0 %collective-permute-start.3 = (bf16[4,32,2176]{2,1,0:T(8,128)(2,1)S(1)}, bf16[4,32,2176]{2,1,0:T(8,128)(2,1)S(1)}, u32[]{:S(2)}, u32[]{:S(2)}) collective-permute-start(bf16[4,32,2176]{2,1,0:T(8,128)(2,1)S(1)} %get-tuple-element.12), channel_id=1, source_target_pairs={{0,2},{2,0},{4,6},{6,4},{8,10},{10,8},{12,14},{14,12},{1,3},{3,1},... | collective-permute-start | bytes 1671176 | tf_op jit(solution)/shard_map/ppermute | solution.py:82
  62.3 18.0 %copy-start.2 = (bf16[2,16,2048]{2,1,0:T(8,128)(2,1)S(1)}, bf16[2,16,2048]{2,1,0:T(8,128)(2,1)}, u32[]{:S(2)}) copy-start(bf16[2,16,2048]{2,1,0:T(8,128)(2,1)} %param.17) | copy-start | bytes 393220
  62.3 18.4 %copy-start.12 = (f32[2048]{0:T(1024)S(1)}, f32[2048]{0:T(1024)}, u32[]{:S(2)}) copy-start(f32[2048]{0:T(1024)} %param.19) | copy-start | bytes 24580
  63.0 0.7 copy-start.5
  63.7 1.4 collective-permute-start.4
  65.1 7.7 %collective-permute-start.5 = (bf16[2,32,512]{2,1,0:T(8,128)(2,1)S(1)}, bf16[2,32,512]{2,1,0:T(8,128)(2,1)S(1)}, u32[]{:S(2)}, u32[]{:S(2)}) collective-permute-start(bf16[2,32,512]{2,1,0:T(8,128)(2,1)S(1)} %get-tuple-element.24), channel_id=1, source_target_pairs={{0,8},{2,10},{4,12},{6,14},{8,0},{10,2},{12,4},{14,6},{1,9},{3,11}... | collective-permute-start | bytes 196616 | tf_op jit(solution)/shard_map/ppermute | solution.py:82
  68.4 6.4 %collective-permute-start.6 = (bf16[2,32,512]{2,1,0:T(8,128)(2,1)S(1)}, bf16[2,32,512]{2,1,0:T(8,128)(2,1)S(1)}, u32[]{:S(2)}, u32[]{:S(2)}) collective-permute-start(bf16[2,32,512]{2,1,0:T(8,128)(2,1)S(1)} %get-tuple-element.25), channel_id=1, source_target_pairs={{0,12},{2,14},{4,8},{6,10},{8,4},{10,6},{12,0},{14,2},{1,13},{3,15... | collective-permute-start | bytes 196616 | tf_op jit(solution)/shard_map/ppermute | solution.py:82
  69.7 5.4 %collective-permute-start.7 = (bf16[2,32,512]{2,1,0:T(8,128)(2,1)S(1)}, bf16[2,32,512]{2,1,0:T(8,128)(2,1)S(1)}, u32[]{:S(2)}, u32[]{:S(2)}) collective-permute-start(bf16[2,32,512]{2,1,0:T(8,128)(2,1)S(1)} %get-tuple-element.26), channel_id=1, source_target_pairs={{0,4},{2,6},{4,0},{6,2},{8,12},{10,14},{12,8},{14,10},{1,5},{3,7},... | collective-permute-start | bytes 196616 | tf_op jit(solution)/shard_map/ppermute | solution.py:82
  75.2 5.0 %collective-permute-start.8 = (bf16[32,2048]{1,0:T(8,128)(2,1)S(1)}, bf16[32,2048]{1,0:T(8,128)(2,1)S(1)}, u32[]{:S(2)}, u32[]{:S(2)}) collective-permute-start(bf16[32,2048]{1,0:T(8,128)(2,1)S(1)} %broadcast_select_fusion.4), channel_id=1, source_target_pairs={{0,1},{1,0},{2,3},{3,2},{4,5},{5,4},{6,7},{7,6},{8,9},{9,8},{10,11... | collective-permute-start | bytes 393224 | tf_op jit(solution)/shard_map/ppermute | solution.py:82
  80.3 13.1 %copy-start.3 = (f32[32,512]{1,0:T(8,128)}, f32[32,512]{1,0:T(8,128)S(1)}, u32[]{:S(2)}) copy-start(f32[32,512]{1,0:T(8,128)S(1)} %get-tuple-element.23) | copy-start | bytes 196612
  80.9 5.4 %collective-permute-start.9 = (bf16[32,2176]{1,0:T(8,128)(2,1)S(1)}, bf16[32,2176]{1,0:T(8,128)(2,1)S(1)}, u32[]{:S(2)}, u32[]{:S(2)}) collective-permute-start(bf16[32,2176]{1,0:T(8,128)(2,1)S(1)} %concatenate.44), channel_id=1, source_target_pairs={{0,4},{2,6},{4,0},{6,2},{8,12},{10,14},{12,8},{14,10},{1,5},{3,7},... | collective-permute-start | bytes 417800 | tf_op jit(solution)/shard_map/ppermute | solution.py:82
  81.4 11.9 %collective-permute-start.10 = (bf16[32,2176]{1,0:T(8,128)(2,1)S(1)}, bf16[32,2176]{1,0:T(8,128)(2,1)S(1)}, u32[]{:S(2)}, u32[]{:S(2)}) collective-permute-start(bf16[32,2176]{1,0:T(8,128)(2,1)S(1)} %concatenate.44), channel_id=1, source_target_pairs={{0,8},{2,10},{4,12},{6,14},{8,0},{10,2},{12,4},{14,6},{1,9},{3,11}... | collective-permute-start | bytes 417800 | tf_op jit(solution)/shard_map/ppermute | solution.py:82
  83.5 9.8 %collective-permute-start.11 = (bf16[32,2176]{1,0:T(8,128)(2,1)S(1)}, bf16[32,2176]{1,0:T(8,128)(2,1)S(1)}, u32[]{:S(2)}, u32[]{:S(2)}) collective-permute-start(bf16[32,2176]{1,0:T(8,128)(2,1)S(1)} %concatenate.44), channel_id=1, source_target_pairs={{0,12},{2,14},{4,8},{6,10},{8,4},{10,6},{12,0},{14,2},{1,13},{3,15... | collective-permute-start | bytes 417800 | tf_op jit(solution)/shard_map/ppermute | solution.py:82
  93.5 2.0 %collective-permute-start.12 = (bf16[4,32,2176]{2,1,0:T(8,128)(2,1)S(1)}, bf16[4,32,2176]{2,1,0:T(8,128)(2,1)S(1)}, u32[]{:S(2)}, u32[]{:S(2)}) collective-permute-start(bf16[4,32,2176]{2,1,0:T(8,128)(2,1)S(1)} %get-tuple-element.10), channel_id=1, source_target_pairs={{0,2},{2,0},{4,6},{6,4},{8,10},{10,8},{12,14},{14,12},{1,3},{3,1},... | collective-permute-start | bytes 1671176 | tf_op jit(solution)/shard_map/ppermute | solution.py:82
  104.3 35.3 %slice-start = ((s8[6291456]{0:T(1024)(128)(4,1)}), s8[4194304]{0:T(1024)(128)(4,1)S(1)}, s32[]{:S(2)}) async-start(s8[6291456]{0:T(1024)(128)(4,1)} %bitcast.205), calls=%async_computation | async-start | bytes 8388608
  107.5 12.1 %collective-permute-start.15 = (bf16[256,768]{1,0:T(8,128)(2,1)S(1)}, bf16[256,768]{1,0:T(8,128)(2,1)S(1)}, u32[]{:S(2)}, u32[]{:S(2)}) collective-permute-start(bf16[256,768]{1,0:T(8,128)(2,1)S(1)} %pad_maximum_fusion.5), channel_id=1, source_target_pairs={{0,1},{1,0},{2,3},{3,2},{4,5},{5,4},{6,7},{7,6},{8,9},{9,8},{10,11... | collective-permute-start | bytes 1179656 | tf_op jit(solution)/shard_map/ppermute | solution.py:82
  109.1 30.5 %slice-start.1 = ((s8[6291456]{0:T(1024)(128)(4,1)}), s8[2097152]{0:T(1024)(128)(4,1)S(1)}, s32[]{:S(2)}) async-start(s8[6291456]{0:T(1024)(128)(4,1)} %bitcast.205), calls=%async_computation.1 | async-start | bytes 4194304
  109.2 19.4 %collective-permute-start.13 = (bf16[256,770]{1,0:T(8,128)(2,1)S(1)}, bf16[256,770]{1,0:T(8,128)(2,1)S(1)}, u32[]{:S(2)}, u32[]{:S(2)}) collective-permute-start(bf16[256,770]{1,0:T(8,128)(2,1)S(1)} %pad_maximum_fusion.4), channel_id=1, source_target_pairs={{0,1},{1,0},{2,3},{3,2},{4,5},{5,4},{6,7},{7,6},{8,9},{9,8},{10,11... | collective-permute-start | bytes 1182728 | tf_op jit(solution)/shard_map/ppermute | solution.py:82
  129.2 7.8 %collective-permute-start.14 = (bf16[256,384]{1,0:T(8,128)(2,1)S(1)}, bf16[256,384]{1,0:T(8,128)(2,1)S(1)}, u32[]{:S(2)}, u32[]{:S(2)}) collective-permute-start(bf16[256,384]{1,0:T(8,128)(2,1)S(1)} %get-tuple-element.41), channel_id=1, source_target_pairs={{0,1},{1,0},{2,3},{3,2},{4,5},{5,4},{6,7},{7,6},{8,9},{9,8},{10,11... | collective-permute-start | bytes 589832 | tf_op jit(solution)/shard_map/ppermute | solution.py:82
  130.7 8.8 %collective-permute-start.16 = (bf16[256,384]{1,0:T(8,128)(2,1)S(1)}, bf16[256,384]{1,0:T(8,128)(2,1)S(1)}, u32[]{:S(2)}, u32[]{:S(2)}) collective-permute-start(bf16[256,384]{1,0:T(8,128)(2,1)S(1)} %get-tuple-element.42), channel_id=1, source_target_pairs={{0,1},{1,0},{2,3},{3,2},{4,5},{5,4},{6,7},{7,6},{8,9},{9,8},{10,11... | collective-permute-start | bytes 589832 | tf_op jit(solution)/shard_map/ppermute | solution.py:82
  141.6 17.2 %copy-start.4 = (f32[32,512]{1,0:T(8,128)S(1)}, f32[32,512]{1,0:T(8,128)}, u32[]{:S(2)}) copy-start(f32[32,512]{1,0:T(8,128)} %copy-done.3) | copy-start | bytes 196612
  141.6 17.9 %copy-start.1 = (bf16[2048,512]{1,0:T(8,128)(2,1)S(1)}, bf16[2048,512]{1,0:T(8,128)(2,1)}, u32[]{:S(2)}) copy-start(bf16[2048,512]{1,0:T(8,128)(2,1)} %param.18) | copy-start | bytes 6291460
  141.6 2.0 %collective-permute-start.17 = (bf16[4,32,2048]{2,1,0:T(8,128)(2,1)S(1)}, bf16[4,32,2048]{2,1,0:T(8,128)(2,1)S(1)}, u32[]{:S(2)}, u32[]{:S(2)}) collective-permute-start(bf16[4,32,2048]{2,1,0:T(8,128)(2,1)S(1)} %bitcast.188), channel_id=1, source_target_pairs={{0,2},{2,0},{4,6},{6,4},{8,10},{10,8},{12,14},{14,12},{1,3},{3,1},... | collective-permute-start | bytes 1572872 | tf_op jit(solution)/shard_map/ppermute | solution.py:82
  143.8 7.8 %collective-permute-start.18 = (bf16[32,2048]{1,0:T(8,128)(2,1)S(1)}, bf16[32,2048]{1,0:T(8,128)(2,1)S(1)}, u32[]{:S(2)}, u32[]{:S(2)}) collective-permute-start(bf16[32,2048]{1,0:T(8,128)(2,1)S(1)} %get-tuple-element.13), channel_id=1, source_target_pairs={{0,4},{2,6},{4,0},{6,2},{8,12},{10,14},{12,8},{14,10},{1,5},{3,7},... | collective-permute-start | bytes 393224 | tf_op jit(solution)/shard_map/ppermute | solution.py:82
  145.9 12.9 %collective-permute-start.19 = (bf16[32,2048]{1,0:T(8,128)(2,1)S(1)}, bf16[32,2048]{1,0:T(8,128)(2,1)S(1)}, u32[]{:S(2)}, u32[]{:S(2)}) collective-permute-start(bf16[32,2048]{1,0:T(8,128)(2,1)S(1)} %get-tuple-element.15), channel_id=1, source_target_pairs={{0,8},{2,10},{4,12},{6,14},{8,0},{10,2},{12,4},{14,6},{1,9},{3,11}... | collective-permute-start | bytes 393224 | tf_op jit(solution)/shard_map/ppermute | solution.py:82
  147.0 11.8 %collective-permute-start.20 = (bf16[32,2048]{1,0:T(8,128)(2,1)S(1)}, bf16[32,2048]{1,0:T(8,128)(2,1)S(1)}, u32[]{:S(2)}, u32[]{:S(2)}) collective-permute-start(bf16[32,2048]{1,0:T(8,128)(2,1)S(1)} %get-tuple-element.14), channel_id=1, source_target_pairs={{0,12},{2,14},{4,8},{6,10},{8,4},{10,6},{12,0},{14,2},{1,13},{3,15... | collective-permute-start | bytes 393224 | tf_op jit(solution)/shard_map/ppermute | solution.py:82

commit v2 on v1

--- a/solution.py
+++ b/solution.py
@@ -1,8 +1,11 @@
+import functools
 import math
 
 import jax
 import jax.numpy as jnp
 from jax import lax
+from jax.experimental import pallas as pl
+from jax.experimental.pallas import tpu as pltpu
 from jax.sharding import PartitionSpec as P
 
 NEG = -1e30
@@ -75,6 +78,168 @@
     )
     attended = jnp.moveaxis(numerator / denominator[..., None], 1, 0)
     return attended.reshape(step_count, req_count, head_count * head_width).astype(jnp.bfloat16)
+
+
+def attend_kernel(
+    req_count, group, page_len, q_ref, code_ref, extra_ref, fresh_hbm, kv_hbm, out_ref,
+    kbuf, vbuf, fkbuf, fvbuf, s_ref, acc_ref, l_ref, m_ref, ksem, vsem, fsem,
+):
+    f32, bf16 = jnp.float32, jnp.bfloat16
+    width = q_ref.shape[2]
+    blocks, columns = code_ref.shape
+    tokens = columns // 2
+    rows = q_ref.shape[0] * group
+
+    def fetch(half, buf, sem, b):
+        part = pl.ds(b * tokens, tokens)
+        return pltpu.make_async_copy(
+            kv_hbm.at[part, :, pl.ds(half * width, width)], buf.at[part], sem.at[b]
+        )
+
+    fresh_copies = [
+        pltpu.make_async_copy(fresh_hbm.at[:, :, pl.ds(h * width, width)], buf, fsem.at[h])
+        for h, buf in enumerate((fkbuf, fvbuf))
+    ]
+    for copy in fresh_copies:
+        copy.start()
+    lax.fori_loop(0, blocks, lambda b, c: (fetch(0, kbuf, ksem, b).start(), c)[1], 0)
+    lax.fori_loop(0, blocks, lambda b, c: (fetch(1, vbuf, vsem, b).start(), c)[1], 0)
+
+    q = q_ref[...].astype(f32)
+    q2 = jnp.concatenate(
+        [q[:, :group].reshape(rows, width), q[:, group:].reshape(rows, width)], axis=1
+    ).astype(bf16)
+    row = lax.broadcasted_iota(jnp.int32, (rows, 1), 0) // group
+    row_req, row_step = row % req_count, row // req_count
+
+    def widen(x):
+        even = lax.broadcasted_iota(jnp.int32, x.shape, 0) % 2 == 0
+        x = x.astype(f32)
+        return jnp.concatenate(
+            [jnp.where(even, x, 0.0), jnp.where(even, 0.0, x)], axis=1
+        ).astype(bf16)
+
+    def scores(keys):
+        return lax.dot_general(
+            q2, widen(keys), (((1,), (1,)), ((), ())), preferred_element_type=f32
+        )
+
+    for copy in fresh_copies:
+        copy.wait()
+    fresh = fkbuf.shape[0] * 2
+    fresh_keys = fkbuf.reshape(fresh, width)[...]
+    col = lax.broadcasted_iota(jnp.int32, (1, fresh), 1) // 2
+    allowed = (col % req_count == row_req) & (col // req_count <= row_step)
+    fresh_scores = jnp.where(allowed, scores(fresh_keys), NEG)
+
+    m_ref[...] = jnp.full(m_ref.shape, NEG, f32)
+    slot = lax.broadcasted_iota(jnp.int32, (1, columns), 1) // 2 % page_len
+
+    def first(b, c):
+        fetch(0, kbuf, ksem, b).wait()
+        keys = kbuf.reshape(kbuf.shape[0] * 2, width)[pl.ds(b * columns, columns), :]
+        code = code_ref[pl.ds(b, 1), :]
+        owner = jnp.where(slot < (code & 31), code >> 5, -1)
+        s = jnp.where(owner == row_req, scores(keys), NEG)
+        s_ref[b] = s
+        m = m_ref[...]
+        for t in range(columns // width):
+            m = jnp.maximum(m, s[:, t * width : (t + 1) * width])
+        m_ref[...] = m
+        return c
+
+    lax.fori_loop(0, blocks, first, 0)
+
+    even = lax.broadcasted_iota(jnp.int32, (1, width), 1) % 2 == 0
+    even_fresh = lax.broadcasted_iota(jnp.int32, (1, fresh), 1) % 2 == 0
+
+    def best(flag, flag_fresh):
+        pool = jnp.max(jnp.where(flag, m_ref[...], NEG), axis=1, keepdims=True)
+        new = jnp.max(jnp.where(flag_fresh, fresh_scores, NEG), axis=1, keepdims=True)
+        return jnp.maximum(pool, new)
+
+    best_even, best_odd = best(even, even_fresh), best(~even, ~even_fresh)
+    m_ref[...] = jnp.where(even, best_even, best_odd)
+    rate = math.log2(math.e) / math.sqrt(width)
+    fresh_probs = jnp.exp2((fresh_scores - jnp.where(even_fresh, best_even, best_odd)) * rate)
+    acc_ref[...] = jnp.dot(
+        fresh_probs.astype(bf16), widen(fvbuf.reshape(fresh, width)[...]), preferred_element_type=f32
+    )
+    l_ref[...] = jnp.zeros(l_ref.shape, f32)
+
+    def second(b, c):
+        fetch(1, vbuf, vsem, b).wait()
+        values = vbuf.reshape(vbuf.shape[0] * 2, width)[pl.ds(b * columns, columns), :]
+        m = m_ref[...]
+        total = l_ref[...]
+        probs = []
+        for t in range(columns // width):
+            p = jnp.exp2((s_ref[b, :, t * width : (t + 1) * width] - m) * rate)
+            total = total + p
+            probs.append(p.astype(bf16))
+        l_ref[...] = total
+        acc_ref[...] += jnp.dot(
+            jnp.concatenate(probs, axis=1), widen(values), preferred_element_type=f32
+        )
+        return c
+
+    lax.fori_loop(0, blocks, second, 0)
+
+    for h, (flag, flag_fresh) in enumerate(((even, even_fresh), (~even, ~even_fresh))):
+        total = jnp.sum(jnp.where(flag, l_ref[...], 0.0), axis=1, keepdims=True)
+        total = total + jnp.sum(jnp.where(flag_fresh, fresh_probs, 0.0), axis=1, keepdims=True)
+        m_ref[...] = acc_ref[:, h * width : (h + 1) * width] / total
+        for g in range(group):
+            at = (h * group + g) * width
+            out_ref[:, at : at + width] = m_ref[pl.ds(g, rows // group, stride=group), :].astype(bf16)
+    out_ref[:, 2 * group * width :] = extra_ref[...]
+
+
+def attend_pool(queries, fresh_kv, kv_pool, page_table, context_lengths, extra):
+    step_count, req_count, head_count, head_width = queries.shape
+    pool_pages, page_len, kv_heads, _ = kv_pool.shape
+    group = head_count // kv_heads
+    slot = jnp.arange(page_table.shape[1], dtype=jnp.int32)
+    live = jnp.clip(context_lengths[:, None] - slot[None, :] * page_len, 0, page_len)
+    entry = jnp.arange(req_count, dtype=jnp.int32)[:, None] * 32 + live
+    pages = jnp.arange(pool_pages, dtype=jnp.int32)
+    code = jnp.sum(
+        jnp.where(page_table[:, :, None] == pages, entry[:, :, None], 0), axis=(0, 1)
+    )
+    blocks = 10
+    code = jnp.repeat(code, page_len * kv_heads).reshape(blocks, -1)
+    tokens = pool_pages * page_len
+    rows, columns = step_count * req_count * group, tokens * 2 // blocks
+    bf16, f32 = jnp.bfloat16, jnp.float32
+    vmem, anyspace = pl.BlockSpec(memory_space=pltpu.VMEM), pl.BlockSpec(memory_space=pl.ANY)
+    own = step_count * req_count
+    return pl.pallas_call(
+        functools.partial(attend_kernel, req_count, group, page_len),
+        out_shape=jax.ShapeDtypeStruct((own, head_count * head_width + extra.shape[1]), bf16),
+        in_specs=[vmem, vmem, vmem, anyspace, anyspace],
+        out_specs=vmem,
+        scratch_shapes=[
+            pltpu.VMEM((tokens, 2, head_width), bf16),
+            pltpu.VMEM((tokens, 2, head_width), bf16),
+            pltpu.VMEM((own, 2, head_width), bf16),
+            pltpu.VMEM((own, 2, head_width), bf16),
+            pltpu.VMEM((blocks, rows, columns), f32),
+            pltpu.VMEM((rows, 2 * head_width), f32),
+            pltpu.VMEM((rows, head_width), f32),
+            pltpu.VMEM((rows, head_width), f32),
+            pltpu.SemaphoreType.DMA((blocks,)),
+            pltpu.SemaphoreType.DMA((blocks,)),
+            pltpu.SemaphoreType.DMA((2,)),
+        ],
+        compiler_params=pltpu.CompilerParams(vmem_limit_bytes=40 * 1024 * 1024),
+        name="attend_pool",
+    )(
+        queries.reshape(own, head_count, head_width),
+        code,
+        extra,
+        fresh_kv.reshape(own, kv_heads, 2 * head_width),
+        kv_pool.reshape(tokens, kv_heads, 2 * head_width),
+    )
 
 
 def exchange(value, axis, mask):
@@ -127,21 +292,20 @@
     named = expert_ids[..., None] == catalog
     routed = jnp.sum(jnp.where(named, share[..., None], 0.0), axis=2)
 
-    attended = attend(queries, fresh_kv, kv_pool, page_table, context_lengths)
-    steps, reqs, head_cols = attended.shape
+    steps, reqs = queries.shape[:2]
     own = steps * reqs
     total = dp_count * own
+    head_cols = queries.shape[2] * queries.shape[3]
     extra = -(-2 * expert_total // 128) * 128
     routed_high, routed_low = split_pair(routed.reshape(own, expert_total))
-    packed = jnp.concatenate(
-        [
-            attended.reshape(own, head_cols),
-            routed_high,
-            routed_low,
-            jnp.zeros((own, extra - 2 * expert_total), bf16),
-        ],
-        axis=1,
-    )
+    routed = jnp.concatenate(
+        [routed_high, routed_low, jnp.zeros((own, extra - 2 * expert_total), bf16)], axis=1
+    )
+    if kv_pool.shape[2] == 2:
+        packed = attend_pool(queries, fresh_kv, kv_pool, page_table, context_lengths, routed)
+    else:
+        attended = attend(queries, fresh_kv, kv_pool, page_table, context_lengths)
+        packed = jnp.concatenate([attended.reshape(own, head_cols), routed], axis=1)
     gathered = gather_rows(packed).reshape(total, head_cols + extra)
     routes = gathered[:, head_cols : head_cols + 2 * expert_total].astype(f32)
     routes = routes[:, :expert_total] + routes[:, expert_total:]

time: 160 us -> 145 us (0.906)
  matrix products: 32.6 us -> 14.3 us
  Pallas kernels: 0 us -> 14.4 us
  other arithmetic: 16.9 us -> 11.5 us
  local copies, waits for them, and re-layouts: 13.2 us -> 7.92 us
    dot_general x6 -> x0, matrix products: 18 us -> none  [the longest x1 5.26 us: attend(): jnp.einsum('pskgd,ptkd->pskgt', page_query, key_rows, preferred_element_t...]
    pallas_call x0 -> x1, Pallas kernels: none -> 14.4 us  [attend_pool(): pl.pallas_call(functools.partial(attend_kernel, req_count, group, page_le...]
    reduce_sum x4 -> x1, other arithmetic: 12.1 us -> 2.3 us  [attend_pool(): jnp.sum(jnp.where(page_table[:, :, None] == pages, entry[:, :, None], 0),...]
    slice x2 -> x0, local copies, waits for them, and re-layouts: 7.6 us -> none  [the longest x1 6.98 us: attend(): key_rows = pool_block[..., :head_width]]
    unnamed x34 -> x22, local copies, waits for them, and re-layouts: 1.82 us -> 6.69 us
    another operation x4, other arithmetic: 0.43 us -> 3.18 us  [gather_rows(): return jnp.stack([mine, exchange(mine, 'dp', 1)])]
  transfers between devices with their start and end apart: 21 -> 21, of which waited for: 18 -> 17; matrix products, arithmetic and copies ran while one was open for 1% -> 1% of each run, Pallas kernels for 0% -> 0%
where the time goes in v2:
time: 145 us; the launch traced here: 144 us
  waiting for transfers between devices  71.2 us (49%)
  starting transfers between devices  24.3 us (17%)
  Pallas kernels  14.4 us (10%)
  matrix products  14.3 us (10%)
  other arithmetic  11.5 us (8%)
  local copies, waits for them, and re-layouts  7.92 us (5%)
    ppermute x21, waiting for transfers between devices, exchange(): return lax.ppermute(value, axis, [(i, i ^ mask) for i in range(count)])  71.2 us
    ppermute x21, starting transfers between devices, exchange(): return lax.ppermute(value, axis, [(i, i ^ mask) for i in range(count)])  24.3 us
    pallas_call x1, Pallas kernels, attend_pool(): pl.pallas_call(functools.partial(attend_kernel, req_count, group, page_le...  14.4 us
    unnamed x22, local copies, waits for them, and re-layouts  6.69 us
    dot_general x2, matrix products, body(): gate = jnp.dot(rows, gate_up[e, 0], preferred_element_type=f32)  5.94 us
    dot_general x2, matrix products, body(): up = jnp.dot(rows, gate_up[e, 1], preferred_element_type=f32)  5.79 us
    another operation x4, other arithmetic, gather_rows(): return jnp.stack([mine, exchange(mine, 'dp', 1)])  3.18 us
  transfers between devices with their start and end apart: 21, of which 17 were waited for; matrix products, arithmetic and copies ran while one was open for 1% of the time, Pallas kernels for 0%

profile of v2, /device:TPU:0, one launch (start us, length us, event | category | flops | bytes accessed | tf_op | source)
XLA Modules:
  0.0 144.1 jit_solution(11953645311031358673)
XLA Ops:
  0.0 0.9 clamp_add_fusion
  1.0 0.8 copy.27
  1.9 2.3 %select_reduce_fusion = s32[320]{0:T(512)S(1)} fusion(s32[16,305]{0,1:T(8,128)S(1)} %copy.28, s32[16,305]{0,1:T(8,128)S(1)} %copy.27), kind=kLoop, calls=%fused_computation | loop fusion | flops 4684480 | bytes 40320 | tf_op jit(solution)/shard_map/reduce_sum | solution.py:206
  4.5 0.7 reduce_sum.66
  5.2 0.7 broadcast_divide_fusion
  6.0 0.8 copy.29
  7.1 2.5 %copy-done.1 = bf16[320,16,2,256]{3,2,1,0:T(2,128)(2,1)S(1)} copy-done((bf16[320,16,2,256]{3,2,1,0:T(2,128)(2,1)S(1)}, bf16[320,16,2,256]{3,2,1,0:T(2,128)(2,1)}, u32[]{:S(2)}) %copy-start.1) | copy-done | bytes 5242904
  9.6 0.9 copy-done.2
  10.5 0.8 copy-done.3
  11.2 14.4 %attend_pool.1 = bf16[32,2176]{1,0:T(8,128)(2,1)S(1)} custom-call(bf16[32,16,128]{2,1,0:T(8,128)(2,1)S(1)} %bitcast.95, s32[10,1024]{1,0:T(8,128)S(1)} %broadcast_in_dim.77.code_ref, bf16[32,128]{1,0:T(8,128)(2,1)S(1)} %maximum_maximum_fusion.extra_ref, bf16[32,2,256]{2,1,0:T(2,128)(2,1)S(1)} %bitcast.96, bf16[5120,2,256]{2,1,0:T(2,128)(2,1)S(1)} %bitcast.93), custom_call_target="tpu_custom_call" | custom-call | tf_op jit(solution)/shard_map/attend_pool/pallas_call | solution.py:216
  25.7 5.1 %collective-permute-start.2 = (bf16[32,2176]{1,0:T(8,128)(2,1)S(1)}, bf16[32,2176]{1,0:T(8,128)(2,1)S(1)}, u32[]{:S(2)}, u32[]{:S(2)}) collective-permute-start(bf16[32,2176]{1,0:T(8,128)(2,1)S(1)} %attend_pool.1), channel_id=1, source_target_pairs={{0,12},{2,14},{4,8},{6,10},{8,4},{10,6},{12,0},{14,2},{1,13},{3,15... | collective-permute-start | bytes 417800 | tf_op jit(solution)/shard_map/ppermute | solution.py:247
  31.5 4.0 %collective-permute-done.2 = bf16[32,2176]{1,0:T(8,128)(2,1)S(1)} collective-permute-done((bf16[32,2176]{1,0:T(8,128)(2,1)S(1)}, bf16[32,2176]{1,0:T(8,128)(2,1)S(1)}, u32[]{:S(2)}, u32[]{:S(2)}) %collective-permute-start.2) | collective-permute-done | bytes 139296 | tf_op jit(solution)/shard_map/ppermute | solution.py:247
  35.5 7.1 %collective-permute-done.1 = bf16[32,2176]{1,0:T(8,128)(2,1)S(1)} collective-permute-done((bf16[32,2176]{1,0:T(8,128)(2,1)S(1)}, bf16[32,2176]{1,0:T(8,128)(2,1)S(1)}, u32[]{:S(2)}, u32[]{:S(2)}) %collective-permute-start.1) | collective-permute-done | bytes 139296 | tf_op jit(solution)/shard_map/ppermute | solution.py:247
  42.8 1.9 %collective-permute-done.3 = bf16[4,32,2176]{2,1,0:T(8,128)(2,1)S(1)} collective-permute-done((bf16[4,32,2176]{2,1,0:T(8,128)(2,1)S(1)}, bf16[4,32,2176]{2,1,0:T(8,128)(2,1)S(1)}, u32[]{:S(2)}, u32[]{:S(2)}) %collective-permute-start.3) | collective-permute-done | bytes 557088 | tf_op jit(solution)/shard_map/ppermute | solution.py:247
  44.9 0.7 convolution_convert_fusion
  46.0 1.2 collective-permute-done.4
  47.3 2.6 %collective-permute-start.6 = (bf16[2,32,512]{2,1,0:T(8,128)(2,1)S(1)}, bf16[2,32,512]{2,1,0:T(8,128)(2,1)S(1)}, u32[]{:S(2)}, u32[]{:S(2)}) collective-permute-start(bf16[2,32,512]{2,1,0:T(8,128)(2,1)S(1)} %get-tuple-element.23), channel_id=1, source_target_pairs={{0,12},{2,14},{4,8},{6,10},{8,4},{10,6},{12,0},{14,2},{1,13},{3,15... | collective-permute-start | bytes 196616 | tf_op jit(solution)/shard_map/ppermute | solution.py:247
  49.9 0.9 collective-permute-start.5
  50.8 0.8 collective-permute-done.7
  51.6 2.3 %collective-permute-done.6 = bf16[2,32,512]{2,1,0:T(8,128)(2,1)S(1)} collective-permute-done((bf16[2,32,512]{2,1,0:T(8,128)(2,1)S(1)}, bf16[2,32,512]{2,1,0:T(8,128)(2,1)S(1)}, u32[]{:S(2)}, u32[]{:S(2)}) %collective-permute-start.6) | collective-permute-done | bytes 65568 | tf_op jit(solution)/shard_map/ppermute | solution.py:247
  53.9 3.2 %collective-permute-done.5 = bf16[2,32,512]{2,1,0:T(8,128)(2,1)S(1)} collective-permute-done((bf16[2,32,512]{2,1,0:T(8,128)(2,1)S(1)}, bf16[2,32,512]{2,1,0:T(8,128)(2,1)S(1)}, u32[]{:S(2)}, u32[]{:S(2)}) %collective-permute-start.5) | collective-permute-done | bytes 65568 | tf_op jit(solution)/shard_map/ppermute | solution.py:247
  57.1 1.6 %collective-permute-start.8 = (bf16[32,2048]{1,0:T(8,128)(2,1)S(1)}, bf16[32,2048]{1,0:T(8,128)(2,1)S(1)}, u32[]{:S(2)}, u32[]{:S(2)}) collective-permute-start(bf16[32,2048]{1,0:T(8,128)(2,1)S(1)} %broadcast_select_fusion.4), channel_id=1, source_target_pairs={{0,1},{1,0},{2,3},{3,2},{4,5},{5,4},{6,7},{7,6},{8,9},{9,8},{10,11... | collective-permute-start | bytes 393224 | tf_op jit(solution)/shard_map/ppermute | solution.py:247
  58.7 3.5 %collective-permute-done.8 = bf16[32,2048]{1,0:T(8,128)(2,1)S(1)} collective-permute-done((bf16[32,2048]{1,0:T(8,128)(2,1)S(1)}, bf16[32,2048]{1,0:T(8,128)(2,1)S(1)}, u32[]{:S(2)}, u32[]{:S(2)}) %collective-permute-start.8) | collective-permute-done | bytes 131104 | tf_op jit(solution)/shard_map/ppermute | solution.py:247
  62.8 2.3 %collective-permute-start.11 = (bf16[32,2176]{1,0:T(8,128)(2,1)S(1)}, bf16[32,2176]{1,0:T(8,128)(2,1)S(1)}, u32[]{:S(2)}, u32[]{:S(2)}) collective-permute-start(bf16[32,2176]{1,0:T(8,128)(2,1)S(1)} %concatenate.44), channel_id=1, source_target_pairs={{0,12},{2,14},{4,8},{6,10},{8,4},{10,6},{12,0},{14,2},{1,13},{3,15... | collective-permute-start | bytes 417800 | tf_op jit(solution)/shard_map/ppermute | solution.py:247
  65.2 2.1 %collective-permute-start.9 = (bf16[32,2176]{1,0:T(8,128)(2,1)S(1)}, bf16[32,2176]{1,0:T(8,128)(2,1)S(1)}, u32[]{:S(2)}, u32[]{:S(2)}) collective-permute-start(bf16[32,2176]{1,0:T(8,128)(2,1)S(1)} %concatenate.44), channel_id=1, source_target_pairs={{0,4},{2,6},{4,0},{6,2},{8,12},{10,14},{12,8},{14,10},{1,5},{3,7},... | collective-permute-start | bytes 417800 | tf_op jit(solution)/shard_map/ppermute | solution.py:247
  67.3 4.0 %collective-permute-done.11 = bf16[32,2176]{1,0:T(8,128)(2,1)S(1)} collective-permute-done((bf16[32,2176]{1,0:T(8,128)(2,1)S(1)}, bf16[32,2176]{1,0:T(8,128)(2,1)S(1)}, u32[]{:S(2)}, u32[]{:S(2)}) %collective-permute-start.11) | collective-permute-done | bytes 139296 | tf_op jit(solution)/shard_map/ppermute | solution.py:247
  71.3 4.8 %collective-permute-done.10 = bf16[32,2176]{1,0:T(8,128)(2,1)S(1)} collective-permute-done((bf16[32,2176]{1,0:T(8,128)(2,1)S(1)}, bf16[32,2176]{1,0:T(8,128)(2,1)S(1)}, u32[]{:S(2)}, u32[]{:S(2)}) %collective-permute-start.10) | collective-permute-done | bytes 139296 | tf_op jit(solution)/shard_map/ppermute | solution.py:247
  76.0 0.7 copy-done.6
  76.7 1.8 %fusion.46 = (bf16[1,4,32,2176]{3,2,1,0:T(8,128)(2,1)S(1)}, bf16[4,32,2176]{2,1,0:T(8,128)(2,1)}) fusion(bf16[1,32,2176]{2,1,0:T(8,128)(2,1)S(1)} %bitcast.115, bf16[1,32,2176]{2,1,0:T(8,128)(2,1)S(1)} %bitcast.116, bf16[1,32,2176]{2,1,0:T(8,128)(2,1)} %bitcast.118, bf16[1,32,2176]{2,1,0:T(8,128)(2,1)S(1)} %bitcast.110), kind=kLoop, calls=%fused_computation.117 | loop fusion | flops 835584 | bytes 1671168 | tf_op jit(solution)/shard_map/stack | solution.py:266
  78.6 0.8 slice_convert_fusion.1
  79.6 1.2 collective-permute-done.12
  80.8 1.2 pad_maximum_fusion.1
  82.0 2.9 %fusion.4 = f32[256,768]{1,0:T(8,128)S(1)} fusion(bf16[2,2,2048,768]{3,2,1,0:T(8,128)(2,1)} %param.22, bf16[256,2176]{1,0:T(8,128)(2,1)S(1)} %bitcast.99), kind=kOutput, calls=%fused_computation.6 | convolution fusion | flops 805306368 | bytes 4980736 | tf_op jit(solution)/shard_map/dot_general | solution.py:352
  84.9 2.9 %fusion.6 = f32[256,768]{1,0:T(8,128)S(1)} fusion(bf16[2,2,2048,768]{3,2,1,0:T(8,128)(2,1)} %param.22, bf16[256,2176]{1,0:T(8,128)(2,1)S(1)} %bitcast.100), kind=kOutput, calls=%fused_computation.8 | convolution fusion | flops 805306368 | bytes 4980736 | tf_op jit(solution)/shard_map/dot_general | solution.py:351
  87.8 2.9 %fusion = f32[256,768]{1,0:T(8,128)S(1)} fusion(bf16[2,2,2048,768]{3,2,1,0:T(8,128)(2,1)} %param.22, bf16[256,2176]{1,0:T(8,128)(2,1)S(1)} %bitcast.101), kind=kOutput, calls=%fused_computation.2 | convolution fusion | flops 805306368 | bytes 4980736 | tf_op jit(solution)/shard_map/dot_general | solution.py:352
  90.7 3.0 %fusion.2 = f32[256,768]{1,0:T(8,128)S(1)} fusion(bf16[2,2,2048,768]{3,2,1,0:T(8,128)(2,1)} %param.22, bf16[256,2176]{1,0:T(8,128)(2,1)S(1)} %bitcast.102), kind=kOutput, calls=%fused_computation.4 | convolution fusion | flops 805306368 | bytes 4980736 | tf_op jit(solution)/shard_map/dot_general | solution.py:351
  93.9 1.5 %collective-permute-start.13 = (bf16[256,770]{1,0:T(8,128)(2,1)S(1)}, bf16[256,770]{1,0:T(8,128)(2,1)S(1)}, u32[]{:S(2)}, u32[]{:S(2)}) collective-permute-start(bf16[256,770]{1,0:T(8,128)(2,1)S(1)} %pad_maximum_fusion.4), channel_id=1, source_target_pairs={{0,1},{1,0},{2,3},{3,2},{4,5},{5,4},{6,7},{7,6},{8,9},{9,8},{10,11... | collective-permute-start | bytes 1182728 | tf_op jit(solution)/shard_map/ppermute | solution.py:247
  96.4 18.6 %collective-permute-done.15 = bf16[256,768]{1,0:T(8,128)(2,1)S(1)} collective-permute-done((bf16[256,768]{1,0:T(8,128)(2,1)S(1)}, bf16[256,768]{1,0:T(8,128)(2,1)S(1)}, u32[]{:S(2)}, u32[]{:S(2)}) %collective-permute-start.15) | collective-permute-done | bytes 393248 | tf_op jit(solution)/shard_map/ppermute | solution.py:247
  115.7 1.6 %collective-permute-start.16 = (bf16[256,384]{1,0:T(8,128)(2,1)S(1)}, bf16[256,384]{1,0:T(8,128)(2,1)S(1)}, u32[]{:S(2)}, u32[]{:S(2)}) collective-permute-start(bf16[256,384]{1,0:T(8,128)(2,1)S(1)} %get-tuple-element.38), channel_id=1, source_target_pairs={{0,1},{1,0},{2,3},{3,2},{4,5},{5,4},{6,7},{7,6},{8,9},{9,8},{10,11... | collective-permute-start | bytes 589832 | tf_op jit(solution)/shard_map/ppermute | solution.py:247
  117.8 5.7 %collective-permute-done.16 = bf16[256,384]{1,0:T(8,128)(2,1)S(1)} collective-permute-done((bf16[256,384]{1,0:T(8,128)(2,1)S(1)}, bf16[256,384]{1,0:T(8,128)(2,1)S(1)}, u32[]{:S(2)}, u32[]{:S(2)}) %collective-permute-start.16) | collective-permute-done | bytes 196640 | tf_op jit(solution)/shard_map/ppermute | solution.py:247
  123.6 2.5 %collective-permute-done.14 = bf16[256,384]{1,0:T(8,128)(2,1)S(1)} collective-permute-done((bf16[256,384]{1,0:T(8,128)(2,1)S(1)}, bf16[256,384]{1,0:T(8,128)(2,1)S(1)}, u32[]{:S(2)}, u32[]{:S(2)}) %collective-permute-start.14) | collective-permute-done | bytes 196640 | tf_op jit(solution)/shard_map/ppermute | solution.py:247
  126.1 1.9 %fusion.13 = f32[256,2048]{1,0:T(8,128)S(1)} fusion(bf16[1536,2048]{1,0:T(8,128)(2,1)S(1)} %bitcast.126, bf16[256,384]{1,0:T(8,128)(2,1)S(1)} %get-tuple-element.17, bf16[256,384]{1,0:T(8,128)(2,1)S(1)} %get-tuple-element.16, bf16[256,384]{1,0:T(8,128)(2,1)S(1)} %get-tuple-element.15, bf16[256,384]{1,0:T(8,128)(2,1)S(1)} %get-tuple-element.14), kind=kOutput, calls=%fused_computation.20 | convolution fusion | flops 1613758464 | bytes 9175040 | tf_op jit(solution)/shard_map/dot_general | solution.py:374
  128.2 1.8 %collective-permute-done.17 = bf16[4,32,2048]{2,1,0:T(8,128)(2,1)S(1)} collective-permute-done((bf16[4,32,2048]{2,1,0:T(8,128)(2,1)S(1)}, bf16[4,32,2048]{2,1,0:T(8,128)(2,1)S(1)}, u32[]{:S(2)}, u32[]{:S(2)}) %collective-permute-start.17) | collective-permute-done | bytes 524320 | tf_op jit(solution)/shard_map/ppermute | solution.py:247
  130.3 2.0 %collective-permute-start.20 = (bf16[32,2048]{1,0:T(8,128)(2,1)S(1)}, bf16[32,2048]{1,0:T(8,128)(2,1)S(1)}, u32[]{:S(2)}, u32[]{:S(2)}) collective-permute-start(bf16[32,2048]{1,0:T(8,128)(2,1)S(1)} %get-tuple-element.12), channel_id=1, source_target_pairs={{0,12},{2,14},{4,8},{6,10},{8,4},{10,6},{12,0},{14,2},{1,13},{3,15... | collective-permute-start | bytes 393224 | tf_op jit(solution)/shard_map/ppermute | solution.py:247
  132.3 2.4 %collective-permute-start.18 = (bf16[32,2048]{1,0:T(8,128)(2,1)S(1)}, bf16[32,2048]{1,0:T(8,128)(2,1)S(1)}, u32[]{:S(2)}, u32[]{:S(2)}) collective-permute-start(bf16[32,2048]{1,0:T(8,128)(2,1)S(1)} %get-tuple-element.11), channel_id=1, source_target_pairs={{0,4},{2,6},{4,0},{6,2},{8,12},{10,14},{12,8},{14,10},{1,5},{3,7},... | collective-permute-start | bytes 393224 | tf_op jit(solution)/shard_map/ppermute | solution.py:247
  134.7 3.9 %collective-permute-done.20 = bf16[32,2048]{1,0:T(8,128)(2,1)S(1)} collective-permute-done((bf16[32,2048]{1,0:T(8,128)(2,1)S(1)}, bf16[32,2048]{1,0:T(8,128)(2,1)S(1)}, u32[]{:S(2)}, u32[]{:S(2)}) %collective-permute-start.20) | collective-permute-done | bytes 131104 | tf_op jit(solution)/shard_map/ppermute | solution.py:247
  138.6 4.7 %collective-permute-done.19 = bf16[32,2048]{1,0:T(8,128)(2,1)S(1)} collective-permute-done((bf16[32,2048]{1,0:T(8,128)(2,1)S(1)}, bf16[32,2048]{1,0:T(8,128)(2,1)S(1)}, u32[]{:S(2)}, u32[]{:S(2)}) %collective-permute-start.19) | collective-permute-done | bytes 131104 | tf_op jit(solution)/shard_map/ppermute | solution.py:247
  143.3 0.7 fusion.39
  (87 shorter events, 6.0 us)
Async XLA Ops:
  0.0 44.9 %copy-start = (bf16[2048,512]{1,0:T(8,128)(2,1)S(1)}, bf16[2048,512]{1,0:T(8,128)(2,1)}, u32[]{:S(2)}) copy-start(bf16[2048,512]{1,0:T(8,128)(2,1)} %param.18) | copy-start | bytes 6291460
  7.1 2.5 %copy-start.1 = (bf16[320,16,2,256]{3,2,1,0:T(2,128)(2,1)S(1)}, bf16[320,16,2,256]{3,2,1,0:T(2,128)(2,1)}, u32[]{:S(2)}) copy-start(bf16[320,16,2,256]{3,2,1,0:T(2,128)(2,1)} %param.14) | copy-start | bytes 15728644
  9.6 0.9 copy-start.2
  10.5 0.8 copy-start.3
  25.7 9.8 %collective-permute-start.2 = (bf16[32,2176]{1,0:T(8,128)(2,1)S(1)}, bf16[32,2176]{1,0:T(8,128)(2,1)S(1)}, u32[]{:S(2)}, u32[]{:S(2)}) collective-permute-start(bf16[32,2176]{1,0:T(8,128)(2,1)S(1)} %attend_pool.1), channel_id=1, source_target_pairs={{0,12},{2,14},{4,8},{6,10},{8,4},{10,6},{12,0},{14,2},{1,13},{3,15... | collective-permute-start | bytes 417800 | tf_op jit(solution)/shard_map/ppermute | solution.py:247
  30.8 11.8 %collective-permute-start.1 = (bf16[32,2176]{1,0:T(8,128)(2,1)S(1)}, bf16[32,2176]{1,0:T(8,128)(2,1)S(1)}, u32[]{:S(2)}, u32[]{:S(2)}) collective-permute-start(bf16[32,2176]{1,0:T(8,128)(2,1)S(1)} %attend_pool.1), channel_id=1, source_target_pairs={{0,8},{2,10},{4,12},{6,14},{8,0},{10,2},{12,4},{14,6},{1,9},{3,11}... | collective-permute-start | bytes 417800 | tf_op jit(solution)/shard_map/ppermute | solution.py:247
  30.8 11.8 %collective-permute-start = (bf16[32,2176]{1,0:T(8,128)(2,1)S(1)}, bf16[32,2176]{1,0:T(8,128)(2,1)S(1)}, u32[]{:S(2)}, u32[]{:S(2)}) collective-permute-start(bf16[32,2176]{1,0:T(8,128)(2,1)S(1)} %attend_pool.1), channel_id=1, source_target_pairs={{0,4},{2,6},{4,0},{6,2},{8,12},{10,14},{12,8},{14,10},{1,5},{3,7},... | collective-permute-start | bytes 417800 | tf_op jit(solution)/shard_map/ppermute | solution.py:247
  42.7 2.0 %collective-permute-start.3 = (bf16[4,32,2176]{2,1,0:T(8,128)(2,1)S(1)}, bf16[4,32,2176]{2,1,0:T(8,128)(2,1)S(1)}, u32[]{:S(2)}, u32[]{:S(2)}) collective-permute-start(bf16[4,32,2176]{2,1,0:T(8,128)(2,1)S(1)} %get-tuple-element.10), channel_id=1, source_target_pairs={{0,2},{2,0},{4,6},{6,4},{8,10},{10,8},{12,14},{14,12},{1,3},{3,1},... | collective-permute-start | bytes 1671176 | tf_op jit(solution)/shard_map/ppermute | solution.py:247
  44.9 1.0 copy-start.4
  45.6 16.7 %copy-start.5 = (bf16[2,16,2048]{2,1,0:T(8,128)(2,1)S(1)}, bf16[2,16,2048]{2,1,0:T(8,128)(2,1)}, u32[]{:S(2)}) copy-start(bf16[2,16,2048]{2,1,0:T(8,128)(2,1)} %param.17) | copy-start | bytes 393220
  45.6 16.7 %copy-start.7 = (f32[2048]{0:T(1024)S(1)}, f32[2048]{0:T(1024)}, u32[]{:S(2)}) copy-start(f32[2048]{0:T(1024)} %param.19) | copy-start | bytes 24580
  45.9 1.3 collective-permute-start.4
  47.2 4.3 %collective-permute-start.7 = (bf16[2,32,512]{2,1,0:T(8,128)(2,1)S(1)}, bf16[2,32,512]{2,1,0:T(8,128)(2,1)S(1)}, u32[]{:S(2)}, u32[]{:S(2)}) collective-permute-start(bf16[2,32,512]{2,1,0:T(8,128)(2,1)S(1)} %get-tuple-element.24), channel_id=1, source_target_pairs={{0,4},{2,6},{4,0},{6,2},{8,12},{10,14},{12,8},{14,10},{1,5},{3,7},... | collective-permute-start | bytes 196616 | tf_op jit(solution)/shard_map/ppermute | solution.py:247
  47.3 6.6 %collective-permute-start.6 = (bf16[2,32,512]{2,1,0:T(8,128)(2,1)S(1)}, bf16[2,32,512]{2,1,0:T(8,128)(2,1)S(1)}, u32[]{:S(2)}, u32[]{:S(2)}) collective-permute-start(bf16[2,32,512]{2,1,0:T(8,128)(2,1)S(1)} %get-tuple-element.23), channel_id=1, source_target_pairs={{0,12},{2,14},{4,8},{6,10},{8,4},{10,6},{12,0},{14,2},{1,13},{3,15... | collective-permute-start | bytes 196616 | tf_op jit(solution)/shard_map/ppermute | solution.py:247
  49.9 7.2 %collective-permute-start.5 = (bf16[2,32,512]{2,1,0:T(8,128)(2,1)S(1)}, bf16[2,32,512]{2,1,0:T(8,128)(2,1)S(1)}, u32[]{:S(2)}, u32[]{:S(2)}) collective-permute-start(bf16[2,32,512]{2,1,0:T(8,128)(2,1)S(1)} %get-tuple-element.22), channel_id=1, source_target_pairs={{0,8},{2,10},{4,12},{6,14},{8,0},{10,2},{12,4},{14,6},{1,9},{3,11}... | collective-permute-start | bytes 196616 | tf_op jit(solution)/shard_map/ppermute | solution.py:247
  57.1 5.1 %collective-permute-start.8 = (bf16[32,2048]{1,0:T(8,128)(2,1)S(1)}, bf16[32,2048]{1,0:T(8,128)(2,1)S(1)}, u32[]{:S(2)}, u32[]{:S(2)}) collective-permute-start(bf16[32,2048]{1,0:T(8,128)(2,1)S(1)} %broadcast_select_fusion.4), channel_id=1, source_target_pairs={{0,1},{1,0},{2,3},{3,2},{4,5},{5,4},{6,7},{7,6},{8,9},{9,8},{10,11... | collective-permute-start | bytes 393224 | tf_op jit(solution)/shard_map/ppermute | solution.py:247
  62.8 8.4 %collective-permute-start.11 = (bf16[32,2176]{1,0:T(8,128)(2,1)S(1)}, bf16[32,2176]{1,0:T(8,128)(2,1)S(1)}, u32[]{:S(2)}, u32[]{:S(2)}) collective-permute-start(bf16[32,2176]{1,0:T(8,128)(2,1)S(1)} %concatenate.44), channel_id=1, source_target_pairs={{0,12},{2,14},{4,8},{6,10},{8,4},{10,6},{12,0},{14,2},{1,13},{3,15... | collective-permute-start | bytes 417800 | tf_op jit(solution)/shard_map/ppermute | solution.py:247
  65.2 10.9 %collective-permute-start.10 = (bf16[32,2176]{1,0:T(8,128)(2,1)S(1)}, bf16[32,2176]{1,0:T(8,128)(2,1)S(1)}, u32[]{:S(2)}, u32[]{:S(2)}) collective-permute-start(bf16[32,2176]{1,0:T(8,128)(2,1)S(1)} %concatenate.44), channel_id=1, source_target_pairs={{0,8},{2,10},{4,12},{6,14},{8,0},{10,2},{12,4},{14,6},{1,9},{3,11}... | collective-permute-start | bytes 417800 | tf_op jit(solution)/shard_map/ppermute | solution.py:247
  65.2 10.9 %collective-permute-start.9 = (bf16[32,2176]{1,0:T(8,128)(2,1)S(1)}, bf16[32,2176]{1,0:T(8,128)(2,1)S(1)}, u32[]{:S(2)}, u32[]{:S(2)}) collective-permute-start(bf16[32,2176]{1,0:T(8,128)(2,1)S(1)} %concatenate.44), channel_id=1, source_target_pairs={{0,4},{2,6},{4,0},{6,2},{8,12},{10,14},{12,8},{14,10},{1,5},{3,7},... | collective-permute-start | bytes 417800 | tf_op jit(solution)/shard_map/ppermute | solution.py:247
  76.0 0.7 copy-start.6
  78.5 2.3 %collective-permute-start.12 = (bf16[4,32,2176]{2,1,0:T(8,128)(2,1)}, bf16[4,32,2176]{2,1,0:T(8,128)(2,1)}, u32[]{:S(2)}, u32[]{:S(2)}) collective-permute-start(bf16[4,32,2176]{2,1,0:T(8,128)(2,1)} %get-tuple-element.8), channel_id=1, source_target_pairs={{0,2},{2,0},{4,6},{6,4},{8,10},{10,8},{12,14},{14,12},{1,3},{3,1},... | collective-permute-start | bytes 1671176 | tf_op jit(solution)/shard_map/ppermute | solution.py:247
  90.7 35.4 %slice-start = ((s8[6291456]{0:T(1024)(128)(4,1)}), s8[4194304]{0:T(1024)(128)(4,1)S(1)}, s32[]{:S(2)}) async-start(s8[6291456]{0:T(1024)(128)(4,1)} %bitcast.124), calls=%async_computation | async-start | bytes 8388608
  93.9 32.2 %slice-start.1 = ((s8[6291456]{0:T(1024)(128)(4,1)}), s8[2097152]{0:T(1024)(128)(4,1)S(1)}, s32[]{:S(2)}) async-start(s8[6291456]{0:T(1024)(128)(4,1)} %bitcast.124), calls=%async_computation.1 | async-start | bytes 4194304
  93.9 21.1 %collective-permute-start.13 = (bf16[256,770]{1,0:T(8,128)(2,1)S(1)}, bf16[256,770]{1,0:T(8,128)(2,1)S(1)}, u32[]{:S(2)}, u32[]{:S(2)}) collective-permute-start(bf16[256,770]{1,0:T(8,128)(2,1)S(1)} %pad_maximum_fusion.4), channel_id=1, source_target_pairs={{0,1},{1,0},{2,3},{3,2},{4,5},{5,4},{6,7},{7,6},{8,9},{9,8},{10,11... | collective-permute-start | bytes 1182728 | tf_op jit(solution)/shard_map/ppermute | solution.py:247
  95.6 19.4 %collective-permute-start.15 = (bf16[256,768]{1,0:T(8,128)(2,1)S(1)}, bf16[256,768]{1,0:T(8,128)(2,1)S(1)}, u32[]{:S(2)}, u32[]{:S(2)}) collective-permute-start(bf16[256,768]{1,0:T(8,128)(2,1)S(1)} %pad_maximum_fusion.5), channel_id=1, source_target_pairs={{0,1},{1,0},{2,3},{3,2},{4,5},{5,4},{6,7},{7,6},{8,9},{9,8},{10,11... | collective-permute-start | bytes 1179656 | tf_op jit(solution)/shard_map/ppermute | solution.py:247
  115.7 7.8 %collective-permute-start.16 = (bf16[256,384]{1,0:T(8,128)(2,1)S(1)}, bf16[256,384]{1,0:T(8,128)(2,1)S(1)}, u32[]{:S(2)}, u32[]{:S(2)}) collective-permute-start(bf16[256,384]{1,0:T(8,128)(2,1)S(1)} %get-tuple-element.38), channel_id=1, source_target_pairs={{0,1},{1,0},{2,3},{3,2},{4,5},{5,4},{6,7},{7,6},{8,9},{9,8},{10,11... | collective-permute-start | bytes 589832 | tf_op jit(solution)/shard_map/ppermute | solution.py:247
  117.3 8.8 %collective-permute-start.14 = (bf16[256,384]{1,0:T(8,128)(2,1)S(1)}, bf16[256,384]{1,0:T(8,128)(2,1)S(1)}, u32[]{:S(2)}, u32[]{:S(2)}) collective-permute-start(bf16[256,384]{1,0:T(8,128)(2,1)S(1)} %get-tuple-element.37), channel_id=1, source_target_pairs={{0,1},{1,0},{2,3},{3,2},{4,5},{5,4},{6,7},{7,6},{8,9},{9,8},{10,11... | collective-permute-start | bytes 589832 | tf_op jit(solution)/shard_map/ppermute | solution.py:247
  128.1 2.0 %collective-permute-start.17 = (bf16[4,32,2048]{2,1,0:T(8,128)(2,1)S(1)}, bf16[4,32,2048]{2,1,0:T(8,128)(2,1)S(1)}, u32[]{:S(2)}, u32[]{:S(2)}) collective-permute-start(bf16[4,32,2048]{2,1,0:T(8,128)(2,1)S(1)} %bitcast.112), channel_id=1, source_target_pairs={{0,2},{2,0},{4,6},{6,4},{8,10},{10,8},{12,14},{14,12},{1,3},{3,1},... | collective-permute-start | bytes 1572872 | tf_op jit(solution)/shard_map/ppermute | solution.py:247
  130.3 8.4 %collective-permute-start.20 = (bf16[32,2048]{1,0:T(8,128)(2,1)S(1)}, bf16[32,2048]{1,0:T(8,128)(2,1)S(1)}, u32[]{:S(2)}, u32[]{:S(2)}) collective-permute-start(bf16[32,2048]{1,0:T(8,128)(2,1)S(1)} %get-tuple-element.12), channel_id=1, source_target_pairs={{0,12},{2,14},{4,8},{6,10},{8,4},{10,6},{12,0},{14,2},{1,13},{3,15... | collective-permute-start | bytes 393224 | tf_op jit(solution)/shard_map/ppermute | solution.py:247
  132.3 11.0 %collective-permute-start.19 = (bf16[32,2048]{1,0:T(8,128)(2,1)S(1)}, bf16[32,2048]{1,0:T(8,128)(2,1)S(1)}, u32[]{:S(2)}, u32[]{:S(2)}) collective-permute-start(bf16[32,2048]{1,0:T(8,128)(2,1)S(1)} %get-tuple-element.13), channel_id=1, source_target_pairs={{0,8},{2,10},{4,12},{6,14},{8,0},{10,2},{12,4},{14,6},{1,9},{3,11}... | collective-permute-start | bytes 393224 | tf_op jit(solution)/shard_map/ppermute | solution.py:247
  132.3 11.0 %collective-permute-start.18 = (bf16[32,2048]{1,0:T(8,128)(2,1)S(1)}, bf16[32,2048]{1,0:T(8,128)(2,1)S(1)}, u32[]{:S(2)}, u32[]{:S(2)}) collective-permute-start(bf16[32,2048]{1,0:T(8,128)(2,1)S(1)} %get-tuple-element.11), channel_id=1, source_target_pairs={{0,4},{2,6},{4,0},{6,2},{8,12},{10,14},{12,8},{14,10},{1,5},{3,7},... | collective-permute-start | bytes 393224 | tf_op jit(solution)/shard_map/ppermute | solution.py:247

commit v3 on v2

--- a/solution.py
+++ b/solution.py
@@ -81,8 +81,8 @@
 
 
 def attend_kernel(
-    req_count, group, page_len, q_ref, code_ref, extra_ref, fresh_hbm, kv_hbm, out_ref,
-    kbuf, vbuf, fkbuf, fvbuf, s_ref, acc_ref, l_ref, m_ref, ksem, vsem, fsem,
+    req_count, group, page_len, index_ref, code_ref, q_hbm, fresh_hbm, kv_hbm, gate_up_hbm, down_hbm,
+    out_ref, gate_up_ref, down_ref, q_ref, kbuf, vbuf, fkbuf, fvbuf, s_ref, acc_ref, l_ref, m_ref, ksem, vsem, fsem, wsem,
 ):
     f32, bf16 = jnp.float32, jnp.bfloat16
     width = q_ref.shape[2]
@@ -100,10 +100,19 @@
         pltpu.make_async_copy(fresh_hbm.at[:, :, pl.ds(h * width, width)], buf, fsem.at[h])
         for h, buf in enumerate((fkbuf, fvbuf))
     ]
+    fresh_copies.append(pltpu.make_async_copy(q_hbm, q_ref, fsem.at[2]))
     for copy in fresh_copies:
         copy.start()
     lax.fori_loop(0, blocks, lambda b, c: (fetch(0, kbuf, ksem, b).start(), c)[1], 0)
     lax.fori_loop(0, blocks, lambda b, c: (fetch(1, vbuf, vsem, b).start(), c)[1], 0)
+    weight_copies = [
+        pltpu.make_async_copy(gate_up_hbm, gate_up_ref, wsem.at[0]),
+        pltpu.make_async_copy(down_hbm, down_ref, wsem.at[1]),
+    ]
+    for copy in weight_copies:
+        copy.start()
+    for copy in fresh_copies:
+        copy.wait()
 
     q = q_ref[...].astype(f32)
     q2 = jnp.concatenate(
@@ -124,8 +133,6 @@
             q2, widen(keys), (((1,), (1,)), ((), ())), preferred_element_type=f32
         )
 
-    for copy in fresh_copies:
-        copy.wait()
     fresh = fkbuf.shape[0] * 2
     fresh_keys = fkbuf.reshape(fresh, width)[...]
     col = lax.broadcasted_iota(jnp.int32, (1, fresh), 1) // 2
@@ -192,10 +199,11 @@
         for g in range(group):
             at = (h * group + g) * width
             out_ref[:, at : at + width] = m_ref[pl.ds(g, rows // group, stride=group), :].astype(bf16)
-    out_ref[:, 2 * group * width :] = extra_ref[...]
-
-
-def attend_pool(queries, fresh_kv, kv_pool, page_table, context_lengths, extra):
+    for copy in weight_copies:
+        copy.wait()
+
+
+def attend_pool(index, queries, fresh_kv, kv_pool, page_table, context_lengths, gate_up, down_proj):
     step_count, req_count, head_count, head_width = queries.shape
     pool_pages, page_len, kv_heads, _ = kv_pool.shape
     group = head_count // kv_heads
@@ -211,14 +219,19 @@
     tokens = pool_pages * page_len
     rows, columns = step_count * req_count * group, tokens * 2 // blocks
     bf16, f32 = jnp.bfloat16, jnp.float32
-    vmem, anyspace = pl.BlockSpec(memory_space=pltpu.VMEM), pl.BlockSpec(memory_space=pl.ANY)
+    vmem, hbm = pl.BlockSpec(memory_space=pltpu.VMEM), pl.BlockSpec(memory_space=pltpu.HBM)
     own = step_count * req_count
     return pl.pallas_call(
         functools.partial(attend_kernel, req_count, group, page_len),
-        out_shape=jax.ShapeDtypeStruct((own, head_count * head_width + extra.shape[1]), bf16),
-        in_specs=[vmem, vmem, vmem, anyspace, anyspace],
-        out_specs=vmem,
+        out_shape=(
+            jax.ShapeDtypeStruct((own, head_count * head_width), bf16),
+            pltpu.VMEM(gate_up.shape, bf16),
+            pltpu.VMEM(down_proj.shape, bf16),
+        ),
+        in_specs=[pl.BlockSpec(memory_space=pltpu.SMEM), vmem, hbm, hbm, hbm, hbm, hbm],
+        out_specs=(vmem, vmem, vmem),
         scratch_shapes=[
+            pltpu.VMEM((own, head_count, head_width), bf16),
             pltpu.VMEM((tokens, 2, head_width), bf16),
             pltpu.VMEM((tokens, 2, head_width), bf16),
             pltpu.VMEM((own, 2, head_width), bf16),
@@ -229,16 +242,24 @@
             pltpu.VMEM((rows, head_width), f32),
             pltpu.SemaphoreType.DMA((blocks,)),
             pltpu.SemaphoreType.DMA((blocks,)),
+            pltpu.SemaphoreType.DMA((3,)),
             pltpu.SemaphoreType.DMA((2,)),
         ],
-        compiler_params=pltpu.CompilerParams(vmem_limit_bytes=40 * 1024 * 1024),
+        compiler_params=pltpu.CompilerParams(vmem_limit_bytes=24 * 1024 * 1024),
         name="attend_pool",
     )(
-        queries.reshape(own, head_count, head_width),
+        index,
         code,
-        extra,
-        fresh_kv.reshape(own, kv_heads, 2 * head_width),
-        kv_pool.reshape(tokens, kv_heads, 2 * head_width),
+        *[
+            pltpu.with_memory_space_constraint(value, pltpu.HBM)
+            for value in (
+                queries.reshape(own, head_count, head_width),
+                fresh_kv.reshape(own, kv_heads, 2 * head_width),
+                kv_pool.reshape(tokens, kv_heads, 2 * head_width),
+                gate_up,
+                down_proj,
+            )
+        ],
     )
 
 
@@ -247,9 +268,9 @@
     return lax.ppermute(value, axis, [(i, i ^ mask) for i in range(count)])
 
 
-def reorder(blocks, index):
+def reorder(blocks, index, low=0):
     blocks = list(blocks)
-    for bit in range(len(blocks).bit_length() - 1):
+    for bit in range(low, len(blocks).bit_length() - 1):
         flip = (index >> bit) & 1 == 1
         blocks = [jnp.where(flip, blocks[j ^ (1 << bit)], blocks[j]) for j in range(len(blocks))]
     return blocks
@@ -260,13 +281,203 @@
     return high.astype(jnp.bfloat16), (value - high).astype(jnp.bfloat16)
 
 
-def gather_rows(rows):
-    chips = lax.axis_size("dp") // 2
-    mine = jnp.stack([rows] + [exchange(rows, "dp", 2 * k) for k in range(1, chips)])
-    return jnp.stack([mine, exchange(mine, "dp", 1)])
-
-
-def body(
+def where_am_i(index_ref):
+    return index_ref[0], index_ref[1]
+
+
+def project_kernel(pieces, index_ref, *refs):
+    weight_ref, keep_ref, send_ref = refs[2 * pieces :]
+    dp_index, x_index = where_am_i(index_ref)
+    rows = jnp.concatenate([ref[...] for ref in refs[: 2 * pieces]], axis=0)
+    near = pieces // 2
+    value = jnp.dot(rows, weight_ref[...], preferred_element_type=jnp.float32)
+    own = rows.shape[0] // (2 * pieces)
+    stay = (dp_index // 2) // near == x_index
+    for at, ref in ((0, keep_ref), (pieces, send_ref)):
+        blocks = [value[(at + k) * own : (at + k + 1) * own] for k in range(pieces)]
+        for k in range(pieces):
+            ref[k] = jnp.where(stay, blocks[k], blocks[k ^ near]).astype(jnp.bfloat16)
+
+
+def pair_kernel(keep_ref, got_ref, *outs):
+    block = keep_ref.shape[2]
+    for k, out in enumerate(outs):
+        out[:, :block] = keep_ref[k]
+        out[:, block:] = got_ref[k]
+
+
+def stream_kernel(pieces, experts, index_ref, *refs):
+    f32, bf16 = jnp.float32, jnp.bfloat16
+    gots = refs[:pieces]
+    residual_ref, gain_ref, ids_ref, weight_ref, stream_ref, rows_ref = refs[pieces:]
+    dp_index, _ = where_am_i(index_ref)
+    near = pieces // 2
+    width = stream_ref.shape[1]
+    extra = rows_ref.shape[1] - width
+    sums = [gots[k][...].astype(f32) + gots[k + near][...].astype(f32) for k in range(near)]
+    sums = reorder(sums, (dp_index // 2) % near)
+    block = sums[0].shape[1] // 2
+    at = 0
+    square = 0.0
+    for both in sums:
+        for part in reorder([both[:, :block], both[:, block:]], dp_index % 2):
+            cut = slice(at, at + block)
+            value = part + residual_ref[:, cut].astype(f32)
+            stream_ref[:, cut] = value
+            rows_ref[:, cut] = (value * gain_ref[:, cut]).astype(bf16)
+            square = square + jnp.sum(value * value, axis=1, keepdims=True)
+            at += block
+    column = lax.broadcasted_iota(jnp.int32, (experts, extra), 1) - 2
+    expert = lax.broadcasted_iota(jnp.int32, (experts, extra), 0)
+    routes = []
+    for step in range(ids_ref.shape[0]):
+        ids, weights = ids_ref[step], weight_ref[step]
+        share = weights / jnp.sum(weights, axis=0, keepdims=True)
+        label = lax.broadcasted_iota(jnp.int32, (experts, ids.shape[1]), 0)
+        table = jnp.zeros(label.shape, f32)
+        for k in range(ids.shape[0]):
+            table = table + jnp.where(label == ids[k : k + 1], share[k : k + 1], 0.0)
+        high = table.astype(bf16)
+        low = (table - high.astype(f32)).astype(bf16)
+        spread = 0.0
+        for value, shift in ((high, 0), (low, experts)):
+            chosen = jnp.where(column == expert + shift, 1.0, 0.0).astype(bf16)
+            spread = spread + lax.dot_general(
+                value, chosen, (((0,), (0,)), ((), ())), preferred_element_type=f32
+            )
+        routes.append(spread)
+    routes = jnp.concatenate(routes, axis=0)
+    high = square.astype(bf16).astype(f32)
+    lane = lax.broadcasted_iota(jnp.int32, routes.shape, 1)
+    routes = jnp.where(lane == 0, high, jnp.where(lane == 1, square - high, routes))
+    rows_ref[:, width:] = routes.astype(bf16)
+
+
+def gate_up_kernel(pieces, index_ref, *refs):
+    weight_ref, keep_ref, send_ref, own_ref = refs[pieces:]
+    local_experts, _, width, hidden = weight_ref.shape
+    part = hidden // 2
+    first = index_ref[1] == 0
+    rows = jnp.concatenate([ref[:, :width] for ref in refs[:pieces]], axis=0)
+    for e in range(local_experts):
+        for side in range(2):
+            at = 2 * e + side
+            value = jnp.dot(rows, weight_ref[e, side], preferred_element_type=jnp.float32)
+            keep_ref[at] = jnp.where(first, value[:, :part], value[:, part:])
+            send = jnp.where(first, value[:, part:], value[:, :part])
+            send_ref[:, at * part : (at + 1) * part] = send.astype(jnp.bfloat16)
+    extra = jnp.concatenate([ref[:, width:] for ref in refs[:pieces]], axis=0)
+    own_ref[...] = extra
+    send_ref[:, 2 * local_experts * part :] = extra
+
+
+def act_kernel(local_experts, experts, width, index_ref, keep_ref, got_ref, own_ref, out_ref):
+    f32 = jnp.float32
+    part = keep_ref.shape[2]
+    own = own_ref[...].astype(f32)
+    lane = lax.broadcasted_iota(jnp.int32, own.shape, 1)
+    other = got_ref[:, 2 * local_experts * part :].astype(f32)
+    square = jnp.sum(jnp.where(lane < 2, own + other, 0.0), axis=1, keepdims=True)
+    inverse = lax.rsqrt(square / width + EPS)
+    for e in range(local_experts):
+        column = 2 + index_ref[0] * local_experts + e
+        chosen = (lane == column) | (lane == column + experts)
+        share = jnp.sum(jnp.where(chosen, own, 0.0), axis=1, keepdims=True)
+        gate = keep_ref[2 * e] + got_ref[:, 2 * e * part : (2 * e + 1) * part].astype(f32)
+        up = keep_ref[2 * e + 1] + got_ref[:, (2 * e + 1) * part : (2 * e + 2) * part].astype(f32)
+        gate = gate * inverse
+        act = gate / (1.0 + jnp.exp(-gate)) * (up * inverse) * share
+        out_ref[:, e * part : (e + 1) * part] = act.astype(jnp.bfloat16)
+
+
+def down_kernel(index_ref, act_ref, got_ref, weight_ref, keep_ref, send_ref):
+    local_experts, hidden, width = weight_ref.shape
+    part = hidden // 2
+    half = keep_ref.shape[0]
+    first = index_ref[1] == 0
+    acts = []
+    for e in range(local_experts):
+        own = act_ref[:, e * part : (e + 1) * part]
+        got = got_ref[:, e * part : (e + 1) * part]
+        acts += [jnp.where(first, own, got), jnp.where(first, got, own)]
+    acts = jnp.concatenate(acts, axis=1)
+    step = 512
+    for at in range(0, width, step):
+        value = jnp.zeros((acts.shape[0], step), jnp.float32)
+        for e in range(local_experts):
+            value = value + jnp.dot(
+                acts[:, e * hidden : (e + 1) * hidden],
+                weight_ref[e, :, at : at + step],
+                preferred_element_type=jnp.float32,
+            )
+        keep_ref[:, at : at + step] = value[:half]
+        send_ref[:, at : at + step] = value[half:].astype(jnp.bfloat16)
+
+
+def fold_kernel(keep_ref, got_ref, *outs):
+    own = outs[0].shape[0]
+    for k, out in enumerate(outs):
+        cut = slice(k * own, (k + 1) * own)
+        value = keep_ref[cut] + got_ref[cut].astype(jnp.float32)
+        out[...] = value.astype(out.dtype)
+
+
+def small_call(kernel, name, outs, *args, index=None, flops=0, limit=8):
+    vmem, smem = pl.BlockSpec(memory_space=pltpu.VMEM), pl.BlockSpec(memory_space=pltpu.SMEM)
+    specs = [vmem] * len(args)
+    if index is not None:
+        specs, args = [smem] + specs, (index,) + args
+    return pl.pallas_call(
+        kernel,
+        out_shape=tuple(jax.ShapeDtypeStruct(shape, dtype) for shape, dtype in outs),
+        in_specs=specs,
+        out_specs=(vmem,) * len(outs),
+        compiler_params=pltpu.CompilerParams(vmem_limit_bytes=limit * 1024 * 1024),
+        cost_estimate=pl.CostEstimate(flops=flops, bytes_accessed=0, transcendentals=0)
+        if flops
+        else None,
+        name=name,
+    )(*args)
+
+
+def expert_chunk(rows, x_index, dp_index, gate_up, down_proj, expert_total):
+    bf16, f32 = jnp.bfloat16, jnp.float32
+    x_count = lax.axis_size("expert")
+    local_experts, _, width, hidden = gate_up.shape
+    part = hidden // x_count
+    own = rows[:, width:]
+    rows = rows[:, :width]
+    routes = own[:, 2 : 2 + 2 * expert_total].astype(f32)
+    routes = routes[:, :expert_total] + routes[:, expert_total:]
+    share = lax.dynamic_slice_in_dim(routes, dp_index * local_experts, local_experts, axis=1)
+    products = [
+        jnp.dot(rows, gate_up[e, s], preferred_element_type=f32)
+        for e in range(local_experts)
+        for s in range(2)
+    ]
+    parts = [
+        reorder([p[:, k * part : (k + 1) * part] for k in range(x_count)], x_index) for p in products
+    ]
+    sums = [p[0] for p in parts]
+    square = jnp.sum(own[:, :2].astype(f32), axis=1)
+    for k in range(1, x_count):
+        sent = jnp.concatenate([p[k].astype(bf16) for p in parts] + [own[:, :2]], axis=1)
+        got = exchange(sent, "expert", k).astype(f32)
+        sums = [s + got[:, i * part : (i + 1) * part] for i, s in enumerate(sums)]
+        square = square + jnp.sum(got[:, len(sums) * part :], axis=1)
+    inverse = lax.rsqrt(square / (width * x_count) + EPS)[:, None]
+    total = 0.0
+    for e in range(local_experts):
+        gate, up = sums[2 * e] * inverse, sums[2 * e + 1] * inverse
+        act = (jax.nn.silu(gate) * up * share[:, e : e + 1]).astype(bf16)
+        pieces = [act] + [exchange(act, "expert", k) for k in range(1, x_count)]
+        act = jnp.concatenate(reorder(pieces, x_index), axis=1)
+        total = total + jnp.dot(act, down_proj[e], preferred_element_type=f32)
+    half = total.shape[0] // 2
+    return total[:half], total[half:].astype(bf16)
+
+
+def body_plain(
     queries,
     fresh_kv,
     kv_pool,
@@ -284,100 +495,206 @@
     dp_count, x_count = lax.axis_size("dp"), lax.axis_size("expert")
     dp_index, x_index = lax.axis_index("dp"), lax.axis_index("expert")
     chips = dp_count // 2
+    chip_index, core_index = dp_index // 2, dp_index % 2
     local_experts, _, width, hidden = gate_up.shape
     expert_total = local_experts * dp_count
+    steps, reqs = queries.shape[:2]
+    own = steps * reqs
+
+    attended = attend(queries, fresh_kv, kv_pool, page_table, context_lengths)
+    attended = attended.reshape(own, attended.shape[2])
+    mine = jnp.stack([attended] + [exchange(attended, "dp", 2 * k) for k in range(1, chips)])
+    gathered = jnp.stack([mine, exchange(mine, "dp", 1)])
+    gathered = gathered.reshape(dp_count * own, attended.shape[1])
+
+    columns = jnp.dot(gathered, out_weight, preferred_element_type=f32).astype(bf16)
+    block = columns.shape[1]
+    columns = columns.reshape(2, chips, own, block)
+    swapped = exchange(columns[1], "dp", 1)
+    paired = [jnp.concatenate([columns[0, k], swapped[k]], axis=1) for k in range(chips)]
+    near = chips // x_count
+    low = near.bit_length() - 1
+    paired = reorder(paired, ((chip_index // near) ^ x_index) * near, low)
+    parts = [0.0] * near
+    for k in range(chips):
+        moves = []
+        for z in range(chips):
+            for c in range(2):
+                for x in range(x_count):
+                    away = (z // near) ^ x
+                    there = z ^ k ^ (away * near)
+                    moves.append(((2 * z + c) * x_count + x, (2 * there + c) * x_count + z // near))
+        got = lax.ppermute(paired[k], ("dp", "expert"), moves).astype(f32)
+        parts[k % near] = parts[k % near] + got
+    parts = [
+        reorder([p[:, c * block : (c + 1) * block] for c in range(2)], core_index)
+        for p in reorder(parts, chip_index % near)
+    ]
+    stream = jnp.concatenate([b for pair in parts for b in pair], axis=1)
+    stream = stream + residual.astype(f32).reshape(own, width)
 
     share = route_weights / jnp.sum(route_weights, axis=2, keepdims=True)
     catalog = jnp.arange(expert_total, dtype=jnp.int32)
     named = expert_ids[..., None] == catalog
     routed = jnp.sum(jnp.where(named, share[..., None], 0.0), axis=2)
-
-    steps, reqs = queries.shape[:2]
-    own = steps * reqs
-    total = dp_count * own
-    head_cols = queries.shape[2] * queries.shape[3]
-    extra = -(-2 * expert_total // 128) * 128
     routed_high, routed_low = split_pair(routed.reshape(own, expert_total))
-    routed = jnp.concatenate(
-        [routed_high, routed_low, jnp.zeros((own, extra - 2 * expert_total), bf16)], axis=1
-    )
-    if kv_pool.shape[2] == 2:
-        packed = attend_pool(queries, fresh_kv, kv_pool, page_table, context_lengths, routed)
-    else:
-        attended = attend(queries, fresh_kv, kv_pool, page_table, context_lengths)
-        packed = jnp.concatenate([attended.reshape(own, head_cols), routed], axis=1)
-    gathered = gather_rows(packed).reshape(total, head_cols + extra)
-    routes = gathered[:, head_cols : head_cols + 2 * expert_total].astype(f32)
-    routes = routes[:, :expert_total] + routes[:, expert_total:]
-
-    columns = jnp.dot(gathered[:, :head_cols], out_weight, preferred_element_type=f32).astype(bf16)
-    block = columns.shape[1]
-    columns = columns.reshape(2, chips, own, block)
-    paired = jnp.stack([columns[0], exchange(columns[1], "dp", 1)], axis=1)
-    arrived = [paired[0]] + [exchange(paired[k], "dp", 2 * k) for k in range(1, chips)]
-    blocks = [arrived[q // 2][q % 2] for q in range(dp_count)]
-    per_x = dp_count // x_count
-    groups = [jnp.concatenate(blocks[g * per_x : (g + 1) * per_x], axis=1) for g in range(x_count)]
-    groups = reorder(groups, (dp_index // per_x) ^ x_index)
-    summed = groups[0].astype(f32)
-    for k in range(1, x_count):
-        summed = summed + exchange(groups[k], "expert", k).astype(f32)
-    summed = [summed[:, q * block : (q + 1) * block] for q in range(per_x)]
-    summed = jnp.concatenate(reorder(summed, dp_index % per_x), axis=1)
-    stream = residual.astype(f32).reshape(own, width) + summed
-
     square_high, square_low = split_pair(jnp.sum(stream * stream, axis=1, keepdims=True))
+    extra = -(-(2 * expert_total + 2) // 128) * 128
     rows = jnp.concatenate(
         [
             (stream * norm_gain[None, :]).astype(bf16),
             square_high,
             square_low,
-            jnp.zeros((own, 126), bf16),
+            routed_high,
+            routed_low,
+            jnp.zeros((own, extra - 2 * expert_total - 2), bf16),
         ],
         axis=1,
     )
-    rows = gather_rows(rows).reshape(total, width + 128)
-    squares = rows[:, width : width + 2]
-    rows = rows[:, :width]
-
-    local = dp_index * local_experts + jnp.arange(local_experts, dtype=jnp.int32)
-    local_share = jnp.sum(
-        jnp.where(local[None, :, None] == catalog[None, None, :], routes[:, None, :], 0.0), axis=2
-    )
-    part = hidden // x_count
-    inverse = None
-    acts = []
-    for e in range(local_experts):
-        gate = jnp.dot(rows, gate_up[e, 0], preferred_element_type=f32)
-        up = jnp.dot(rows, gate_up[e, 1], preferred_element_type=f32)
-        gates = reorder([gate[:, k * part : (k + 1) * part] for k in range(x_count)], x_index)
-        ups = reorder([up[:, k * part : (k + 1) * part] for k in range(x_count)], x_index)
-        gate, up = gates[0], ups[0]
-        square = jnp.sum(squares.astype(f32), axis=1)
-        for k in range(1, x_count):
-            sent = [gates[k].astype(bf16), ups[k].astype(bf16)]
-            if e == 0:
-                sent.append(squares)
-            got = exchange(jnp.concatenate(sent, axis=1), "expert", k).astype(f32)
-            gate = gate + got[:, :part]
-            up = up + got[:, part : 2 * part]
-            if e == 0:
-                square = square + jnp.sum(got[:, 2 * part :], axis=1)
-        if e == 0:
-            inverse = lax.rsqrt(square / (width * x_count) + EPS)[:, None]
-        act = jax.nn.silu(gate * inverse) * (up * inverse) * local_share[:, e : e + 1]
-        act = act.astype(bf16)
-        pieces = [act] + [exchange(act, "expert", k) for k in range(1, x_count)]
-        acts.extend(reorder(pieces, x_index))
-    activated = jnp.concatenate(acts, axis=1)
-    down = down_proj.reshape(local_experts * hidden, width)
-    mixed = jnp.dot(activated, down, preferred_element_type=f32)
-    mixed = mixed.reshape(2, chips, own, width)
-    mixed = mixed[0] + exchange(mixed[1].astype(bf16), "dp", 1).astype(f32)
-    result = stream + mixed[0]
-    for k in range(1, chips):
-        result = result + exchange(mixed[k].astype(bf16), "dp", 2 * k).astype(f32)
+    from_chip = [rows] + [exchange(rows, "dp", 2 * k) for k in range(1, chips)]
+    result = stream
+    for chunk in (range(chips // 2, chips), range(chips // 2)):
+        mine = jnp.concatenate([from_chip[k] for k in chunk], axis=0)
+        taken = jnp.concatenate([mine, exchange(mine, "dp", 1)], axis=0)
+        keep, send = expert_chunk(taken, x_index, dp_index, gate_up, down_proj, expert_total)
+        keep = keep + exchange(send, "dp", 1).astype(f32)
+        for i, k in enumerate(chunk):
+            piece = keep[i * own : (i + 1) * own]
+            if k > 0:
+                piece = exchange(piece.astype(bf16), "dp", 2 * k).astype(f32)
+            result = result + piece
     return result.reshape(steps, reqs, width).astype(bf16)
+
+
+def body_fast(
+    queries,
+    fresh_kv,
+    kv_pool,
+    page_table,
+    context_lengths,
+    residual,
+    out_weight,
+    norm_gain,
+    expert_ids,
+    route_weights,
+    gate_up,
+    down_proj,
+):
+    bf16, f32 = jnp.bfloat16, jnp.float32
+    dp_count, x_count = lax.axis_size("dp"), lax.axis_size("expert")
+    dp_index, x_index = lax.axis_index("dp"), lax.axis_index("expert")
+    index = jnp.stack([dp_index, x_index]).astype(jnp.int32)
+    chips = dp_count // 2
+    local_experts, _, width, hidden = gate_up.shape
+    part = hidden // 2
+    expert_total = local_experts * dp_count
+    steps, reqs = queries.shape[:2]
+    own = steps * reqs
+
+    attended, gate_up, down_proj = attend_pool(
+        index, queries, fresh_kv, kv_pool, page_table, context_lengths, gate_up, down_proj
+    )
+    head_cols = attended.shape[1]
+    mine = [attended] + [exchange(attended, "dp", 2 * k) for k in range(1, chips)]
+    mine = mine + [exchange(piece, "dp", 1) for piece in mine]
+    block = out_weight.shape[1]
+    keep, send = small_call(
+        functools.partial(project_kernel, chips),
+        "project",
+        [((chips, own, block), bf16)] * 2,
+        *mine,
+        out_weight,
+        index=index,
+        flops=2 * dp_count * own * head_cols * block,
+    )
+    paired = small_call(
+        pair_kernel, "pair", [((own, 2 * block), bf16)] * chips, keep, exchange(send, "dp", 1)
+    )
+    near = chips // x_count
+    arrived = []
+    for k in range(chips):
+        moves = []
+        for z in range(chips):
+            for c in range(2):
+                for x in range(x_count):
+                    away = (z // near) ^ x
+                    there = z ^ k ^ (away * near)
+                    moves.append(((2 * z + c) * x_count + x, (2 * there + c) * x_count + z // near))
+        arrived.append(lax.ppermute(paired[k], ("dp", "expert"), moves))
+
+    extra = -(-(2 * expert_total + 2) // 128) * 128
+    stream, rows = small_call(
+        functools.partial(stream_kernel, chips, expert_total),
+        "stream",
+        [((own, width), f32), ((own, width + extra), bf16)],
+        *arrived,
+        residual.reshape(own, width),
+        norm_gain.reshape(1, width),
+        jnp.swapaxes(expert_ids, 1, 2),
+        jnp.swapaxes(route_weights, 1, 2),
+        index=index,
+    )
+    from_chip = [rows] + [exchange(rows, "dp", 2 * k) for k in range(1, chips)]
+    result = stream
+    for chunk in (range(chips // 2, chips), range(chips // 2)):
+        pieces = [from_chip[k] for k in chunk]
+        pieces = pieces + [exchange(piece, "dp", 1) for piece in pieces]
+        count = len(pieces) * own
+        keep, send, extras = small_call(
+            functools.partial(gate_up_kernel, len(pieces)),
+            "gate_up",
+            [
+                ((2 * local_experts, count, part), f32),
+                ((count, 2 * local_experts * part + extra), bf16),
+                ((count, extra), bf16),
+            ],
+            *pieces,
+            gate_up,
+            index=index,
+            flops=4 * count * width * hidden * local_experts,
+        )
+        (act,) = small_call(
+            functools.partial(act_kernel, local_experts, expert_total, x_count * width),
+            "act",
+            [((count, local_experts * part), bf16)],
+            keep,
+            exchange(send, "expert", 1),
+            extras,
+            index=index,
+        )
+        keep, send = small_call(
+            down_kernel,
+            "down",
+            [((count // 2, width), f32), ((count // 2, width), bf16)],
+            act,
+            exchange(act, "expert", 1),
+            down_proj,
+            index=index,
+            flops=2 * count * width * hidden * local_experts,
+        )
+        folded = small_call(
+            fold_kernel,
+            "fold",
+            [((own, width), bf16 if k else f32) for k in chunk],
+            keep,
+            exchange(send, "dp", 1),
+        )
+        for k, piece in zip(chunk, folded):
+            if k > 0:
+                piece = exchange(piece, "dp", 2 * k).astype(f32)
+            result = result + piece
+    return result.reshape(steps, reqs, width).astype(bf16)
+
+
+def body(*args):
+    fast = (
+        args[2].shape[2] == 2
+        and lax.axis_size("expert") == 2
+        and lax.axis_size("dp") >= 4
+        and args[10].shape[3] % 256 == 0
+        and args[10].shape[2] % 512 == 0
+    )
+    return (body_fast if fast else body_plain)(*args)
 
 
 def solution(mesh):

time: 145 us -> 115 us (0.79)
  waiting for transfers between devices: 71.2 us -> 52 us
  matrix products: 14.3 us -> 0 us
  Pallas kernels: 14.4 us -> 24.1 us
  starting transfers between devices: 24.3 us -> 33.3 us
  other arithmetic: 11.5 us -> 3.84 us
  local copies, waits for them, and re-layouts: 7.92 us -> 1.27 us
    ppermute x21 -> x24, waiting for transfers between devices: 71.2 us -> 48.6 us  [exchange(): return lax.ppermute(value, axis, [(i, i ^ mask) for i in range(count)])]
    dot_general x6 -> x0, matrix products: 14.3 us -> none  [the longest x2 5.94 us: body(): gate = jnp.dot(rows, gate_up[e, 0], preferred_element_type=f32)]
    pallas_call x0 -> x11, Pallas kernels: none -> 11.6 us  [small_call(): pl.pallas_call(kernel, out_shape=tuple((jax.ShapeDtypeStruct(shape, dtype...]
    unnamed x22 -> x11, local copies, waits for them, and re-layouts: 6.69 us -> 0.87 us
    ppermute x0 -> x4, starting transfers between devices: none -> 5.65 us  [body_fast(): arrived.append(lax.ppermute(paired[k], ('dp', 'expert'), moves))]
    ppermute x0 -> x4, waiting for transfers between devices: none -> 3.45 us  [body_fast(): arrived.append(lax.ppermute(paired[k], ('dp', 'expert'), moves))]
    ppermute x21 -> x24, starting transfers between devices: 24.3 us -> 27.7 us  [exchange(): return lax.ppermute(value, axis, [(i, i ^ mask) for i in range(count)])]
    another operation x5 -> x1, other arithmetic: 3.34 us -> 0.08 us  [body_fast(): index = jnp.stack([dp_index, x_index]).astype(jnp.int32)]
  transfers between devices with their start and end apart: 21 -> 28, of which waited for: 17 -> 16; matrix products, arithmetic and copies ran while one was open for 1% -> 0% of each run, Pallas kernels for 0% -> 8%
where the time goes in v3:
time: 115 us
  waiting for transfers between devices  52 us (45%)
  starting transfers between devices  33.3 us (29%)
  Pallas kernels  24.1 us (21%)
  other arithmetic  3.84 us (3%)
  local copies, waits for them, and re-layouts  1.27 us (1%)
    ppermute x24, waiting for transfers between devices, exchange(): return lax.ppermute(value, axis, [(i, i ^ mask) for i in range(count)])  48.6 us
    ppermute x24, starting transfers between devices, exchange(): return lax.ppermute(value, axis, [(i, i ^ mask) for i in range(count)])  27.7 us
    pallas_call x1, Pallas kernels, attend_pool(): pl.pallas_call(functools.partial(attend_kernel, req_count, group, page_le...  12.4 us
    pallas_call x11, Pallas kernels, small_call(): pl.pallas_call(kernel, out_shape=tuple((jax.ShapeDtypeStruct(shape, dtype...  11.6 us
    ppermute x4, starting transfers between devices, body_fast(): arrived.append(lax.ppermute(paired[k], ('dp', 'expert'), moves))  5.65 us
    ppermute x4, waiting for transfers between devices, body_fast(): arrived.append(lax.ppermute(paired[k], ('dp', 'expert'), moves))  3.45 us
    reduce_sum x1, other arithmetic, attend_pool(): jnp.sum(jnp.where(page_table[:, :, None] == pages, entry[:, :, None], 0),...  2.3 us
  transfers between devices with their start and end apart: 28, of which 16 were waited for; matrix products, arithmetic and copies ran while one was open for 0% of the time, Pallas kernels for 8%

profile of v3, /device:TPU:0, one launch (start us, length us, event | category | flops | bytes accessed | tf_op | source)
XLA Modules:
  0.0 114.8 jit_solution(5120831952301471297)
XLA Ops:
  0.0 0.7 clamp_add_fusion
  0.7 0.1 copy.15
  0.8 0.8 copy.14
  1.7 2.3 %select_reduce_fusion = s32[320]{0:T(512)S(1)} fusion(s32[16,305]{0,1:T(8,128)S(1)} %copy.15, s32[16,305]{0,1:T(8,128)S(1)} %copy.14), kind=kLoop, calls=%fused_computation | loop fusion | flops 4684480 | bytes 40320 | tf_op jit(solution)/shard_map/reduce_sum | solution.py:214
  4.2 0.1 broadcast_in_dim.29.code_ref
  4.4 12.4 %attend_pool.1 = (bf16[32,2048]{1,0:T(8,128)(2,1)S(1)}, bf16[2,2,2048,768]{3,2,1,0:T(8,128)(2,1)S(1)}, bf16[2,768,2048]{2,1,0:T(8,128)(2,1)S(1)}) custom-call(s32[2]{0:T(128)S(1)} %pad_add_fusion.index_ref, s32[10,1024]{1,0:T(8,128)S(1)} %broadcast_in_dim.29.code_ref, bf16[32,16,128]{2,1,0:T(8,128)(2,1)} %bitcast.15, bf16[32,2,256]{2,1,0:T(2,128)(2,1)} %bitcast.16, ...), custom_call_target="tpu_custom_call" | custom-call | tf_op jit(solution)/shard_map/attend_pool/pallas_call | solution.py:224
  16.9 3.1 %collective-permute-start = (bf16[32,2048]{1,0:T(8,128)(2,1)S(1)}, bf16[32,2048]{1,0:T(8,128)(2,1)S(1)}, u32[]{:S(2)}, u32[]{:S(2)}) collective-permute-start(bf16[32,2048]{1,0:T(8,128)(2,1)S(1)} %get-tuple-element.30.refs_0_), channel_id=1, source_target_pairs={{0,4},{2,6},{4,0},{6,2},{8,12},{10,14},{12,8},{14,10},{1,5},{3,7},... | collective-permute-start | bytes 393224 | tf_op jit(solution)/shard_map/ppermute | solution.py:268
  20.0 2.6 %collective-permute-start.1 = (bf16[32,2048]{1,0:T(8,128)(2,1)S(1)}, bf16[32,2048]{1,0:T(8,128)(2,1)S(1)}, u32[]{:S(2)}, u32[]{:S(2)}) collective-permute-start(bf16[32,2048]{1,0:T(8,128)(2,1)S(1)} %get-tuple-element.30.refs_0_), channel_id=1, source_target_pairs={{0,8},{2,10},{4,12},{6,14},{8,0},{10,2},{12,4},{14,6},{1,9},{3,11}... | collective-permute-start | bytes 393224 | tf_op jit(solution)/shard_map/ppermute | solution.py:268
  22.6 2.5 %collective-permute-done.refs_1_ = bf16[32,2048]{1,0:T(8,128)(2,1)S(1)} collective-permute-done((bf16[32,2048]{1,0:T(8,128)(2,1)S(1)}, bf16[32,2048]{1,0:T(8,128)(2,1)S(1)}, u32[]{:S(2)}, u32[]{:S(2)}) %collective-permute-start) | collective-permute-done | bytes 131104 | tf_op jit(solution)/shard_map/ppermute | solution.py:268
  25.1 7.8 %collective-permute-done.1.refs_2_ = bf16[32,2048]{1,0:T(8,128)(2,1)S(1)} collective-permute-done((bf16[32,2048]{1,0:T(8,128)(2,1)S(1)}, bf16[32,2048]{1,0:T(8,128)(2,1)S(1)}, u32[]{:S(2)}, u32[]{:S(2)}) %collective-permute-start.1) | collective-permute-done | bytes 131104 | tf_op jit(solution)/shard_map/ppermute | solution.py:268
  32.9 0.5 collective-permute-start.6
  33.4 0.8 collective-permute-done.5.refs_6_
  34.2 0.2 collective-permute-done.6.refs_7_
  34.4 1.2 %project.1 = (bf16[4,32,512]{2,1,0:T(8,128)(2,1)S(1)}, bf16[4,32,512]{2,1,0:T(8,128)(2,1)S(1)}) custom-call(s32[2]{0:T(128)S(1)} %pad_add_fusion.index_ref, bf16[32,2048]{1,0:T(8,128)(2,1)S(1)} %get-tuple-element.30.refs_0_, bf16[32,2048]{1,0:T(8,128)(2,1)S(1)} %collective-permute-done.refs_1_, bf16[32,2048]{1,0:T(8,128)(2,1)S(1)} %collective-permute-done.1.refs_2_, ...), custom_call_target="tpu_custom_call" | custom-call | flops 536870912 | tf_op jit(solution)/shard_map/project/pallas_call | solution.py:430
  35.7 0.4 collective-permute-start.7
  36.1 1.0 collective-permute-done.7.got_ref
  37.1 2.9 %collective-permute-start.10 = (bf16[32,1024]{1,0:T(8,128)(2,1)S(1)}, bf16[32,1024]{1,0:T(8,128)(2,1)S(1)}, u32[]{:S(2)}, u32[]{:S(2)}) collective-permute-start(bf16[32,1024]{1,0:T(8,128)(2,1)S(1)} %get-tuple-element.35), channel_id=1, source_target_pairs={{0,8},{1,0},{2,10},{3,2},{4,12},{5,4},{6,14},{7,6},{8,9},{9,1},{10... | collective-permute-start | bytes 196616 | tf_op jit(solution)/shard_map/ppermute | solution.py:623
  40.0 0.9 collective-permute-start.11
  40.9 0.7 collective-permute-start.8
  41.6 1.2 %collective-permute-start.9 = (bf16[32,1024]{1,0:T(8,128)(2,1)S(1)}, bf16[32,1024]{1,0:T(8,128)(2,1)S(1)}, u32[]{:S(2)}, u32[]{:S(2)}) collective-permute-start(bf16[32,1024]{1,0:T(8,128)(2,1)S(1)} %get-tuple-element.34), channel_id=1, source_target_pairs={{0,4},{1,12},{2,6},{3,14},{4,0},{5,8},{6,2},{7,10},{8,5},{9,13},{1... | collective-permute-start | bytes 196616 | tf_op jit(solution)/shard_map/ppermute | solution.py:623
  42.8 3.4 %collective-permute-done.11.refs_3_ = bf16[32,1024]{1,0:T(8,128)(2,1)S(1)} collective-permute-done((bf16[32,1024]{1,0:T(8,128)(2,1)S(1)}, bf16[32,1024]{1,0:T(8,128)(2,1)S(1)}, u32[]{:S(2)}, u32[]{:S(2)}) %collective-permute-start.11) | collective-permute-done | bytes 65568 | tf_op jit(solution)/shard_map/ppermute | solution.py:623
  46.2 0.7 stream.1
  47.0 7.4 %collective-permute-start.12 = (bf16[32,2176]{1,0:T(8,128)(2,1)S(1)}, bf16[32,2176]{1,0:T(8,128)(2,1)S(1)}, u32[]{:S(2)}, u32[]{:S(2)}) collective-permute-start(bf16[32,2176]{1,0:T(8,128)(2,1)S(1)} %get-tuple-element.38.refs_0_), channel_id=1, source_target_pairs={{0,8},{2,10},{4,12},{6,14},{8,0},{10,2},{12,4},{14,6},{1,9},{3,11}... | collective-permute-start | bytes 417800 | tf_op jit(solution)/shard_map/ppermute | solution.py:268
  54.4 0.8 collective-permute-start.13
  55.2 0.5 collective-permute-start.21
  55.7 7.8 %collective-permute-done.12.refs_0_ = bf16[32,2176]{1,0:T(8,128)(2,1)S(1)} collective-permute-done((bf16[32,2176]{1,0:T(8,128)(2,1)S(1)}, bf16[32,2176]{1,0:T(8,128)(2,1)S(1)}, u32[]{:S(2)}, u32[]{:S(2)}) %collective-permute-start.12) | collective-permute-done | bytes 139296 | tf_op jit(solution)/shard_map/ppermute | solution.py:268
  63.5 0.5 collective-permute-start.15
  64.1 0.4 collective-permute-start.23
  64.5 0.3 collective-permute-done.14.refs_2_
  64.9 0.2 collective-permute-done.15.refs_3_
  65.0 2.4 %gate_up.2 = (f32[4,128,384]{2,1,0:T(8,128)S(1)}, bf16[128,1664]{1,0:T(8,128)(2,1)S(1)}, bf16[128,128]{1,0:T(8,128)(2,1)S(1)}) custom-call(s32[2]{0:T(128)S(1)} %pad_add_fusion.index_ref, bf16[32,2176]{1,0:T(8,128)(2,1)S(1)} %collective-permute-done.12.refs_0_, bf16[32,2176]{1,0:T(8,128)(2,1)S(1)} %collective-permute-done.13.refs_1_, ...), custom_call_target="tpu_custom_call" | custom-call | flops 1610612736 | tf_op jit(solution)/shard_map/gate_up/pallas_call | solution.py:430
  67.4 2.4 %collective-permute-start.16 = (bf16[128,1664]{1,0:T(8,128)(2,1)S(1)}, bf16[128,1664]{1,0:T(8,128)(2,1)S(1)}, u32[]{:S(2)}, u32[]{:S(2)}) collective-permute-start(bf16[128,1664]{1,0:T(8,128)(2,1)S(1)} %get-tuple-element.41), channel_id=1, source_target_pairs={{0,1},{1,0},{2,3},{3,2},{4,5},{5,4},{6,7},{7,6},{8,9},{9,8},{10,11... | collective-permute-start | bytes 1277960 | tf_op jit(solution)/shard_map/ppermute | solution.py:268
  69.9 2.4 %gate_up.3 = (f32[4,128,384]{2,1,0:T(8,128)S(1)}, bf16[128,1664]{1,0:T(8,128)(2,1)S(1)}, bf16[128,128]{1,0:T(8,128)(2,1)S(1)}) custom-call(s32[2]{0:T(128)S(1)} %pad_add_fusion.index_ref, bf16[32,2176]{1,0:T(8,128)(2,1)S(1)} %get-tuple-element.38.refs_0_, bf16[32,2176]{1,0:T(8,128)(2,1)S(1)} %collective-permute-done.21.refs_1_, ...), custom_call_target="tpu_custom_call" | custom-call | flops 1610612736 | tf_op jit(solution)/shard_map/gate_up/pallas_call | solution.py:430
  72.4 8.1 %collective-permute-done.16.got_ref = bf16[128,1664]{1,0:T(8,128)(2,1)S(1)} collective-permute-done((bf16[128,1664]{1,0:T(8,128)(2,1)S(1)}, bf16[128,1664]{1,0:T(8,128)(2,1)S(1)}, u32[]{:S(2)}, u32[]{:S(2)}) %collective-permute-start.16) | collective-permute-done | bytes 426016 | tf_op jit(solution)/shard_map/ppermute | solution.py:268
  80.6 0.8 act.2.act_ref
  81.4 2.1 %collective-permute-start.17 = (bf16[128,768]{1,0:T(8,128)(2,1)S(1)}, bf16[128,768]{1,0:T(8,128)(2,1)S(1)}, u32[]{:S(2)}, u32[]{:S(2)}) collective-permute-start(bf16[128,768]{1,0:T(8,128)(2,1)S(1)} %act.2.act_ref), channel_id=1, source_target_pairs={{0,1},{1,0},{2,3},{3,2},{4,5},{5,4},{6,7},{7,6},{8,9},{9,8},{10,11... | collective-permute-start | bytes 589832 | tf_op jit(solution)/shard_map/ppermute | solution.py:268
  83.4 6.2 %collective-permute-done.24.got_ref = bf16[128,1664]{1,0:T(8,128)(2,1)S(1)} collective-permute-done((bf16[128,1664]{1,0:T(8,128)(2,1)S(1)}, bf16[128,1664]{1,0:T(8,128)(2,1)S(1)}, u32[]{:S(2)}, u32[]{:S(2)}) %collective-permute-start.24) | collective-permute-done | bytes 426016 | tf_op jit(solution)/shard_map/ppermute | solution.py:268
  89.7 0.8 act.3.act_ref
  90.5 2.1 %collective-permute-start.25 = (bf16[128,768]{1,0:T(8,128)(2,1)S(1)}, bf16[128,768]{1,0:T(8,128)(2,1)S(1)}, u32[]{:S(2)}, u32[]{:S(2)}) collective-permute-start(bf16[128,768]{1,0:T(8,128)(2,1)S(1)} %act.3.act_ref), channel_id=1, source_target_pairs={{0,1},{1,0},{2,3},{3,2},{4,5},{5,4},{6,7},{7,6},{8,9},{9,8},{10,11... | collective-permute-start | bytes 589832 | tf_op jit(solution)/shard_map/ppermute | solution.py:268
  92.6 1.3 %collective-permute-done.17.got_ref = bf16[128,768]{1,0:T(8,128)(2,1)S(1)} collective-permute-done((bf16[128,768]{1,0:T(8,128)(2,1)S(1)}, bf16[128,768]{1,0:T(8,128)(2,1)S(1)}, u32[]{:S(2)}, u32[]{:S(2)}) %collective-permute-start.17) | collective-permute-done | bytes 196640 | tf_op jit(solution)/shard_map/ppermute | solution.py:268
  93.9 1.6 %down.2 = (f32[64,2048]{1,0:T(8,128)S(1)}, bf16[64,2048]{1,0:T(8,128)(2,1)S(1)}) custom-call(s32[2]{0:T(128)S(1)} %pad_add_fusion.index_ref, bf16[128,768]{1,0:T(8,128)(2,1)S(1)} %act.2.act_ref, bf16[128,768]{1,0:T(8,128)(2,1)S(1)} %collective-permute-done.17.got_ref, bf16[2,768,2048]{2,1,0:T(8,128)(2,1)S(1)} %get-tuple-element.43.weight_ref), custom_call_target="tpu_custom_call" | custom-call | flops 805306368 | tf_op jit(solution)/shard_map/down/pallas_call | solution.py:430
  95.5 2.2 %collective-permute-done.25.got_ref = bf16[128,768]{1,0:T(8,128)(2,1)S(1)} collective-permute-done((bf16[128,768]{1,0:T(8,128)(2,1)S(1)}, bf16[128,768]{1,0:T(8,128)(2,1)S(1)}, u32[]{:S(2)}, u32[]{:S(2)}) %collective-permute-start.25) | collective-permute-done | bytes 196640 | tf_op jit(solution)/shard_map/ppermute | solution.py:268
  97.7 1.6 %down.3 = (f32[64,2048]{1,0:T(8,128)S(1)}, bf16[64,2048]{1,0:T(8,128)(2,1)S(1)}) custom-call(s32[2]{0:T(128)S(1)} %pad_add_fusion.index_ref, bf16[128,768]{1,0:T(8,128)(2,1)S(1)} %act.3.act_ref, bf16[128,768]{1,0:T(8,128)(2,1)S(1)} %collective-permute-done.25.got_ref, bf16[2,768,2048]{2,1,0:T(8,128)(2,1)S(1)} %get-tuple-element.43.weight_ref), custom_call_target="tpu_custom_call" | custom-call | flops 805306368 | tf_op jit(solution)/shard_map/down/pallas_call | solution.py:430
  99.4 3.3 %collective-permute-start.19 = (bf16[32,2048]{1,0:T(8,128)(2,1)S(1)}, bf16[32,2048]{1,0:T(8,128)(2,1)S(1)}, u32[]{:S(2)}, u32[]{:S(2)}) collective-permute-start(bf16[32,2048]{1,0:T(8,128)(2,1)S(1)} %get-tuple-element.46), channel_id=1, source_target_pairs={{0,8},{2,10},{4,12},{6,14},{8,0},{10,2},{12,4},{14,6},{1,9},{3,11}... | collective-permute-start | bytes 393224 | tf_op jit(solution)/shard_map/ppermute | solution.py:268
  102.8 1.2 %collective-permute-start.20 = (bf16[32,2048]{1,0:T(8,128)(2,1)S(1)}, bf16[32,2048]{1,0:T(8,128)(2,1)S(1)}, u32[]{:S(2)}, u32[]{:S(2)}) collective-permute-start(bf16[32,2048]{1,0:T(8,128)(2,1)S(1)} %get-tuple-element.47), channel_id=1, source_target_pairs={{0,12},{2,14},{4,8},{6,10},{8,4},{10,6},{12,0},{14,2},{1,13},{3,15... | collective-permute-start | bytes 393224 | tf_op jit(solution)/shard_map/ppermute | solution.py:268
  104.1 8.7 %collective-permute-done.19 = bf16[32,2048]{1,0:T(8,128)(2,1)S(1)} collective-permute-done((bf16[32,2048]{1,0:T(8,128)(2,1)S(1)}, bf16[32,2048]{1,0:T(8,128)(2,1)S(1)}, u32[]{:S(2)}, u32[]{:S(2)}) %collective-permute-start.19) | collective-permute-done | bytes 131104 | tf_op jit(solution)/shard_map/ppermute | solution.py:268
  112.8 1.2 %collective-permute-done.27 = bf16[32,2048]{1,0:T(8,128)(2,1)S(1)} collective-permute-done((bf16[32,2048]{1,0:T(8,128)(2,1)S(1)}, bf16[32,2048]{1,0:T(8,128)(2,1)S(1)}, u32[]{:S(2)}, u32[]{:S(2)}) %collective-permute-start.27) | collective-permute-done | bytes 131104 | tf_op jit(solution)/shard_map/ppermute | solution.py:268
  114.1 0.7 add_convert_fusion
  (41 shorter events, 0.9 us)
Async XLA Ops:
  4.4 30.0 %copy-start = (bf16[2048,512]{1,0:T(8,128)(2,1)S(1)}, bf16[2048,512]{1,0:T(8,128)(2,1)}, u32[]{:S(2)}) copy-start(bf16[2048,512]{1,0:T(8,128)(2,1)} %refs_8_.1) | copy-start | bytes 6291460
  4.4 41.8 %copy-start.1 = (bf16[2,16,2048]{2,1,0:T(8,128)(2,1)S(1)}, bf16[2,16,2048]{2,1,0:T(8,128)(2,1)}, u32[]{:S(2)}) copy-start(bf16[2,16,2048]{2,1,0:T(8,128)(2,1)} %param.17) | copy-start | bytes 393220
  4.4 41.8 %copy-start.2 = (f32[2048]{0:T(1024)S(1)}, f32[2048]{0:T(1024)}, u32[]{:S(2)}) copy-start(f32[2048]{0:T(1024)} %param.19) | copy-start | bytes 24580
  4.4 41.8 %copy-start.3 = (s32[2,16,8]{1,2,0:T(8,128)S(1)}, s32[2,16,8]{1,2,0:T(8,128)}, u32[]{:S(2)}) copy-start(s32[2,16,8]{1,2,0:T(8,128)} %param.20) | copy-start | bytes 3076
  4.4 41.8 %copy-start.4 = (f32[2,16,8]{1,2,0:T(8,128)S(1)}, f32[2,16,8]{1,2,0:T(8,128)}, u32[]{:S(2)}) copy-start(f32[2,16,8]{1,2,0:T(8,128)} %param.21) | copy-start | bytes 3076
  16.9 8.2 %collective-permute-start = (bf16[32,2048]{1,0:T(8,128)(2,1)S(1)}, bf16[32,2048]{1,0:T(8,128)(2,1)S(1)}, u32[]{:S(2)}, u32[]{:S(2)}) collective-permute-start(bf16[32,2048]{1,0:T(8,128)(2,1)S(1)} %get-tuple-element.30.refs_0_), channel_id=1, source_target_pairs={{0,4},{2,6},{4,0},{6,2},{8,12},{10,14},{12,8},{14,10},{1,5},{3,7},... | collective-permute-start | bytes 393224 | tf_op jit(solution)/shard_map/ppermute | solution.py:268
  20.0 12.9 %collective-permute-start.1 = (bf16[32,2048]{1,0:T(8,128)(2,1)S(1)}, bf16[32,2048]{1,0:T(8,128)(2,1)S(1)}, u32[]{:S(2)}, u32[]{:S(2)}) collective-permute-start(bf16[32,2048]{1,0:T(8,128)(2,1)S(1)} %get-tuple-element.30.refs_0_), channel_id=1, source_target_pairs={{0,8},{2,10},{4,12},{6,14},{8,0},{10,2},{12,4},{14,6},{1,9},{3,11}... | collective-permute-start | bytes 393224 | tf_op jit(solution)/shard_map/ppermute | solution.py:268
  22.6 10.3 %collective-permute-start.2 = (bf16[32,2048]{1,0:T(8,128)(2,1)S(1)}, bf16[32,2048]{1,0:T(8,128)(2,1)S(1)}, u32[]{:S(2)}, u32[]{:S(2)}) collective-permute-start(bf16[32,2048]{1,0:T(8,128)(2,1)S(1)} %get-tuple-element.30.refs_0_), channel_id=1, source_target_pairs={{0,12},{2,14},{4,8},{6,10},{8,4},{10,6},{12,0},{14,2},{1,13},{3,15... | collective-permute-start | bytes 393224 | tf_op jit(solution)/shard_map/ppermute | solution.py:268
  22.6 10.8 %collective-permute-start.3 = (bf16[32,2048]{1,0:T(8,128)(2,1)S(1)}, bf16[32,2048]{1,0:T(8,128)(2,1)S(1)}, u32[]{:S(2)}, u32[]{:S(2)}) collective-permute-start(bf16[32,2048]{1,0:T(8,128)(2,1)S(1)} %get-tuple-element.30.refs_0_), channel_id=1, source_target_pairs={{0,2},{2,0},{4,6},{6,4},{8,10},{10,8},{12,14},{14,12},{1,3},{3,1},... | collective-permute-start | bytes 393224 | tf_op jit(solution)/shard_map/ppermute | solution.py:268
  25.1 8.3 %collective-permute-start.4 = (bf16[32,2048]{1,0:T(8,128)(2,1)S(1)}, bf16[32,2048]{1,0:T(8,128)(2,1)S(1)}, u32[]{:S(2)}, u32[]{:S(2)}) collective-permute-start(bf16[32,2048]{1,0:T(8,128)(2,1)S(1)} %collective-permute-done.refs_1_), channel_id=1, source_target_pairs={{0,2},{2,0},{4,6},{6,4},{8,10},{10,8},{12,14},{14,12},{1,3},{3,1},... | collective-permute-start | bytes 393224 | tf_op jit(solution)/shard_map/ppermute | solution.py:268
  32.9 1.3 %collective-permute-start.5 = (bf16[32,2048]{1,0:T(8,128)(2,1)S(1)}, bf16[32,2048]{1,0:T(8,128)(2,1)S(1)}, u32[]{:S(2)}, u32[]{:S(2)}) collective-permute-start(bf16[32,2048]{1,0:T(8,128)(2,1)S(1)} %collective-permute-done.1.refs_2_), channel_id=1, source_target_pairs={{0,2},{2,0},{4,6},{6,4},{8,10},{10,8},{12,14},{14,12},{1,3},{3,1},... | collective-permute-start | bytes 393224 | tf_op jit(solution)/shard_map/ppermute | solution.py:268
  32.9 1.5 %collective-permute-start.6 = (bf16[32,2048]{1,0:T(8,128)(2,1)S(1)}, bf16[32,2048]{1,0:T(8,128)(2,1)S(1)}, u32[]{:S(2)}, u32[]{:S(2)}) collective-permute-start(bf16[32,2048]{1,0:T(8,128)(2,1)S(1)} %collective-permute-done.2.refs_3_), channel_id=1, source_target_pairs={{0,2},{2,0},{4,6},{6,4},{8,10},{10,8},{12,14},{14,12},{1,3},{3,1},... | collective-permute-start | bytes 393224 | tf_op jit(solution)/shard_map/ppermute | solution.py:268
  35.7 1.4 %collective-permute-start.7 = (bf16[4,32,512]{2,1,0:T(8,128)(2,1)S(1)}, bf16[4,32,512]{2,1,0:T(8,128)(2,1)S(1)}, u32[]{:S(2)}, u32[]{:S(2)}) collective-permute-start(bf16[4,32,512]{2,1,0:T(8,128)(2,1)S(1)} %get-tuple-element.32), channel_id=1, source_target_pairs={{0,2},{2,0},{4,6},{6,4},{8,10},{10,8},{12,14},{14,12},{1,3},{3,1},... | collective-permute-start | bytes 393224 | tf_op jit(solution)/shard_map/ppermute | solution.py:268
  37.1 5.7 %collective-permute-start.10 = (bf16[32,1024]{1,0:T(8,128)(2,1)S(1)}, bf16[32,1024]{1,0:T(8,128)(2,1)S(1)}, u32[]{:S(2)}, u32[]{:S(2)}) collective-permute-start(bf16[32,1024]{1,0:T(8,128)(2,1)S(1)} %get-tuple-element.35), channel_id=1, source_target_pairs={{0,8},{1,0},{2,10},{3,2},{4,12},{5,4},{6,14},{7,6},{8,9},{9,1},{10... | collective-permute-start | bytes 196616 | tf_op jit(solution)/shard_map/ppermute | solution.py:623
  40.0 6.2 %collective-permute-start.11 = (bf16[32,1024]{1,0:T(8,128)(2,1)S(1)}, bf16[32,1024]{1,0:T(8,128)(2,1)S(1)}, u32[]{:S(2)}, u32[]{:S(2)}) collective-permute-start(bf16[32,1024]{1,0:T(8,128)(2,1)S(1)} %get-tuple-element.36), channel_id=1, source_target_pairs={{0,12},{1,4},{2,14},{3,6},{4,8},{5,0},{6,10},{7,2},{8,13},{9,5},{1... | collective-permute-start | bytes 196616 | tf_op jit(solution)/shard_map/ppermute | solution.py:623
  40.9 5.3 %collective-permute-start.8 = (bf16[32,1024]{1,0:T(8,128)(2,1)S(1)}, bf16[32,1024]{1,0:T(8,128)(2,1)S(1)}, u32[]{:S(2)}, u32[]{:S(2)}) collective-permute-start(bf16[32,1024]{1,0:T(8,128)(2,1)S(1)} %get-tuple-element.33), channel_id=1, source_target_pairs={{0,0},{1,8},{2,2},{3,10},{4,4},{5,12},{6,6},{7,14},{8,1},{9,9},{10... | collective-permute-start | bytes 196616 | tf_op jit(solution)/shard_map/ppermute | solution.py:623
  41.6 4.6 %collective-permute-start.9 = (bf16[32,1024]{1,0:T(8,128)(2,1)S(1)}, bf16[32,1024]{1,0:T(8,128)(2,1)S(1)}, u32[]{:S(2)}, u32[]{:S(2)}) collective-permute-start(bf16[32,1024]{1,0:T(8,128)(2,1)S(1)} %get-tuple-element.34), channel_id=1, source_target_pairs={{0,4},{1,12},{2,6},{3,14},{4,0},{5,8},{6,2},{7,10},{8,5},{9,13},{1... | collective-permute-start | bytes 196616 | tf_op jit(solution)/shard_map/ppermute | solution.py:623
  47.0 16.5 %collective-permute-start.12 = (bf16[32,2176]{1,0:T(8,128)(2,1)S(1)}, bf16[32,2176]{1,0:T(8,128)(2,1)S(1)}, u32[]{:S(2)}, u32[]{:S(2)}) collective-permute-start(bf16[32,2176]{1,0:T(8,128)(2,1)S(1)} %get-tuple-element.38.refs_0_), channel_id=1, source_target_pairs={{0,8},{2,10},{4,12},{6,14},{8,0},{10,2},{12,4},{14,6},{1,9},{3,11}... | collective-permute-start | bytes 417800 | tf_op jit(solution)/shard_map/ppermute | solution.py:268
  54.4 9.1 %collective-permute-start.13 = (bf16[32,2176]{1,0:T(8,128)(2,1)S(1)}, bf16[32,2176]{1,0:T(8,128)(2,1)S(1)}, u32[]{:S(2)}, u32[]{:S(2)}) collective-permute-start(bf16[32,2176]{1,0:T(8,128)(2,1)S(1)} %get-tuple-element.38.refs_0_), channel_id=1, source_target_pairs={{0,12},{2,14},{4,8},{6,10},{8,4},{10,6},{12,0},{14,2},{1,13},{3,15... | collective-permute-start | bytes 417800 | tf_op jit(solution)/shard_map/ppermute | solution.py:268
  55.2 8.9 %collective-permute-start.21 = (bf16[32,2176]{1,0:T(8,128)(2,1)S(1)}, bf16[32,2176]{1,0:T(8,128)(2,1)S(1)}, u32[]{:S(2)}, u32[]{:S(2)}) collective-permute-start(bf16[32,2176]{1,0:T(8,128)(2,1)S(1)} %get-tuple-element.38.refs_0_), channel_id=1, source_target_pairs={{0,4},{2,6},{4,0},{6,2},{8,12},{10,14},{12,8},{14,10},{1,5},{3,7},... | collective-permute-start | bytes 417800 | tf_op jit(solution)/shard_map/ppermute | solution.py:268
  63.5 1.4 %collective-permute-start.14 = (bf16[32,2176]{1,0:T(8,128)(2,1)S(1)}, bf16[32,2176]{1,0:T(8,128)(2,1)S(1)}, u32[]{:S(2)}, u32[]{:S(2)}) collective-permute-start(bf16[32,2176]{1,0:T(8,128)(2,1)S(1)} %collective-permute-done.12.refs_0_), channel_id=1, source_target_pairs={{0,2},{2,0},{4,6},{6,4},{8,10},{10,8},{12,14},{14,12},{1,3},{3,1},... | collective-permute-start | bytes 417800 | tf_op jit(solution)/shard_map/ppermute | solution.py:268
  63.5 1.6 %collective-permute-start.15 = (bf16[32,2176]{1,0:T(8,128)(2,1)S(1)}, bf16[32,2176]{1,0:T(8,128)(2,1)S(1)}, u32[]{:S(2)}, u32[]{:S(2)}) collective-permute-start(bf16[32,2176]{1,0:T(8,128)(2,1)S(1)} %collective-permute-done.13.refs_1_), channel_id=1, source_target_pairs={{0,2},{2,0},{4,6},{6,4},{8,10},{10,8},{12,14},{14,12},{1,3},{3,1},... | collective-permute-start | bytes 417800 | tf_op jit(solution)/shard_map/ppermute | solution.py:268
  64.0 5.9 %collective-permute-start.22 = (bf16[32,2176]{1,0:T(8,128)(2,1)S(1)}, bf16[32,2176]{1,0:T(8,128)(2,1)S(1)}, u32[]{:S(2)}, u32[]{:S(2)}) collective-permute-start(bf16[32,2176]{1,0:T(8,128)(2,1)S(1)} %get-tuple-element.38.refs_0_), channel_id=1, source_target_pairs={{0,2},{2,0},{4,6},{6,4},{8,10},{10,8},{12,14},{14,12},{1,3},{3,1},... | collective-permute-start | bytes 417800 | tf_op jit(solution)/shard_map/ppermute | solution.py:268
  64.1 5.8 %collective-permute-start.23 = (bf16[32,2176]{1,0:T(8,128)(2,1)S(1)}, bf16[32,2176]{1,0:T(8,128)(2,1)S(1)}, u32[]{:S(2)}, u32[]{:S(2)}) collective-permute-start(bf16[32,2176]{1,0:T(8,128)(2,1)S(1)} %collective-permute-done.21.refs_1_), channel_id=1, source_target_pairs={{0,2},{2,0},{4,6},{6,4},{8,10},{10,8},{12,14},{14,12},{1,3},{3,1},... | collective-permute-start | bytes 417800 | tf_op jit(solution)/shard_map/ppermute | solution.py:268
  67.4 13.1 %collective-permute-start.16 = (bf16[128,1664]{1,0:T(8,128)(2,1)S(1)}, bf16[128,1664]{1,0:T(8,128)(2,1)S(1)}, u32[]{:S(2)}, u32[]{:S(2)}) collective-permute-start(bf16[128,1664]{1,0:T(8,128)(2,1)S(1)} %get-tuple-element.41), channel_id=1, source_target_pairs={{0,1},{1,0},{2,3},{3,2},{4,5},{5,4},{6,7},{7,6},{8,9},{9,8},{10,11... | collective-permute-start | bytes 1277960 | tf_op jit(solution)/shard_map/ppermute | solution.py:268
  72.3 17.4 %collective-permute-start.24 = (bf16[128,1664]{1,0:T(8,128)(2,1)S(1)}, bf16[128,1664]{1,0:T(8,128)(2,1)S(1)}, u32[]{:S(2)}, u32[]{:S(2)}) collective-permute-start(bf16[128,1664]{1,0:T(8,128)(2,1)S(1)} %get-tuple-element.49), channel_id=1, source_target_pairs={{0,1},{1,0},{2,3},{3,2},{4,5},{5,4},{6,7},{7,6},{8,9},{9,8},{10,11... | collective-permute-start | bytes 1277960 | tf_op jit(solution)/shard_map/ppermute | solution.py:268
  81.4 12.5 %collective-permute-start.17 = (bf16[128,768]{1,0:T(8,128)(2,1)S(1)}, bf16[128,768]{1,0:T(8,128)(2,1)S(1)}, u32[]{:S(2)}, u32[]{:S(2)}) collective-permute-start(bf16[128,768]{1,0:T(8,128)(2,1)S(1)} %act.2.act_ref), channel_id=1, source_target_pairs={{0,1},{1,0},{2,3},{3,2},{4,5},{5,4},{6,7},{7,6},{8,9},{9,8},{10,11... | collective-permute-start | bytes 589832 | tf_op jit(solution)/shard_map/ppermute | solution.py:268
  90.5 7.2 %collective-permute-start.25 = (bf16[128,768]{1,0:T(8,128)(2,1)S(1)}, bf16[128,768]{1,0:T(8,128)(2,1)S(1)}, u32[]{:S(2)}, u32[]{:S(2)}) collective-permute-start(bf16[128,768]{1,0:T(8,128)(2,1)S(1)} %act.3.act_ref), channel_id=1, source_target_pairs={{0,1},{1,0},{2,3},{3,2},{4,5},{5,4},{6,7},{7,6},{8,9},{9,8},{10,11... | collective-permute-start | bytes 589832 | tf_op jit(solution)/shard_map/ppermute | solution.py:268
  95.5 3.9 %collective-permute-start.18 = (bf16[64,2048]{1,0:T(8,128)(2,1)S(1)}, bf16[64,2048]{1,0:T(8,128)(2,1)S(1)}, u32[]{:S(2)}, u32[]{:S(2)}) collective-permute-start(bf16[64,2048]{1,0:T(8,128)(2,1)S(1)} %get-tuple-element.45), channel_id=1, source_target_pairs={{0,2},{2,0},{4,6},{6,4},{8,10},{10,8},{12,14},{14,12},{1,3},{3,1},... | collective-permute-start | bytes 786440 | tf_op jit(solution)/shard_map/ppermute | solution.py:268
  99.3 4.7 %collective-permute-start.26 = (bf16[64,2048]{1,0:T(8,128)(2,1)S(1)}, bf16[64,2048]{1,0:T(8,128)(2,1)S(1)}, u32[]{:S(2)}, u32[]{:S(2)}) collective-permute-start(bf16[64,2048]{1,0:T(8,128)(2,1)S(1)} %get-tuple-element.52), channel_id=1, source_target_pairs={{0,2},{2,0},{4,6},{6,4},{8,10},{10,8},{12,14},{14,12},{1,3},{3,1},... | collective-permute-start | bytes 786440 | tf_op jit(solution)/shard_map/ppermute | solution.py:268
  99.4 13.4 %collective-permute-start.19 = (bf16[32,2048]{1,0:T(8,128)(2,1)S(1)}, bf16[32,2048]{1,0:T(8,128)(2,1)S(1)}, u32[]{:S(2)}, u32[]{:S(2)}) collective-permute-start(bf16[32,2048]{1,0:T(8,128)(2,1)S(1)} %get-tuple-element.46), channel_id=1, source_target_pairs={{0,8},{2,10},{4,12},{6,14},{8,0},{10,2},{12,4},{14,6},{1,9},{3,11}... | collective-permute-start | bytes 393224 | tf_op jit(solution)/shard_map/ppermute | solution.py:268
  102.8 10.0 %collective-permute-start.20 = (bf16[32,2048]{1,0:T(8,128)(2,1)S(1)}, bf16[32,2048]{1,0:T(8,128)(2,1)S(1)}, u32[]{:S(2)}, u32[]{:S(2)}) collective-permute-start(bf16[32,2048]{1,0:T(8,128)(2,1)S(1)} %get-tuple-element.47), channel_id=1, source_target_pairs={{0,12},{2,14},{4,8},{6,10},{8,4},{10,6},{12,0},{14,2},{1,13},{3,15... | collective-permute-start | bytes 393224 | tf_op jit(solution)/shard_map/ppermute | solution.py:268
  104.0 10.0 %collective-permute-start.27 = (bf16[32,2048]{1,0:T(8,128)(2,1)S(1)}, bf16[32,2048]{1,0:T(8,128)(2,1)S(1)}, u32[]{:S(2)}, u32[]{:S(2)}) collective-permute-start(bf16[32,2048]{1,0:T(8,128)(2,1)S(1)} %get-tuple-element.54), channel_id=1, source_target_pairs={{0,4},{2,6},{4,0},{6,2},{8,12},{10,14},{12,8},{14,10},{1,5},{3,7},... | collective-permute-start | bytes 393224 | tf_op jit(solution)/shard_map/ppermute | solution.py:268

commit v4 on v3

--- a/solution.py
+++ b/solution.py
@@ -6,6 +6,7 @@
 from jax import lax
 from jax.experimental import pallas as pl
 from jax.experimental.pallas import tpu as pltpu
+
 from jax.sharding import PartitionSpec as P
 
 NEG = -1e30
@@ -81,13 +82,14 @@
 
 
 def attend_kernel(
-    req_count, group, page_len, index_ref, code_ref, q_hbm, fresh_hbm, kv_hbm, gate_up_hbm, down_hbm,
-    out_ref, gate_up_ref, down_ref, q_ref, kbuf, vbuf, fkbuf, fvbuf, s_ref, acc_ref, l_ref, m_ref, ksem, vsem, fsem, wsem,
+    req_count, group, page_len, blocks, index_ref, table_ref, length_ref, q_hbm, fresh_hbm, kv_hbm, gate_up_hbm, down_hbm,
+    out_ref, gate_up_ref, down_ref, q_ref, kbuf, vbuf, fkbuf, fvbuf, s_ref, acc_ref, l_ref, m_ref, code_ref, ksem, vsem, fsem, wsem,
 ):
     f32, bf16 = jnp.float32, jnp.bfloat16
     width = q_ref.shape[2]
-    blocks, columns = code_ref.shape
-    tokens = columns // 2
+    tokens = kbuf.shape[0] // blocks
+    columns = 2 * tokens
+    pages = tokens // page_len
     rows = q_ref.shape[0] * group
 
     def fetch(half, buf, sem, b):
@@ -111,6 +113,42 @@
     ]
     for copy in weight_copies:
         copy.start()
+
+    def clear(p, c):
+        code_ref[p] = 0
+        return c
+
+    lax.fori_loop(0, blocks * pages, clear, 0, unroll=16)
+    for r in range(req_count):
+        length = length_ref[r]
+
+        def put(j, c, r=r, length=length):
+            code_ref[table_ref[r, j]] = r * 32 + jnp.minimum(length - j * page_len, page_len)
+            return c
+
+        count = (length + page_len - 1) // page_len
+
+        def four(i, c, r=r, length=length):
+            spots = [table_ref[r, 4 * i + k] for k in range(4)]
+            for k, spot in enumerate(spots):
+                code_ref[spot] = r * 32 + jnp.minimum(length - (4 * i + k) * page_len, page_len)
+            return c
+
+        lax.fori_loop(0, count // 4, four, 0)
+        lax.fori_loop(count // 4 * 4, count, put, 0)
+    lane_page = lax.broadcasted_iota(jnp.int32, (1, width), 1) // (2 * page_len)
+    per_tile = width // (2 * page_len)
+
+    def codes(b):
+        tiles = []
+        for t in range(columns // width):
+            at = b * pages + t * per_tile
+            tile = jnp.zeros((1, width), jnp.int32)
+            for i in range(per_tile):
+                tile = jnp.where(lane_page == i, code_ref[at + i], tile)
+            tiles.append(tile)
+        return jnp.concatenate(tiles, axis=1)
+
     for copy in fresh_copies:
         copy.wait()
 
@@ -129,9 +167,10 @@
         ).astype(bf16)
 
     def scores(keys):
-        return lax.dot_general(
-            q2, widen(keys), (((1,), (1,)), ((), ())), preferred_element_type=f32
-        )
+        flat = keys.T.astype(f32)
+        even = lax.broadcasted_iota(jnp.int32, (1, keys.shape[0]), 1) % 2 == 0
+        both = jnp.concatenate([jnp.where(even, flat, 0.0), jnp.where(even, 0.0, flat)], axis=0)
+        return jnp.dot(q2, both.astype(bf16), preferred_element_type=f32)
 
     fresh = fkbuf.shape[0] * 2
     fresh_keys = fkbuf.reshape(fresh, width)[...]
@@ -145,7 +184,7 @@
     def first(b, c):
         fetch(0, kbuf, ksem, b).wait()
         keys = kbuf.reshape(kbuf.shape[0] * 2, width)[pl.ds(b * columns, columns), :]
-        code = code_ref[pl.ds(b, 1), :]
+        code = codes(b)
         owner = jnp.where(slot < (code & 31), code >> 5, -1)
         s = jnp.where(owner == row_req, scores(keys), NEG)
         s_ref[b] = s
@@ -207,28 +246,20 @@
     step_count, req_count, head_count, head_width = queries.shape
     pool_pages, page_len, kv_heads, _ = kv_pool.shape
     group = head_count // kv_heads
-    slot = jnp.arange(page_table.shape[1], dtype=jnp.int32)
-    live = jnp.clip(context_lengths[:, None] - slot[None, :] * page_len, 0, page_len)
-    entry = jnp.arange(req_count, dtype=jnp.int32)[:, None] * 32 + live
-    pages = jnp.arange(pool_pages, dtype=jnp.int32)
-    code = jnp.sum(
-        jnp.where(page_table[:, :, None] == pages, entry[:, :, None], 0), axis=(0, 1)
-    )
-    blocks = 10
-    code = jnp.repeat(code, page_len * kv_heads).reshape(blocks, -1)
+    blocks = next(b for b in (4, 5, 2, 1) if pool_pages * page_len * 2 % (b * head_width) == 0)
     tokens = pool_pages * page_len
     rows, columns = step_count * req_count * group, tokens * 2 // blocks
     bf16, f32 = jnp.bfloat16, jnp.float32
     vmem, hbm = pl.BlockSpec(memory_space=pltpu.VMEM), pl.BlockSpec(memory_space=pltpu.HBM)
     own = step_count * req_count
     return pl.pallas_call(
-        functools.partial(attend_kernel, req_count, group, page_len),
+        functools.partial(attend_kernel, req_count, group, page_len, blocks),
         out_shape=(
             jax.ShapeDtypeStruct((own, head_count * head_width), bf16),
             pltpu.VMEM(gate_up.shape, bf16),
             pltpu.VMEM(down_proj.shape, bf16),
         ),
-        in_specs=[pl.BlockSpec(memory_space=pltpu.SMEM), vmem, hbm, hbm, hbm, hbm, hbm],
+        in_specs=[pl.BlockSpec(memory_space=pltpu.SMEM)] * 3 + [hbm] * 5,
         out_specs=(vmem, vmem, vmem),
         scratch_shapes=[
             pltpu.VMEM((own, head_count, head_width), bf16),
@@ -240,6 +271,7 @@
             pltpu.VMEM((rows, 2 * head_width), f32),
             pltpu.VMEM((rows, head_width), f32),
             pltpu.VMEM((rows, head_width), f32),
+            pltpu.SMEM((pool_pages,), jnp.int32),
             pltpu.SemaphoreType.DMA((blocks,)),
             pltpu.SemaphoreType.DMA((blocks,)),
             pltpu.SemaphoreType.DMA((3,)),
@@ -249,7 +281,8 @@
         name="attend_pool",
     )(
         index,
-        code,
+        page_table,
+        context_lengths,
         *[
             pltpu.with_memory_space_constraint(value, pltpu.HBM)
             for value in (
@@ -414,6 +447,10 @@
         send_ref[:, at : at + step] = value[half:].astype(jnp.bfloat16)
 
 
+def hold_kernel(piece_ref, out_ref):
+    out_ref[...] = piece_ref[...]
+
+
 def fold_kernel(keep_ref, got_ref, *outs):
     own = outs[0].shape[0]
     for k, out in enumerate(outs):
@@ -422,7 +459,7 @@
         out[...] = value.astype(out.dtype)
 
 
-def small_call(kernel, name, outs, *args, index=None, flops=0, limit=8):
+def small_call(kernel, outs, *args, index=None, flops=0, limit=8):
     vmem, smem = pl.BlockSpec(memory_space=pltpu.VMEM), pl.BlockSpec(memory_space=pltpu.SMEM)
     specs = [vmem] * len(args)
     if index is not None:
@@ -436,7 +473,6 @@
         cost_estimate=pl.CostEstimate(flops=flops, bytes_accessed=0, transcendentals=0)
         if flops
         else None,
-        name=name,
     )(*args)
 
 
@@ -496,7 +532,7 @@
     dp_index, x_index = lax.axis_index("dp"), lax.axis_index("expert")
     chips = dp_count // 2
     chip_index, core_index = dp_index // 2, dp_index % 2
-    local_experts, _, width, hidden = gate_up.shape
+    local_experts, _, width, _ = gate_up.shape
     expert_total = local_experts * dp_count
     steps, reqs = queries.shape[:2]
     own = steps * reqs
@@ -600,7 +636,6 @@
     block = out_weight.shape[1]
     keep, send = small_call(
         functools.partial(project_kernel, chips),
-        "project",
         [((chips, own, block), bf16)] * 2,
         *mine,
         out_weight,
@@ -608,7 +643,7 @@
         flops=2 * dp_count * own * head_cols * block,
     )
     paired = small_call(
-        pair_kernel, "pair", [((own, 2 * block), bf16)] * chips, keep, exchange(send, "dp", 1)
+        pair_kernel, [((own, 2 * block), bf16)] * chips, keep, exchange(send, "dp", 1)
     )
     near = chips // x_count
     arrived = []
@@ -625,7 +660,6 @@
     extra = -(-(2 * expert_total + 2) // 128) * 128
     stream, rows = small_call(
         functools.partial(stream_kernel, chips, expert_total),
-        "stream",
         [((own, width), f32), ((own, width + extra), bf16)],
         *arrived,
         residual.reshape(own, width),
@@ -634,15 +668,18 @@
         jnp.swapaxes(route_weights, 1, 2),
         index=index,
     )
-    from_chip = [rows] + [exchange(rows, "dp", 2 * k) for k in range(1, chips)]
+    from_chip = [rows]
+    for k in range(1, chips):
+        from_chip.append(exchange(rows, "dp", 2 * k))
+        if k == 1 or k % 2 == 0:
+            (from_chip[k],) = small_call(hold_kernel, [(rows.shape, bf16)], from_chip[k])
     result = stream
-    for chunk in (range(chips // 2, chips), range(chips // 2)):
+    for chunk in (range(1, chips, 2), range(0, chips, 2)):
         pieces = [from_chip[k] for k in chunk]
         pieces = pieces + [exchange(piece, "dp", 1) for piece in pieces]
         count = len(pieces) * own
         keep, send, extras = small_call(
             functools.partial(gate_up_kernel, len(pieces)),
-            "gate_up",
             [
                 ((2 * local_experts, count, part), f32),
                 ((count, 2 * local_experts * part + extra), bf16),
@@ -653,28 +690,27 @@
             index=index,
             flops=4 * count * width * hidden * local_experts,
         )
+        got = exchange(send, "expert", 1)
         (act,) = small_call(
             functools.partial(act_kernel, local_experts, expert_total, x_count * width),
-            "act",
             [((count, local_experts * part), bf16)],
             keep,
-            exchange(send, "expert", 1),
+            got,
             extras,
             index=index,
         )
+        got = exchange(act, "expert", 1)
         keep, send = small_call(
             down_kernel,
-            "down",
             [((count // 2, width), f32), ((count // 2, width), bf16)],
             act,
-            exchange(act, "expert", 1),
+            got,
             down_proj,
             index=index,
             flops=2 * count * width * hidden * local_experts,
         )
         folded = small_call(
             fold_kernel,
-            "fold",
             [((own, width), bf16 if k else f32) for k in chunk],
             keep,
             exchange(send, "dp", 1),
@@ -694,7 +730,9 @@
         and args[10].shape[3] % 256 == 0
         and args[10].shape[2] % 512 == 0
     )
-    return (body_fast if fast else body_plain)(*args)
+    if not fast:
+        return body_plain(*args)
+    return body_fast(*args)
 
 
 def solution(mesh):

time: 115 us -> 113 us (0.983)
  waiting for transfers between devices: 52 us -> 56.9 us
  other arithmetic: 3.84 us -> 0.81 us
  Pallas kernels: 24.1 us -> 21.8 us
  starting transfers between devices: 33.3 us -> 32 us
    ppermute x24, waiting for transfers between devices: 48.6 us -> 53.6 us  [exchange(): return lax.ppermute(value, axis, [(i, i ^ mask) for i in range(count)])]
    reduce_sum x1 -> x0, other arithmetic: 2.3 us -> none  [attend_pool(): jnp.sum(jnp.where(page_table[:, :, None] == pages, entry[:, :, None], 0),...]
    pallas_call x1, Pallas kernels: 12.4 us -> 10.2 us  [attend_pool(): pl.pallas_call(functools.partial(attend_kernel, req_count, group, page_le...]
    ppermute x24, starting transfers between devices: 27.7 us -> 25.9 us  [exchange(): return lax.ppermute(value, axis, [(i, i ^ mask) for i in range(count)])]
    pallas_call x11 -> x13, Pallas kernels: 11.6 us -> 11.7 us  [small_call(): pl.pallas_call(kernel, out_shape=tuple((jax.ShapeDtypeStruct(shape, dtype...]
  transfers between devices with their start and end apart: 28 -> 28, of which waited for: 16 -> 14; matrix products, arithmetic and copies ran while one was open for 0% -> 0% of each run, Pallas kernels for 8% -> 9%
where the time goes in v4:
time: 113 us
  waiting for transfers between devices  56.9 us (50%)
  starting transfers between devices  32 us (28%)
  Pallas kernels  21.8 us (19%)
  local copies, waits for them, and re-layouts  1.41 us (1%)
    ppermute x24, waiting for transfers between devices, exchange(): return lax.ppermute(value, axis, [(i, i ^ mask) for i in range(count)])  53.6 us
    ppermute x24, starting transfers between devices, exchange(): return lax.ppermute(value, axis, [(i, i ^ mask) for i in range(count)])  25.9 us
    pallas_call x13, Pallas kernels, small_call(): pl.pallas_call(kernel, out_shape=tuple((jax.ShapeDtypeStruct(shape, dtype...  11.7 us
    pallas_call x1, Pallas kernels, attend_pool(): pl.pallas_call(functools.partial(attend_kernel, req_count, group, page_le...  10.2 us
    ppermute x4, starting transfers between devices, body_fast(): arrived.append(lax.ppermute(paired[k], ('dp', 'expert'), moves))  6.16 us
    ppermute x4, waiting for transfers between devices, body_fast(): arrived.append(lax.ppermute(paired[k], ('dp', 'expert'), moves))  3.29 us
  transfers between devices with their start and end apart: 28, of which 14 were waited for; matrix products, arithmetic and copies ran while one was open for 0% of the time, Pallas kernels for 9%

profile of v4, /device:TPU:0, one launch (start us, length us, event | category | flops | bytes accessed | tf_op | source)
XLA Modules:
  0.0 113.2 jit_solution(2102142447854547679)
XLA Ops:
  0.0 0.1 pad_add_fusion.index_ref
  0.1 0.7 copy-done.2
  0.8 0.7 copy-done.6
  1.5 10.2 %attend_pool.1 = (bf16[32,2048]{1,0:T(8,128)(2,1)S(1)}, bf16[2,2,2048,768]{3,2,1,0:T(8,128)(2,1)S(1)}, bf16[2,768,2048]{2,1,0:T(8,128)(2,1)S(1)}) custom-call(s32[2]{0:T(128)S(1)} %pad_add_fusion.index_ref, s32[16,305]{1,0:T(8,128)S(1)} %copy-done.2, s32[16]{0:T(128)S(1)} %copy-done.6, bf16[32,16,128]{2,1,0:T(8,128)(2,1)} %bitcast.15, ...), custom_call_target="tpu_custom_call" | custom-call | tf_op jit(solution)/shard_map/attend_pool/pallas_call | solution.py:255
  11.7 3.7 %collective-permute-start = (bf16[32,2048]{1,0:T(8,128)(2,1)S(1)}, bf16[32,2048]{1,0:T(8,128)(2,1)S(1)}, u32[]{:S(2)}, u32[]{:S(2)}) collective-permute-start(bf16[32,2048]{1,0:T(8,128)(2,1)S(1)} %get-tuple-element.30.refs_0_), channel_id=1, source_target_pairs={{0,4},{2,6},{4,0},{6,2},{8,12},{10,14},{12,8},{14,10},{1,5},{3,7},... | collective-permute-start | bytes 393224 | tf_op jit(solution)/shard_map/ppermute | solution.py:301
  15.4 2.4 %collective-permute-start.1 = (bf16[32,2048]{1,0:T(8,128)(2,1)S(1)}, bf16[32,2048]{1,0:T(8,128)(2,1)S(1)}, u32[]{:S(2)}, u32[]{:S(2)}) collective-permute-start(bf16[32,2048]{1,0:T(8,128)(2,1)S(1)} %get-tuple-element.30.refs_0_), channel_id=1, source_target_pairs={{0,8},{2,10},{4,12},{6,14},{8,0},{10,2},{12,4},{14,6},{1,9},{3,11}... | collective-permute-start | bytes 393224 | tf_op jit(solution)/shard_map/ppermute | solution.py:301
  17.8 0.6 collective-permute-start.2
  18.3 0.5 collective-permute-start.4
  18.8 9.4 %collective-permute-done.1.refs_2_ = bf16[32,2048]{1,0:T(8,128)(2,1)S(1)} collective-permute-done((bf16[32,2048]{1,0:T(8,128)(2,1)S(1)}, bf16[32,2048]{1,0:T(8,128)(2,1)S(1)}, u32[]{:S(2)}, u32[]{:S(2)}) %collective-permute-start.1) | collective-permute-done | bytes 131104 | tf_op jit(solution)/shard_map/ppermute | solution.py:301
  28.3 0.5 collective-permute-start.6
  28.8 0.8 collective-permute-done.5.refs_6_
  29.6 0.2 collective-permute-done.6.refs_7_
  29.8 1.3 %shard_map.118 = (bf16[4,32,512]{2,1,0:T(8,128)(2,1)S(1)}, bf16[4,32,512]{2,1,0:T(8,128)(2,1)S(1)}) custom-call(s32[2]{0:T(128)S(1)} %pad_add_fusion.index_ref, bf16[32,2048]{1,0:T(8,128)(2,1)S(1)} %get-tuple-element.30.refs_0_, bf16[32,2048]{1,0:T(8,128)(2,1)S(1)} %collective-permute-done.refs_1_, bf16[32,2048]{1,0:T(8,128)(2,1)S(1)} %collective-permute-done.1.refs_2_, ...), custom_call_target="tpu_custom_call" | custom-call | flops 536870912 | tf_op jit(solution)/shard_map/pallas_call | solution.py:467
  31.1 0.4 collective-permute-start.7
  31.5 1.0 collective-permute-done.7.got_ref
  32.5 3.2 %collective-permute-start.10 = (bf16[32,1024]{1,0:T(8,128)(2,1)S(1)}, bf16[32,1024]{1,0:T(8,128)(2,1)S(1)}, u32[]{:S(2)}, u32[]{:S(2)}) collective-permute-start(bf16[32,1024]{1,0:T(8,128)(2,1)S(1)} %get-tuple-element.35), channel_id=1, source_target_pairs={{0,8},{1,0},{2,10},{3,2},{4,12},{5,4},{6,14},{7,6},{8,9},{9,1},{10... | collective-permute-start | bytes 196616 | tf_op jit(solution)/shard_map/ppermute | solution.py:658
  35.7 0.9 collective-permute-start.11
  36.6 0.8 collective-permute-start.8
  37.5 1.2 %collective-permute-start.9 = (bf16[32,1024]{1,0:T(8,128)(2,1)S(1)}, bf16[32,1024]{1,0:T(8,128)(2,1)S(1)}, u32[]{:S(2)}, u32[]{:S(2)}) collective-permute-start(bf16[32,1024]{1,0:T(8,128)(2,1)S(1)} %get-tuple-element.34), channel_id=1, source_target_pairs={{0,4},{1,12},{2,6},{3,14},{4,0},{5,8},{6,2},{7,10},{8,5},{9,13},{1... | collective-permute-start | bytes 196616 | tf_op jit(solution)/shard_map/ppermute | solution.py:658
  38.7 3.3 %collective-permute-done.11.refs_3_ = bf16[32,1024]{1,0:T(8,128)(2,1)S(1)} collective-permute-done((bf16[32,1024]{1,0:T(8,128)(2,1)S(1)}, bf16[32,1024]{1,0:T(8,128)(2,1)S(1)}, u32[]{:S(2)}, u32[]{:S(2)}) %collective-permute-start.11) | collective-permute-done | bytes 65568 | tf_op jit(solution)/shard_map/ppermute | solution.py:658
  42.0 0.7 shard_map.120
  42.8 1.0 collective-permute-start.12
  43.8 7.8 %collective-permute-start.13 = (bf16[32,2176]{1,0:T(8,128)(2,1)S(1)}, bf16[32,2176]{1,0:T(8,128)(2,1)S(1)}, u32[]{:S(2)}, u32[]{:S(2)}) collective-permute-start(bf16[32,2176]{1,0:T(8,128)(2,1)S(1)} %get-tuple-element.38.refs_0_), channel_id=1, source_target_pairs={{0,12},{2,14},{4,8},{6,10},{8,4},{10,6},{12,0},{14,2},{1,13},{3,15... | collective-permute-start | bytes 417800 | tf_op jit(solution)/shard_map/ppermute | solution.py:301
  51.6 0.1 collective-permute-start.14
  51.7 6.7 %collective-permute-done.13.refs_1_ = bf16[32,2176]{1,0:T(8,128)(2,1)S(1)} collective-permute-done((bf16[32,2176]{1,0:T(8,128)(2,1)S(1)}, bf16[32,2176]{1,0:T(8,128)(2,1)S(1)}, u32[]{:S(2)}, u32[]{:S(2)}) %collective-permute-start.13) | collective-permute-done | bytes 139296 | tf_op jit(solution)/shard_map/ppermute | solution.py:301
  58.5 0.5 collective-permute-start.22
  59.0 3.9 %collective-permute-done.21.piece_ref = bf16[32,2176]{1,0:T(8,128)(2,1)S(1)} collective-permute-done((bf16[32,2176]{1,0:T(8,128)(2,1)S(1)}, bf16[32,2176]{1,0:T(8,128)(2,1)S(1)}, u32[]{:S(2)}, u32[]{:S(2)}) %collective-permute-start.21) | collective-permute-done | bytes 139296 | tf_op jit(solution)/shard_map/ppermute | solution.py:301
  62.9 0.1 collective-permute-start.23
  63.0 2.4 %shard_map.122 = (f32[4,128,384]{2,1,0:T(8,128)S(1)}, bf16[128,1664]{1,0:T(8,128)(2,1)S(1)}, bf16[128,128]{1,0:T(8,128)(2,1)S(1)}) custom-call(s32[2]{0:T(128)S(1)} %pad_add_fusion.index_ref, bf16[32,2176]{1,0:T(8,128)(2,1)S(1)} %shard_map.121.refs_0_, bf16[32,2176]{1,0:T(8,128)(2,1)S(1)} %collective-permute-done.13.refs_1_, ...), custom_call_target="tpu_custom_call" | custom-call | flops 1610612736 | tf_op jit(solution)/shard_map/pallas_call | solution.py:467
  65.4 1.2 %collective-permute-start.16 = (bf16[128,1664]{1,0:T(8,128)(2,1)S(1)}, bf16[128,1664]{1,0:T(8,128)(2,1)S(1)}, u32[]{:S(2)}, u32[]{:S(2)}) collective-permute-start(bf16[128,1664]{1,0:T(8,128)(2,1)S(1)} %get-tuple-element.41), channel_id=1, source_target_pairs={{0,1},{1,0},{2,3},{3,2},{4,5},{5,4},{6,7},{7,6},{8,9},{9,8},{10,11... | collective-permute-start | bytes 1277960 | tf_op jit(solution)/shard_map/ppermute | solution.py:301
  66.6 2.4 %shard_map.127 = (f32[4,128,384]{2,1,0:T(8,128)S(1)}, bf16[128,1664]{1,0:T(8,128)(2,1)S(1)}, bf16[128,128]{1,0:T(8,128)(2,1)S(1)}) custom-call(s32[2]{0:T(128)S(1)} %pad_add_fusion.index_ref, bf16[32,2176]{1,0:T(8,128)(2,1)S(1)} %get-tuple-element.38.refs_0_, bf16[32,2176]{1,0:T(8,128)(2,1)S(1)} %shard_map.126.refs_1_, ...), custom_call_target="tpu_custom_call" | custom-call | flops 1610612736 | tf_op jit(solution)/shard_map/pallas_call | solution.py:467
  69.0 1.0 collective-permute-start.24
  70.0 8.2 %collective-permute-done.16.got_ref = bf16[128,1664]{1,0:T(8,128)(2,1)S(1)} collective-permute-done((bf16[128,1664]{1,0:T(8,128)(2,1)S(1)}, bf16[128,1664]{1,0:T(8,128)(2,1)S(1)}, u32[]{:S(2)}, u32[]{:S(2)}) %collective-permute-start.16) | collective-permute-done | bytes 426016 | tf_op jit(solution)/shard_map/ppermute | solution.py:301
  78.1 0.8 shard_map.123.act_ref
  78.9 1.2 %collective-permute-start.17 = (bf16[128,768]{1,0:T(8,128)(2,1)S(1)}, bf16[128,768]{1,0:T(8,128)(2,1)S(1)}, u32[]{:S(2)}, u32[]{:S(2)}) collective-permute-start(bf16[128,768]{1,0:T(8,128)(2,1)S(1)} %shard_map.123.act_ref), channel_id=1, source_target_pairs={{0,1},{1,0},{2,3},{3,2},{4,5},{5,4},{6,7},{7,6},{8,9},{9,8},{10,11... | collective-permute-start | bytes 589832 | tf_op jit(solution)/shard_map/ppermute | solution.py:301
  80.1 7.1 %collective-permute-done.24.got_ref = bf16[128,1664]{1,0:T(8,128)(2,1)S(1)} collective-permute-done((bf16[128,1664]{1,0:T(8,128)(2,1)S(1)}, bf16[128,1664]{1,0:T(8,128)(2,1)S(1)}, u32[]{:S(2)}, u32[]{:S(2)}) %collective-permute-start.24) | collective-permute-done | bytes 426016 | tf_op jit(solution)/shard_map/ppermute | solution.py:301
  87.3 0.8 shard_map.128.act_ref
  88.1 1.2 %collective-permute-start.25 = (bf16[128,768]{1,0:T(8,128)(2,1)S(1)}, bf16[128,768]{1,0:T(8,128)(2,1)S(1)}, u32[]{:S(2)}, u32[]{:S(2)}) collective-permute-start(bf16[128,768]{1,0:T(8,128)(2,1)S(1)} %shard_map.128.act_ref), channel_id=1, source_target_pairs={{0,1},{1,0},{2,3},{3,2},{4,5},{5,4},{6,7},{7,6},{8,9},{9,8},{10,11... | collective-permute-start | bytes 589832 | tf_op jit(solution)/shard_map/ppermute | solution.py:301
  89.2 2.2 %collective-permute-done.17.got_ref = bf16[128,768]{1,0:T(8,128)(2,1)S(1)} collective-permute-done((bf16[128,768]{1,0:T(8,128)(2,1)S(1)}, bf16[128,768]{1,0:T(8,128)(2,1)S(1)}, u32[]{:S(2)}, u32[]{:S(2)}) %collective-permute-start.17) | collective-permute-done | bytes 196640 | tf_op jit(solution)/shard_map/ppermute | solution.py:301
  91.5 1.5 %shard_map.124 = (f32[64,2048]{1,0:T(8,128)S(1)}, bf16[64,2048]{1,0:T(8,128)(2,1)S(1)}) custom-call(s32[2]{0:T(128)S(1)} %pad_add_fusion.index_ref, bf16[128,768]{1,0:T(8,128)(2,1)S(1)} %shard_map.123.act_ref, bf16[128,768]{1,0:T(8,128)(2,1)S(1)} %collective-permute-done.17.got_ref, bf16[2,768,2048]{2,1,0:T(8,128)(2,1)S(1)} %get-tuple-element.43.weight_ref), custom_call_target="tpu_custom_call" | custom-call | flops 805306368 | tf_op jit(solution)/shard_map/pallas_call | solution.py:467
  93.1 2.1 %collective-permute-done.25.got_ref = bf16[128,768]{1,0:T(8,128)(2,1)S(1)} collective-permute-done((bf16[128,768]{1,0:T(8,128)(2,1)S(1)}, bf16[128,768]{1,0:T(8,128)(2,1)S(1)}, u32[]{:S(2)}, u32[]{:S(2)}) %collective-permute-start.25) | collective-permute-done | bytes 196640 | tf_op jit(solution)/shard_map/ppermute | solution.py:301
  95.2 1.5 %shard_map.129 = (f32[64,2048]{1,0:T(8,128)S(1)}, bf16[64,2048]{1,0:T(8,128)(2,1)S(1)}) custom-call(s32[2]{0:T(128)S(1)} %pad_add_fusion.index_ref, bf16[128,768]{1,0:T(8,128)(2,1)S(1)} %shard_map.128.act_ref, bf16[128,768]{1,0:T(8,128)(2,1)S(1)} %collective-permute-done.25.got_ref, bf16[2,768,2048]{2,1,0:T(8,128)(2,1)S(1)} %get-tuple-element.43.weight_ref), custom_call_target="tpu_custom_call" | custom-call | flops 805306368 | tf_op jit(solution)/shard_map/pallas_call | solution.py:467
  97.0 2.1 %collective-permute-start.20 = (bf16[32,2048]{1,0:T(8,128)(2,1)S(1)}, bf16[32,2048]{1,0:T(8,128)(2,1)S(1)}, u32[]{:S(2)}, u32[]{:S(2)}) collective-permute-start(bf16[32,2048]{1,0:T(8,128)(2,1)S(1)} %get-tuple-element.47), channel_id=1, source_target_pairs={{0,12},{2,14},{4,8},{6,10},{8,4},{10,6},{12,0},{14,2},{1,13},{3,15... | collective-permute-start | bytes 393224 | tf_op jit(solution)/shard_map/ppermute | solution.py:301
  99.1 1.5 %collective-permute-start.27 = (bf16[32,2048]{1,0:T(8,128)(2,1)S(1)}, bf16[32,2048]{1,0:T(8,128)(2,1)S(1)}, u32[]{:S(2)}, u32[]{:S(2)}) collective-permute-start(bf16[32,2048]{1,0:T(8,128)(2,1)S(1)} %get-tuple-element.54), channel_id=1, source_target_pairs={{0,8},{2,10},{4,12},{6,14},{8,0},{10,2},{12,4},{14,6},{1,9},{3,11}... | collective-permute-start | bytes 393224 | tf_op jit(solution)/shard_map/ppermute | solution.py:301
  100.6 2.3 %collective-permute-done.19 = bf16[32,2048]{1,0:T(8,128)(2,1)S(1)} collective-permute-done((bf16[32,2048]{1,0:T(8,128)(2,1)S(1)}, bf16[32,2048]{1,0:T(8,128)(2,1)S(1)}, u32[]{:S(2)}, u32[]{:S(2)}) %collective-permute-start.19) | collective-permute-done | bytes 131104 | tf_op jit(solution)/shard_map/ppermute | solution.py:301
  102.8 3.4 %collective-permute-done.20 = bf16[32,2048]{1,0:T(8,128)(2,1)S(1)} collective-permute-done((bf16[32,2048]{1,0:T(8,128)(2,1)S(1)}, bf16[32,2048]{1,0:T(8,128)(2,1)S(1)}, u32[]{:S(2)}, u32[]{:S(2)}) %collective-permute-start.20) | collective-permute-done | bytes 131104 | tf_op jit(solution)/shard_map/ppermute | solution.py:301
  106.2 6.2 %collective-permute-done.27 = bf16[32,2048]{1,0:T(8,128)(2,1)S(1)} collective-permute-done((bf16[32,2048]{1,0:T(8,128)(2,1)S(1)}, bf16[32,2048]{1,0:T(8,128)(2,1)S(1)}, u32[]{:S(2)}, u32[]{:S(2)}) %collective-permute-start.27) | collective-permute-done | bytes 131104 | tf_op jit(solution)/shard_map/ppermute | solution.py:301
  112.5 0.7 add_convert_fusion
  (38 shorter events, 0.4 us)
Async XLA Ops:
  0.1 0.7 copy-start.2
  0.8 0.7 copy-start.6
  1.5 28.3 %copy-start = (bf16[2048,512]{1,0:T(8,128)(2,1)S(1)}, bf16[2048,512]{1,0:T(8,128)(2,1)}, u32[]{:S(2)}) copy-start(bf16[2048,512]{1,0:T(8,128)(2,1)} %refs_8_.1) | copy-start | bytes 6291460
  1.5 40.5 %copy-start.1 = (bf16[2,16,2048]{2,1,0:T(8,128)(2,1)S(1)}, bf16[2,16,2048]{2,1,0:T(8,128)(2,1)}, u32[]{:S(2)}) copy-start(bf16[2,16,2048]{2,1,0:T(8,128)(2,1)} %param.17) | copy-start | bytes 393220
  1.5 40.5 %copy-start.3 = (f32[2048]{0:T(1024)S(1)}, f32[2048]{0:T(1024)}, u32[]{:S(2)}) copy-start(f32[2048]{0:T(1024)} %param.19) | copy-start | bytes 24580
  1.5 40.5 %copy-start.4 = (s32[2,16,8]{1,2,0:T(8,128)S(1)}, s32[2,16,8]{1,2,0:T(8,128)}, u32[]{:S(2)}) copy-start(s32[2,16,8]{1,2,0:T(8,128)} %param.20) | copy-start | bytes 3076
  1.5 40.5 %copy-start.5 = (f32[2,16,8]{1,2,0:T(8,128)S(1)}, f32[2,16,8]{1,2,0:T(8,128)}, u32[]{:S(2)}) copy-start(f32[2,16,8]{1,2,0:T(8,128)} %param.21) | copy-start | bytes 3076
  11.7 6.7 %collective-permute-start = (bf16[32,2048]{1,0:T(8,128)(2,1)S(1)}, bf16[32,2048]{1,0:T(8,128)(2,1)S(1)}, u32[]{:S(2)}, u32[]{:S(2)}) collective-permute-start(bf16[32,2048]{1,0:T(8,128)(2,1)S(1)} %get-tuple-element.30.refs_0_), channel_id=1, source_target_pairs={{0,4},{2,6},{4,0},{6,2},{8,12},{10,14},{12,8},{14,10},{1,5},{3,7},... | collective-permute-start | bytes 393224 | tf_op jit(solution)/shard_map/ppermute | solution.py:301
  15.4 12.9 %collective-permute-start.1 = (bf16[32,2048]{1,0:T(8,128)(2,1)S(1)}, bf16[32,2048]{1,0:T(8,128)(2,1)S(1)}, u32[]{:S(2)}, u32[]{:S(2)}) collective-permute-start(bf16[32,2048]{1,0:T(8,128)(2,1)S(1)} %get-tuple-element.30.refs_0_), channel_id=1, source_target_pairs={{0,8},{2,10},{4,12},{6,14},{8,0},{10,2},{12,4},{14,6},{1,9},{3,11}... | collective-permute-start | bytes 393224 | tf_op jit(solution)/shard_map/ppermute | solution.py:301
  17.8 10.5 %collective-permute-start.2 = (bf16[32,2048]{1,0:T(8,128)(2,1)S(1)}, bf16[32,2048]{1,0:T(8,128)(2,1)S(1)}, u32[]{:S(2)}, u32[]{:S(2)}) collective-permute-start(bf16[32,2048]{1,0:T(8,128)(2,1)S(1)} %get-tuple-element.30.refs_0_), channel_id=1, source_target_pairs={{0,12},{2,14},{4,8},{6,10},{8,4},{10,6},{12,0},{14,2},{1,13},{3,15... | collective-permute-start | bytes 393224 | tf_op jit(solution)/shard_map/ppermute | solution.py:301
  18.3 10.5 %collective-permute-start.3 = (bf16[32,2048]{1,0:T(8,128)(2,1)S(1)}, bf16[32,2048]{1,0:T(8,128)(2,1)S(1)}, u32[]{:S(2)}, u32[]{:S(2)}) collective-permute-start(bf16[32,2048]{1,0:T(8,128)(2,1)S(1)} %get-tuple-element.30.refs_0_), channel_id=1, source_target_pairs={{0,2},{2,0},{4,6},{6,4},{8,10},{10,8},{12,14},{14,12},{1,3},{3,1},... | collective-permute-start | bytes 393224 | tf_op jit(solution)/shard_map/ppermute | solution.py:301
  18.3 10.5 %collective-permute-start.4 = (bf16[32,2048]{1,0:T(8,128)(2,1)S(1)}, bf16[32,2048]{1,0:T(8,128)(2,1)S(1)}, u32[]{:S(2)}, u32[]{:S(2)}) collective-permute-start(bf16[32,2048]{1,0:T(8,128)(2,1)S(1)} %collective-permute-done.refs_1_), channel_id=1, source_target_pairs={{0,2},{2,0},{4,6},{6,4},{8,10},{10,8},{12,14},{14,12},{1,3},{3,1},... | collective-permute-start | bytes 393224 | tf_op jit(solution)/shard_map/ppermute | solution.py:301
  28.3 1.3 %collective-permute-start.5 = (bf16[32,2048]{1,0:T(8,128)(2,1)S(1)}, bf16[32,2048]{1,0:T(8,128)(2,1)S(1)}, u32[]{:S(2)}, u32[]{:S(2)}) collective-permute-start(bf16[32,2048]{1,0:T(8,128)(2,1)S(1)} %collective-permute-done.1.refs_2_), channel_id=1, source_target_pairs={{0,2},{2,0},{4,6},{6,4},{8,10},{10,8},{12,14},{14,12},{1,3},{3,1},... | collective-permute-start | bytes 393224 | tf_op jit(solution)/shard_map/ppermute | solution.py:301
  28.3 1.5 %collective-permute-start.6 = (bf16[32,2048]{1,0:T(8,128)(2,1)S(1)}, bf16[32,2048]{1,0:T(8,128)(2,1)S(1)}, u32[]{:S(2)}, u32[]{:S(2)}) collective-permute-start(bf16[32,2048]{1,0:T(8,128)(2,1)S(1)} %collective-permute-done.2.refs_3_), channel_id=1, source_target_pairs={{0,2},{2,0},{4,6},{6,4},{8,10},{10,8},{12,14},{14,12},{1,3},{3,1},... | collective-permute-start | bytes 393224 | tf_op jit(solution)/shard_map/ppermute | solution.py:301
  31.1 1.4 %collective-permute-start.7 = (bf16[4,32,512]{2,1,0:T(8,128)(2,1)S(1)}, bf16[4,32,512]{2,1,0:T(8,128)(2,1)S(1)}, u32[]{:S(2)}, u32[]{:S(2)}) collective-permute-start(bf16[4,32,512]{2,1,0:T(8,128)(2,1)S(1)} %get-tuple-element.32), channel_id=1, source_target_pairs={{0,2},{2,0},{4,6},{6,4},{8,10},{10,8},{12,14},{14,12},{1,3},{3,1},... | collective-permute-start | bytes 393224 | tf_op jit(solution)/shard_map/ppermute | solution.py:301
  32.5 6.2 %collective-permute-start.10 = (bf16[32,1024]{1,0:T(8,128)(2,1)S(1)}, bf16[32,1024]{1,0:T(8,128)(2,1)S(1)}, u32[]{:S(2)}, u32[]{:S(2)}) collective-permute-start(bf16[32,1024]{1,0:T(8,128)(2,1)S(1)} %get-tuple-element.35), channel_id=1, source_target_pairs={{0,8},{1,0},{2,10},{3,2},{4,12},{5,4},{6,14},{7,6},{8,9},{9,1},{10... | collective-permute-start | bytes 196616 | tf_op jit(solution)/shard_map/ppermute | solution.py:658
  35.7 6.2 %collective-permute-start.11 = (bf16[32,1024]{1,0:T(8,128)(2,1)S(1)}, bf16[32,1024]{1,0:T(8,128)(2,1)S(1)}, u32[]{:S(2)}, u32[]{:S(2)}) collective-permute-start(bf16[32,1024]{1,0:T(8,128)(2,1)S(1)} %get-tuple-element.36), channel_id=1, source_target_pairs={{0,12},{1,4},{2,14},{3,6},{4,8},{5,0},{6,10},{7,2},{8,13},{9,5},{1... | collective-permute-start | bytes 196616 | tf_op jit(solution)/shard_map/ppermute | solution.py:658
  36.6 5.3 %collective-permute-start.8 = (bf16[32,1024]{1,0:T(8,128)(2,1)S(1)}, bf16[32,1024]{1,0:T(8,128)(2,1)S(1)}, u32[]{:S(2)}, u32[]{:S(2)}) collective-permute-start(bf16[32,1024]{1,0:T(8,128)(2,1)S(1)} %get-tuple-element.33), channel_id=1, source_target_pairs={{0,0},{1,8},{2,2},{3,10},{4,4},{5,12},{6,6},{7,14},{8,1},{9,9},{10... | collective-permute-start | bytes 196616 | tf_op jit(solution)/shard_map/ppermute | solution.py:658
  37.5 4.5 %collective-permute-start.9 = (bf16[32,1024]{1,0:T(8,128)(2,1)S(1)}, bf16[32,1024]{1,0:T(8,128)(2,1)S(1)}, u32[]{:S(2)}, u32[]{:S(2)}) collective-permute-start(bf16[32,1024]{1,0:T(8,128)(2,1)S(1)} %get-tuple-element.34), channel_id=1, source_target_pairs={{0,4},{1,12},{2,6},{3,14},{4,0},{5,8},{6,2},{7,10},{8,5},{9,13},{1... | collective-permute-start | bytes 196616 | tf_op jit(solution)/shard_map/ppermute | solution.py:658
  42.8 8.9 %collective-permute-start.12 = (bf16[32,2176]{1,0:T(8,128)(2,1)S(1)}, bf16[32,2176]{1,0:T(8,128)(2,1)S(1)}, u32[]{:S(2)}, u32[]{:S(2)}) collective-permute-start(bf16[32,2176]{1,0:T(8,128)(2,1)S(1)} %get-tuple-element.38.refs_0_), channel_id=1, source_target_pairs={{0,4},{2,6},{4,0},{6,2},{8,12},{10,14},{12,8},{14,10},{1,5},{3,7},... | collective-permute-start | bytes 417800 | tf_op jit(solution)/shard_map/ppermute | solution.py:301
  43.8 14.7 %collective-permute-start.13 = (bf16[32,2176]{1,0:T(8,128)(2,1)S(1)}, bf16[32,2176]{1,0:T(8,128)(2,1)S(1)}, u32[]{:S(2)}, u32[]{:S(2)}) collective-permute-start(bf16[32,2176]{1,0:T(8,128)(2,1)S(1)} %get-tuple-element.38.refs_0_), channel_id=1, source_target_pairs={{0,12},{2,14},{4,8},{6,10},{8,4},{10,6},{12,0},{14,2},{1,13},{3,15... | collective-permute-start | bytes 417800 | tf_op jit(solution)/shard_map/ppermute | solution.py:301
  51.6 11.2 %collective-permute-start.21 = (bf16[32,2176]{1,0:T(8,128)(2,1)S(1)}, bf16[32,2176]{1,0:T(8,128)(2,1)S(1)}, u32[]{:S(2)}, u32[]{:S(2)}) collective-permute-start(bf16[32,2176]{1,0:T(8,128)(2,1)S(1)} %get-tuple-element.38.refs_0_), channel_id=1, source_target_pairs={{0,8},{2,10},{4,12},{6,14},{8,0},{10,2},{12,4},{14,6},{1,9},{3,11}... | collective-permute-start | bytes 417800 | tf_op jit(solution)/shard_map/ppermute | solution.py:301
  51.6 11.3 %collective-permute-start.14 = (bf16[32,2176]{1,0:T(8,128)(2,1)S(1)}, bf16[32,2176]{1,0:T(8,128)(2,1)S(1)}, u32[]{:S(2)}, u32[]{:S(2)}) collective-permute-start(bf16[32,2176]{1,0:T(8,128)(2,1)S(1)} %shard_map.121.refs_0_), channel_id=1, source_target_pairs={{0,2},{2,0},{4,6},{6,4},{8,10},{10,8},{12,14},{14,12},{1,3},{3,1},... | collective-permute-start | bytes 417800 | tf_op jit(solution)/shard_map/ppermute | solution.py:301
  58.5 4.5 %collective-permute-start.15 = (bf16[32,2176]{1,0:T(8,128)(2,1)S(1)}, bf16[32,2176]{1,0:T(8,128)(2,1)S(1)}, u32[]{:S(2)}, u32[]{:S(2)}) collective-permute-start(bf16[32,2176]{1,0:T(8,128)(2,1)S(1)} %collective-permute-done.13.refs_1_), channel_id=1, source_target_pairs={{0,2},{2,0},{4,6},{6,4},{8,10},{10,8},{12,14},{14,12},{1,3},{3,1},... | collective-permute-start | bytes 417800 | tf_op jit(solution)/shard_map/ppermute | solution.py:301
  58.5 8.1 %collective-permute-start.22 = (bf16[32,2176]{1,0:T(8,128)(2,1)S(1)}, bf16[32,2176]{1,0:T(8,128)(2,1)S(1)}, u32[]{:S(2)}, u32[]{:S(2)}) collective-permute-start(bf16[32,2176]{1,0:T(8,128)(2,1)S(1)} %get-tuple-element.38.refs_0_), channel_id=1, source_target_pairs={{0,2},{2,0},{4,6},{6,4},{8,10},{10,8},{12,14},{14,12},{1,3},{3,1},... | collective-permute-start | bytes 417800 | tf_op jit(solution)/shard_map/ppermute | solution.py:301
  62.9 3.7 %collective-permute-start.23 = (bf16[32,2176]{1,0:T(8,128)(2,1)S(1)}, bf16[32,2176]{1,0:T(8,128)(2,1)S(1)}, u32[]{:S(2)}, u32[]{:S(2)}) collective-permute-start(bf16[32,2176]{1,0:T(8,128)(2,1)S(1)} %shard_map.126.refs_1_), channel_id=1, source_target_pairs={{0,2},{2,0},{4,6},{6,4},{8,10},{10,8},{12,14},{14,12},{1,3},{3,1},... | collective-permute-start | bytes 417800 | tf_op jit(solution)/shard_map/ppermute | solution.py:301
  65.4 12.8 %collective-permute-start.16 = (bf16[128,1664]{1,0:T(8,128)(2,1)S(1)}, bf16[128,1664]{1,0:T(8,128)(2,1)S(1)}, u32[]{:S(2)}, u32[]{:S(2)}) collective-permute-start(bf16[128,1664]{1,0:T(8,128)(2,1)S(1)} %get-tuple-element.41), channel_id=1, source_target_pairs={{0,1},{1,0},{2,3},{3,2},{4,5},{5,4},{6,7},{7,6},{8,9},{9,8},{10,11... | collective-permute-start | bytes 1277960 | tf_op jit(solution)/shard_map/ppermute | solution.py:301
  69.0 18.3 %collective-permute-start.24 = (bf16[128,1664]{1,0:T(8,128)(2,1)S(1)}, bf16[128,1664]{1,0:T(8,128)(2,1)S(1)}, u32[]{:S(2)}, u32[]{:S(2)}) collective-permute-start(bf16[128,1664]{1,0:T(8,128)(2,1)S(1)} %get-tuple-element.49), channel_id=1, source_target_pairs={{0,1},{1,0},{2,3},{3,2},{4,5},{5,4},{6,7},{7,6},{8,9},{9,8},{10,11... | collective-permute-start | bytes 1277960 | tf_op jit(solution)/shard_map/ppermute | solution.py:301
  78.9 12.5 %collective-permute-start.17 = (bf16[128,768]{1,0:T(8,128)(2,1)S(1)}, bf16[128,768]{1,0:T(8,128)(2,1)S(1)}, u32[]{:S(2)}, u32[]{:S(2)}) collective-permute-start(bf16[128,768]{1,0:T(8,128)(2,1)S(1)} %shard_map.123.act_ref), channel_id=1, source_target_pairs={{0,1},{1,0},{2,3},{3,2},{4,5},{5,4},{6,7},{7,6},{8,9},{9,8},{10,11... | collective-permute-start | bytes 589832 | tf_op jit(solution)/shard_map/ppermute | solution.py:301
  88.1 7.1 %collective-permute-start.25 = (bf16[128,768]{1,0:T(8,128)(2,1)S(1)}, bf16[128,768]{1,0:T(8,128)(2,1)S(1)}, u32[]{:S(2)}, u32[]{:S(2)}) collective-permute-start(bf16[128,768]{1,0:T(8,128)(2,1)S(1)} %shard_map.128.act_ref), channel_id=1, source_target_pairs={{0,1},{1,0},{2,3},{3,2},{4,5},{5,4},{6,7},{7,6},{8,9},{9,8},{10,11... | collective-permute-start | bytes 589832 | tf_op jit(solution)/shard_map/ppermute | solution.py:301
  93.0 3.8 %collective-permute-start.18 = (bf16[64,2048]{1,0:T(8,128)(2,1)S(1)}, bf16[64,2048]{1,0:T(8,128)(2,1)S(1)}, u32[]{:S(2)}, u32[]{:S(2)}) collective-permute-start(bf16[64,2048]{1,0:T(8,128)(2,1)S(1)} %get-tuple-element.45), channel_id=1, source_target_pairs={{0,2},{2,0},{4,6},{6,4},{8,10},{10,8},{12,14},{14,12},{1,3},{3,1},... | collective-permute-start | bytes 786440 | tf_op jit(solution)/shard_map/ppermute | solution.py:301
  96.8 2.3 %collective-permute-start.26 = (bf16[64,2048]{1,0:T(8,128)(2,1)S(1)}, bf16[64,2048]{1,0:T(8,128)(2,1)S(1)}, u32[]{:S(2)}, u32[]{:S(2)}) collective-permute-start(bf16[64,2048]{1,0:T(8,128)(2,1)S(1)} %get-tuple-element.52), channel_id=1, source_target_pairs={{0,2},{2,0},{4,6},{6,4},{8,10},{10,8},{12,14},{14,12},{1,3},{3,1},... | collective-permute-start | bytes 786440 | tf_op jit(solution)/shard_map/ppermute | solution.py:301
  96.9 6.0 %collective-permute-start.19 = (bf16[32,2048]{1,0:T(8,128)(2,1)S(1)}, bf16[32,2048]{1,0:T(8,128)(2,1)S(1)}, u32[]{:S(2)}, u32[]{:S(2)}) collective-permute-start(bf16[32,2048]{1,0:T(8,128)(2,1)S(1)} %get-tuple-element.46), channel_id=1, source_target_pairs={{0,4},{2,6},{4,0},{6,2},{8,12},{10,14},{12,8},{14,10},{1,5},{3,7},... | collective-permute-start | bytes 393224 | tf_op jit(solution)/shard_map/ppermute | solution.py:301
  97.0 9.2 %collective-permute-start.20 = (bf16[32,2048]{1,0:T(8,128)(2,1)S(1)}, bf16[32,2048]{1,0:T(8,128)(2,1)S(1)}, u32[]{:S(2)}, u32[]{:S(2)}) collective-permute-start(bf16[32,2048]{1,0:T(8,128)(2,1)S(1)} %get-tuple-element.47), channel_id=1, source_target_pairs={{0,12},{2,14},{4,8},{6,10},{8,4},{10,6},{12,0},{14,2},{1,13},{3,15... | collective-permute-start | bytes 393224 | tf_op jit(solution)/shard_map/ppermute | solution.py:301
  99.1 13.4 %collective-permute-start.27 = (bf16[32,2048]{1,0:T(8,128)(2,1)S(1)}, bf16[32,2048]{1,0:T(8,128)(2,1)S(1)}, u32[]{:S(2)}, u32[]{:S(2)}) collective-permute-start(bf16[32,2048]{1,0:T(8,128)(2,1)S(1)} %get-tuple-element.54), channel_id=1, source_target_pairs={{0,8},{2,10},{4,12},{6,14},{8,0},{10,2},{12,4},{14,6},{1,9},{3,11}... | collective-permute-start | bytes 393224 | tf_op jit(solution)/shard_map/ppermute | solution.py:301

commit v5 on v4

--- a/solution.py
+++ b/solution.py
@@ -82,8 +82,8 @@
 
 
 def attend_kernel(
-    req_count, group, page_len, blocks, index_ref, table_ref, length_ref, q_hbm, fresh_hbm, kv_hbm, gate_up_hbm, down_hbm,
-    out_ref, gate_up_ref, down_ref, q_ref, kbuf, vbuf, fkbuf, fvbuf, s_ref, acc_ref, l_ref, m_ref, code_ref, ksem, vsem, fsem, wsem,
+    req_count, group, page_len, blocks, index_ref, table_hbm, q_hbm, fresh_hbm, kv_hbm, gate_up_hbm, down_hbm,
+    out_ref, gate_up_ref, down_ref, q_ref, kbuf, vbuf, fkbuf, fvbuf, s_ref, acc_ref, l_ref, m_ref, code_ref, table_ref, ksem, vsem, fsem, wsem,
 ):
     f32, bf16 = jnp.float32, jnp.bfloat16
     width = q_ref.shape[2]
@@ -103,6 +103,8 @@
         for h, buf in enumerate((fkbuf, fvbuf))
     ]
     fresh_copies.append(pltpu.make_async_copy(q_hbm, q_ref, fsem.at[2]))
+    table_copy = pltpu.make_async_copy(table_hbm, table_ref, fsem.at[3])
+    table_copy.start()
     for copy in fresh_copies:
         copy.start()
     lax.fori_loop(0, blocks, lambda b, c: (fetch(0, kbuf, ksem, b).start(), c)[1], 0)
@@ -119,8 +121,9 @@
         return c
 
     lax.fori_loop(0, blocks * pages, clear, 0, unroll=16)
+    table_copy.wait()
     for r in range(req_count):
-        length = length_ref[r]
+        length = index_ref[2 + r]
 
         def put(j, c, r=r, length=length):
             code_ref[table_ref[r, j]] = r * 32 + jnp.minimum(length - j * page_len, page_len)
@@ -242,7 +245,7 @@
         copy.wait()
 
 
-def attend_pool(index, queries, fresh_kv, kv_pool, page_table, context_lengths, gate_up, down_proj):
+def attend_pool(index, queries, fresh_kv, kv_pool, page_table, gate_up, down_proj):
     step_count, req_count, head_count, head_width = queries.shape
     pool_pages, page_len, kv_heads, _ = kv_pool.shape
     group = head_count // kv_heads
@@ -259,7 +262,7 @@
             pltpu.VMEM(gate_up.shape, bf16),
             pltpu.VMEM(down_proj.shape, bf16),
         ),
-        in_specs=[pl.BlockSpec(memory_space=pltpu.SMEM)] * 3 + [hbm] * 5,
+        in_specs=[pl.BlockSpec(memory_space=pltpu.SMEM)] + [hbm] * 6,
         out_specs=(vmem, vmem, vmem),
         scratch_shapes=[
             pltpu.VMEM((own, head_count, head_width), bf16),
@@ -272,20 +275,20 @@
             pltpu.VMEM((rows, head_width), f32),
             pltpu.VMEM((rows, head_width), f32),
             pltpu.SMEM((pool_pages,), jnp.int32),
+            pltpu.SMEM(page_table.shape, jnp.int32),
             pltpu.SemaphoreType.DMA((blocks,)),
             pltpu.SemaphoreType.DMA((blocks,)),
-            pltpu.SemaphoreType.DMA((3,)),
+            pltpu.SemaphoreType.DMA((4,)),
             pltpu.SemaphoreType.DMA((2,)),
         ],
         compiler_params=pltpu.CompilerParams(vmem_limit_bytes=24 * 1024 * 1024),
         name="attend_pool",
     )(
         index,
-        page_table,
-        context_lengths,
         *[
             pltpu.with_memory_space_constraint(value, pltpu.HBM)
             for value in (
+                page_table,
                 queries.reshape(own, head_count, head_width),
                 fresh_kv.reshape(own, kv_heads, 2 * head_width),
                 kv_pool.reshape(tokens, kv_heads, 2 * head_width),
@@ -619,7 +622,7 @@
     bf16, f32 = jnp.bfloat16, jnp.float32
     dp_count, x_count = lax.axis_size("dp"), lax.axis_size("expert")
     dp_index, x_index = lax.axis_index("dp"), lax.axis_index("expert")
-    index = jnp.stack([dp_index, x_index]).astype(jnp.int32)
+    index = jnp.concatenate([jnp.stack([dp_index, x_index]).astype(jnp.int32), context_lengths])
     chips = dp_count // 2
     local_experts, _, width, hidden = gate_up.shape
     part = hidden // 2
@@ -628,7 +631,7 @@
     own = steps * reqs
 
     attended, gate_up, down_proj = attend_pool(
-        index, queries, fresh_kv, kv_pool, page_table, context_lengths, gate_up, down_proj
+        index, queries, fresh_kv, kv_pool, page_table, gate_up, down_proj
     )
     head_cols = attended.shape[1]
     mine = [attended] + [exchange(attended, "dp", 2 * k) for k in range(1, chips)]

time: 113 us -> 113 us (level)
  local copies, waits for them, and re-layouts: 1.41 us -> 0.02 us
    unnamed x14 -> x10, local copies, waits for them, and re-layouts: 1.41 us -> 0.02 us
where the time goes in v5:
time: 113 us
  waiting for transfers between devices  56.9 us (50%)
  starting transfers between devices  32.1 us (28%)
  Pallas kernels  22.3 us (20%)
  other arithmetic  1.46 us (1%)
    ppermute x24, waiting for transfers between devices, exchange(): return lax.ppermute(value, axis, [(i, i ^ mask) for i in range(count)])  53.6 us
    ppermute x24, starting transfers between devices, exchange(): return lax.ppermute(value, axis, [(i, i ^ mask) for i in range(count)])  25.9 us
    pallas_call x13, Pallas kernels, small_call(): pl.pallas_call(kernel, out_shape=tuple((jax.ShapeDtypeStruct(shape, dtype...  11.7 us
    pallas_call x1, Pallas kernels, attend_pool(): pl.pallas_call(functools.partial(attend_kernel, req_count, group, page_le...  10.6 us
    ppermute x4, starting transfers between devices, body_fast(): arrived.append(lax.ppermute(paired[k], ('dp', 'expert'), moves))  6.16 us
    ppermute x4, waiting for transfers between devices, body_fast(): arrived.append(lax.ppermute(paired[k], ('dp', 'expert'), moves))  3.27 us
  transfers between devices with their start and end apart: 28, of which 14 were waited for; matrix products, arithmetic and copies ran while one was open for 0% of the time, Pallas kernels for 9%

profile of v5, /device:TPU:0, one launch (start us, length us, event | category | flops | bytes accessed | tf_op | source)
XLA Modules:
  0.0 112.9 jit_solution(6284037016644226697)
XLA Ops:
  0.0 0.7 pad_add_fusion.index_ref
  0.8 10.6 %attend_pool.1 = (bf16[32,2048]{1,0:T(8,128)(2,1)S(1)}, bf16[2,2,2048,768]{3,2,1,0:T(8,128)(2,1)S(1)}, bf16[2,768,2048]{2,1,0:T(8,128)(2,1)S(1)}) custom-call(s32[18]{0:T(128)S(1)} %pad_add_fusion.index_ref, s32[16,305]{1,0:T(8,128)} %table_hbm.1, bf16[32,16,128]{2,1,0:T(8,128)(2,1)} %bitcast.15, bf16[32,2,256]{2,1,0:T(2,128)(2,1)} %bitcast.16, ...), custom_call_target="tpu_custom_call" | custom-call | tf_op jit(solution)/shard_map/attend_pool/pallas_call | solution.py:258
  11.4 3.7 %collective-permute-start = (bf16[32,2048]{1,0:T(8,128)(2,1)S(1)}, bf16[32,2048]{1,0:T(8,128)(2,1)S(1)}, u32[]{:S(2)}, u32[]{:S(2)}) collective-permute-start(bf16[32,2048]{1,0:T(8,128)(2,1)S(1)} %get-tuple-element.30.refs_0_), channel_id=1, source_target_pairs={{0,4},{2,6},{4,0},{6,2},{8,12},{10,14},{12,8},{14,10},{1,5},{3,7},... | collective-permute-start | bytes 393224 | tf_op jit(solution)/shard_map/ppermute | solution.py:304
  15.1 2.4 %collective-permute-start.1 = (bf16[32,2048]{1,0:T(8,128)(2,1)S(1)}, bf16[32,2048]{1,0:T(8,128)(2,1)S(1)}, u32[]{:S(2)}, u32[]{:S(2)}) collective-permute-start(bf16[32,2048]{1,0:T(8,128)(2,1)S(1)} %get-tuple-element.30.refs_0_), channel_id=1, source_target_pairs={{0,8},{2,10},{4,12},{6,14},{8,0},{10,2},{12,4},{14,6},{1,9},{3,11}... | collective-permute-start | bytes 393224 | tf_op jit(solution)/shard_map/ppermute | solution.py:304
  17.5 0.6 collective-permute-start.2
  18.0 0.5 collective-permute-start.4
  18.5 9.4 %collective-permute-done.1.refs_2_ = bf16[32,2048]{1,0:T(8,128)(2,1)S(1)} collective-permute-done((bf16[32,2048]{1,0:T(8,128)(2,1)S(1)}, bf16[32,2048]{1,0:T(8,128)(2,1)S(1)}, u32[]{:S(2)}, u32[]{:S(2)}) %collective-permute-start.1) | collective-permute-done | bytes 131104 | tf_op jit(solution)/shard_map/ppermute | solution.py:304
  28.0 0.5 collective-permute-start.6
  28.5 0.8 collective-permute-done.5.refs_6_
  29.3 0.2 collective-permute-done.6.refs_7_
  29.5 1.2 %shard_map.118 = (bf16[4,32,512]{2,1,0:T(8,128)(2,1)S(1)}, bf16[4,32,512]{2,1,0:T(8,128)(2,1)S(1)}) custom-call(s32[18]{0:T(128)S(1)} %pad_add_fusion.index_ref, bf16[32,2048]{1,0:T(8,128)(2,1)S(1)} %get-tuple-element.30.refs_0_, bf16[32,2048]{1,0:T(8,128)(2,1)S(1)} %collective-permute-done.refs_1_, bf16[32,2048]{1,0:T(8,128)(2,1)S(1)} %collective-permute-done.1.refs_2_, ...), custom_call_target="tpu_custom_call" | custom-call | flops 536870912 | tf_op jit(solution)/shard_map/pallas_call | solution.py:470
  30.8 0.4 collective-permute-start.7
  31.2 1.0 collective-permute-done.7.got_ref
  32.2 3.2 %collective-permute-start.10 = (bf16[32,1024]{1,0:T(8,128)(2,1)S(1)}, bf16[32,1024]{1,0:T(8,128)(2,1)S(1)}, u32[]{:S(2)}, u32[]{:S(2)}) collective-permute-start(bf16[32,1024]{1,0:T(8,128)(2,1)S(1)} %get-tuple-element.35), channel_id=1, source_target_pairs={{0,8},{1,0},{2,10},{3,2},{4,12},{5,4},{6,14},{7,6},{8,9},{9,1},{10... | collective-permute-start | bytes 196616 | tf_op jit(solution)/shard_map/ppermute | solution.py:661
  35.4 0.9 collective-permute-start.11
  36.3 0.8 collective-permute-start.8
  37.2 1.2 %collective-permute-start.9 = (bf16[32,1024]{1,0:T(8,128)(2,1)S(1)}, bf16[32,1024]{1,0:T(8,128)(2,1)S(1)}, u32[]{:S(2)}, u32[]{:S(2)}) collective-permute-start(bf16[32,1024]{1,0:T(8,128)(2,1)S(1)} %get-tuple-element.34), channel_id=1, source_target_pairs={{0,4},{1,12},{2,6},{3,14},{4,0},{5,8},{6,2},{7,10},{8,5},{9,13},{1... | collective-permute-start | bytes 196616 | tf_op jit(solution)/shard_map/ppermute | solution.py:661
  38.4 3.3 %collective-permute-done.11.refs_3_ = bf16[32,1024]{1,0:T(8,128)(2,1)S(1)} collective-permute-done((bf16[32,1024]{1,0:T(8,128)(2,1)S(1)}, bf16[32,1024]{1,0:T(8,128)(2,1)S(1)}, u32[]{:S(2)}, u32[]{:S(2)}) %collective-permute-start.11) | collective-permute-done | bytes 65568 | tf_op jit(solution)/shard_map/ppermute | solution.py:661
  41.7 0.7 shard_map.120
  42.4 1.0 collective-permute-start.12
  43.5 7.8 %collective-permute-start.13 = (bf16[32,2176]{1,0:T(8,128)(2,1)S(1)}, bf16[32,2176]{1,0:T(8,128)(2,1)S(1)}, u32[]{:S(2)}, u32[]{:S(2)}) collective-permute-start(bf16[32,2176]{1,0:T(8,128)(2,1)S(1)} %get-tuple-element.38.refs_0_), channel_id=1, source_target_pairs={{0,12},{2,14},{4,8},{6,10},{8,4},{10,6},{12,0},{14,2},{1,13},{3,15... | collective-permute-start | bytes 417800 | tf_op jit(solution)/shard_map/ppermute | solution.py:304
  51.3 0.1 collective-permute-start.14
  51.4 6.7 %collective-permute-done.13.refs_1_ = bf16[32,2176]{1,0:T(8,128)(2,1)S(1)} collective-permute-done((bf16[32,2176]{1,0:T(8,128)(2,1)S(1)}, bf16[32,2176]{1,0:T(8,128)(2,1)S(1)}, u32[]{:S(2)}, u32[]{:S(2)}) %collective-permute-start.13) | collective-permute-done | bytes 139296 | tf_op jit(solution)/shard_map/ppermute | solution.py:304
  58.2 0.5 collective-permute-start.22
  58.7 3.9 %collective-permute-done.21.piece_ref = bf16[32,2176]{1,0:T(8,128)(2,1)S(1)} collective-permute-done((bf16[32,2176]{1,0:T(8,128)(2,1)S(1)}, bf16[32,2176]{1,0:T(8,128)(2,1)S(1)}, u32[]{:S(2)}, u32[]{:S(2)}) %collective-permute-start.21) | collective-permute-done | bytes 139296 | tf_op jit(solution)/shard_map/ppermute | solution.py:304
  62.6 0.1 collective-permute-start.23
  62.7 2.4 %shard_map.122 = (f32[4,128,384]{2,1,0:T(8,128)S(1)}, bf16[128,1664]{1,0:T(8,128)(2,1)S(1)}, bf16[128,128]{1,0:T(8,128)(2,1)S(1)}) custom-call(s32[18]{0:T(128)S(1)} %pad_add_fusion.index_ref, bf16[32,2176]{1,0:T(8,128)(2,1)S(1)} %shard_map.121.refs_0_, bf16[32,2176]{1,0:T(8,128)(2,1)S(1)} %collective-permute-done.13.refs_1_, ...), custom_call_target="tpu_custom_call" | custom-call | flops 1610612736 | tf_op jit(solution)/shard_map/pallas_call | solution.py:470
  65.1 1.2 %collective-permute-start.16 = (bf16[128,1664]{1,0:T(8,128)(2,1)S(1)}, bf16[128,1664]{1,0:T(8,128)(2,1)S(1)}, u32[]{:S(2)}, u32[]{:S(2)}) collective-permute-start(bf16[128,1664]{1,0:T(8,128)(2,1)S(1)} %get-tuple-element.41), channel_id=1, source_target_pairs={{0,1},{1,0},{2,3},{3,2},{4,5},{5,4},{6,7},{7,6},{8,9},{9,8},{10,11... | collective-permute-start | bytes 1277960 | tf_op jit(solution)/shard_map/ppermute | solution.py:304
  66.3 2.4 %shard_map.127 = (f32[4,128,384]{2,1,0:T(8,128)S(1)}, bf16[128,1664]{1,0:T(8,128)(2,1)S(1)}, bf16[128,128]{1,0:T(8,128)(2,1)S(1)}) custom-call(s32[18]{0:T(128)S(1)} %pad_add_fusion.index_ref, bf16[32,2176]{1,0:T(8,128)(2,1)S(1)} %get-tuple-element.38.refs_0_, bf16[32,2176]{1,0:T(8,128)(2,1)S(1)} %shard_map.126.refs_1_, ...), custom_call_target="tpu_custom_call" | custom-call | flops 1610612736 | tf_op jit(solution)/shard_map/pallas_call | solution.py:470
  68.7 1.0 collective-permute-start.24
  69.7 8.2 %collective-permute-done.16.got_ref = bf16[128,1664]{1,0:T(8,128)(2,1)S(1)} collective-permute-done((bf16[128,1664]{1,0:T(8,128)(2,1)S(1)}, bf16[128,1664]{1,0:T(8,128)(2,1)S(1)}, u32[]{:S(2)}, u32[]{:S(2)}) %collective-permute-start.16) | collective-permute-done | bytes 426016 | tf_op jit(solution)/shard_map/ppermute | solution.py:304
  77.8 0.8 shard_map.123.act_ref
  78.6 1.2 %collective-permute-start.17 = (bf16[128,768]{1,0:T(8,128)(2,1)S(1)}, bf16[128,768]{1,0:T(8,128)(2,1)S(1)}, u32[]{:S(2)}, u32[]{:S(2)}) collective-permute-start(bf16[128,768]{1,0:T(8,128)(2,1)S(1)} %shard_map.123.act_ref), channel_id=1, source_target_pairs={{0,1},{1,0},{2,3},{3,2},{4,5},{5,4},{6,7},{7,6},{8,9},{9,8},{10,11... | collective-permute-start | bytes 589832 | tf_op jit(solution)/shard_map/ppermute | solution.py:304
  79.8 7.1 %collective-permute-done.24.got_ref = bf16[128,1664]{1,0:T(8,128)(2,1)S(1)} collective-permute-done((bf16[128,1664]{1,0:T(8,128)(2,1)S(1)}, bf16[128,1664]{1,0:T(8,128)(2,1)S(1)}, u32[]{:S(2)}, u32[]{:S(2)}) %collective-permute-start.24) | collective-permute-done | bytes 426016 | tf_op jit(solution)/shard_map/ppermute | solution.py:304
  87.0 0.8 shard_map.128.act_ref
  87.8 1.2 %collective-permute-start.25 = (bf16[128,768]{1,0:T(8,128)(2,1)S(1)}, bf16[128,768]{1,0:T(8,128)(2,1)S(1)}, u32[]{:S(2)}, u32[]{:S(2)}) collective-permute-start(bf16[128,768]{1,0:T(8,128)(2,1)S(1)} %shard_map.128.act_ref), channel_id=1, source_target_pairs={{0,1},{1,0},{2,3},{3,2},{4,5},{5,4},{6,7},{7,6},{8,9},{9,8},{10,11... | collective-permute-start | bytes 589832 | tf_op jit(solution)/shard_map/ppermute | solution.py:304
  88.9 2.2 %collective-permute-done.17.got_ref = bf16[128,768]{1,0:T(8,128)(2,1)S(1)} collective-permute-done((bf16[128,768]{1,0:T(8,128)(2,1)S(1)}, bf16[128,768]{1,0:T(8,128)(2,1)S(1)}, u32[]{:S(2)}, u32[]{:S(2)}) %collective-permute-start.17) | collective-permute-done | bytes 196640 | tf_op jit(solution)/shard_map/ppermute | solution.py:304
  91.2 1.6 %shard_map.124 = (f32[64,2048]{1,0:T(8,128)S(1)}, bf16[64,2048]{1,0:T(8,128)(2,1)S(1)}) custom-call(s32[18]{0:T(128)S(1)} %pad_add_fusion.index_ref, bf16[128,768]{1,0:T(8,128)(2,1)S(1)} %shard_map.123.act_ref, bf16[128,768]{1,0:T(8,128)(2,1)S(1)} %collective-permute-done.17.got_ref, bf16[2,768,2048]{2,1,0:T(8,128)(2,1)S(1)} %get-tuple-element.43.weight_ref), custom_call_target="tpu_custom_call" | custom-call | flops 805306368 | tf_op jit(solution)/shard_map/pallas_call | solution.py:470
  92.8 2.1 %collective-permute-done.25.got_ref = bf16[128,768]{1,0:T(8,128)(2,1)S(1)} collective-permute-done((bf16[128,768]{1,0:T(8,128)(2,1)S(1)}, bf16[128,768]{1,0:T(8,128)(2,1)S(1)}, u32[]{:S(2)}, u32[]{:S(2)}) %collective-permute-start.25) | collective-permute-done | bytes 196640 | tf_op jit(solution)/shard_map/ppermute | solution.py:304
  94.9 1.6 %shard_map.129 = (f32[64,2048]{1,0:T(8,128)S(1)}, bf16[64,2048]{1,0:T(8,128)(2,1)S(1)}) custom-call(s32[18]{0:T(128)S(1)} %pad_add_fusion.index_ref, bf16[128,768]{1,0:T(8,128)(2,1)S(1)} %shard_map.128.act_ref, bf16[128,768]{1,0:T(8,128)(2,1)S(1)} %collective-permute-done.25.got_ref, bf16[2,768,2048]{2,1,0:T(8,128)(2,1)S(1)} %get-tuple-element.43.weight_ref), custom_call_target="tpu_custom_call" | custom-call | flops 805306368 | tf_op jit(solution)/shard_map/pallas_call | solution.py:470
  96.5 0.1 collective-permute-start.26
  96.6 0.1 collective-permute-start.19
  96.7 2.0 %collective-permute-start.20 = (bf16[32,2048]{1,0:T(8,128)(2,1)S(1)}, bf16[32,2048]{1,0:T(8,128)(2,1)S(1)}, u32[]{:S(2)}, u32[]{:S(2)}) collective-permute-start(bf16[32,2048]{1,0:T(8,128)(2,1)S(1)} %get-tuple-element.47), channel_id=1, source_target_pairs={{0,12},{2,14},{4,8},{6,10},{8,4},{10,6},{12,0},{14,2},{1,13},{3,15... | collective-permute-start | bytes 393224 | tf_op jit(solution)/shard_map/ppermute | solution.py:304
  98.8 1.5 %collective-permute-start.27 = (bf16[32,2048]{1,0:T(8,128)(2,1)S(1)}, bf16[32,2048]{1,0:T(8,128)(2,1)S(1)}, u32[]{:S(2)}, u32[]{:S(2)}) collective-permute-start(bf16[32,2048]{1,0:T(8,128)(2,1)S(1)} %get-tuple-element.54), channel_id=1, source_target_pairs={{0,8},{2,10},{4,12},{6,14},{8,0},{10,2},{12,4},{14,6},{1,9},{3,11}... | collective-permute-start | bytes 393224 | tf_op jit(solution)/shard_map/ppermute | solution.py:304
  100.3 2.3 %collective-permute-done.19 = bf16[32,2048]{1,0:T(8,128)(2,1)S(1)} collective-permute-done((bf16[32,2048]{1,0:T(8,128)(2,1)S(1)}, bf16[32,2048]{1,0:T(8,128)(2,1)S(1)}, u32[]{:S(2)}, u32[]{:S(2)}) %collective-permute-start.19) | collective-permute-done | bytes 131104 | tf_op jit(solution)/shard_map/ppermute | solution.py:304
  102.6 3.4 %collective-permute-done.20 = bf16[32,2048]{1,0:T(8,128)(2,1)S(1)} collective-permute-done((bf16[32,2048]{1,0:T(8,128)(2,1)S(1)}, bf16[32,2048]{1,0:T(8,128)(2,1)S(1)}, u32[]{:S(2)}, u32[]{:S(2)}) %collective-permute-start.20) | collective-permute-done | bytes 131104 | tf_op jit(solution)/shard_map/ppermute | solution.py:304
  105.9 6.3 %collective-permute-done.27 = bf16[32,2048]{1,0:T(8,128)(2,1)S(1)} collective-permute-done((bf16[32,2048]{1,0:T(8,128)(2,1)S(1)}, bf16[32,2048]{1,0:T(8,128)(2,1)S(1)}, u32[]{:S(2)}, u32[]{:S(2)}) %collective-permute-start.27) | collective-permute-done | bytes 131104 | tf_op jit(solution)/shard_map/ppermute | solution.py:304
  112.2 0.7 add_convert_fusion
  (34 shorter events, 0.3 us)
Async XLA Ops:
  0.7 28.8 %copy-start = (bf16[2048,512]{1,0:T(8,128)(2,1)S(1)}, bf16[2048,512]{1,0:T(8,128)(2,1)}, u32[]{:S(2)}) copy-start(bf16[2048,512]{1,0:T(8,128)(2,1)} %refs_8_.1) | copy-start | bytes 6291460
  0.7 40.9 %copy-start.1 = (bf16[2,16,2048]{2,1,0:T(8,128)(2,1)S(1)}, bf16[2,16,2048]{2,1,0:T(8,128)(2,1)}, u32[]{:S(2)}) copy-start(bf16[2,16,2048]{2,1,0:T(8,128)(2,1)} %param.17) | copy-start | bytes 393220
  0.7 40.9 %copy-start.2 = (f32[2048]{0:T(1024)S(1)}, f32[2048]{0:T(1024)}, u32[]{:S(2)}) copy-start(f32[2048]{0:T(1024)} %param.19) | copy-start | bytes 24580
  0.7 40.9 %copy-start.3 = (s32[2,16,8]{1,2,0:T(8,128)S(1)}, s32[2,16,8]{1,2,0:T(8,128)}, u32[]{:S(2)}) copy-start(s32[2,16,8]{1,2,0:T(8,128)} %param.20) | copy-start | bytes 3076
  0.7 40.9 %copy-start.4 = (f32[2,16,8]{1,2,0:T(8,128)S(1)}, f32[2,16,8]{1,2,0:T(8,128)}, u32[]{:S(2)}) copy-start(f32[2,16,8]{1,2,0:T(8,128)} %param.21) | copy-start | bytes 3076
  11.4 6.7 %collective-permute-start = (bf16[32,2048]{1,0:T(8,128)(2,1)S(1)}, bf16[32,2048]{1,0:T(8,128)(2,1)S(1)}, u32[]{:S(2)}, u32[]{:S(2)}) collective-permute-start(bf16[32,2048]{1,0:T(8,128)(2,1)S(1)} %get-tuple-element.30.refs_0_), channel_id=1, source_target_pairs={{0,4},{2,6},{4,0},{6,2},{8,12},{10,14},{12,8},{14,10},{1,5},{3,7},... | collective-permute-start | bytes 393224 | tf_op jit(solution)/shard_map/ppermute | solution.py:304
  15.1 12.9 %collective-permute-start.1 = (bf16[32,2048]{1,0:T(8,128)(2,1)S(1)}, bf16[32,2048]{1,0:T(8,128)(2,1)S(1)}, u32[]{:S(2)}, u32[]{:S(2)}) collective-permute-start(bf16[32,2048]{1,0:T(8,128)(2,1)S(1)} %get-tuple-element.30.refs_0_), channel_id=1, source_target_pairs={{0,8},{2,10},{4,12},{6,14},{8,0},{10,2},{12,4},{14,6},{1,9},{3,11}... | collective-permute-start | bytes 393224 | tf_op jit(solution)/shard_map/ppermute | solution.py:304
  17.5 10.5 %collective-permute-start.2 = (bf16[32,2048]{1,0:T(8,128)(2,1)S(1)}, bf16[32,2048]{1,0:T(8,128)(2,1)S(1)}, u32[]{:S(2)}, u32[]{:S(2)}) collective-permute-start(bf16[32,2048]{1,0:T(8,128)(2,1)S(1)} %get-tuple-element.30.refs_0_), channel_id=1, source_target_pairs={{0,12},{2,14},{4,8},{6,10},{8,4},{10,6},{12,0},{14,2},{1,13},{3,15... | collective-permute-start | bytes 393224 | tf_op jit(solution)/shard_map/ppermute | solution.py:304
  18.0 10.5 %collective-permute-start.3 = (bf16[32,2048]{1,0:T(8,128)(2,1)S(1)}, bf16[32,2048]{1,0:T(8,128)(2,1)S(1)}, u32[]{:S(2)}, u32[]{:S(2)}) collective-permute-start(bf16[32,2048]{1,0:T(8,128)(2,1)S(1)} %get-tuple-element.30.refs_0_), channel_id=1, source_target_pairs={{0,2},{2,0},{4,6},{6,4},{8,10},{10,8},{12,14},{14,12},{1,3},{3,1},... | collective-permute-start | bytes 393224 | tf_op jit(solution)/shard_map/ppermute | solution.py:304
  18.0 10.5 %collective-permute-start.4 = (bf16[32,2048]{1,0:T(8,128)(2,1)S(1)}, bf16[32,2048]{1,0:T(8,128)(2,1)S(1)}, u32[]{:S(2)}, u32[]{:S(2)}) collective-permute-start(bf16[32,2048]{1,0:T(8,128)(2,1)S(1)} %collective-permute-done.refs_1_), channel_id=1, source_target_pairs={{0,2},{2,0},{4,6},{6,4},{8,10},{10,8},{12,14},{14,12},{1,3},{3,1},... | collective-permute-start | bytes 393224 | tf_op jit(solution)/shard_map/ppermute | solution.py:304
  28.0 1.3 %collective-permute-start.5 = (bf16[32,2048]{1,0:T(8,128)(2,1)S(1)}, bf16[32,2048]{1,0:T(8,128)(2,1)S(1)}, u32[]{:S(2)}, u32[]{:S(2)}) collective-permute-start(bf16[32,2048]{1,0:T(8,128)(2,1)S(1)} %collective-permute-done.1.refs_2_), channel_id=1, source_target_pairs={{0,2},{2,0},{4,6},{6,4},{8,10},{10,8},{12,14},{14,12},{1,3},{3,1},... | collective-permute-start | bytes 393224 | tf_op jit(solution)/shard_map/ppermute | solution.py:304
  28.0 1.5 %collective-permute-start.6 = (bf16[32,2048]{1,0:T(8,128)(2,1)S(1)}, bf16[32,2048]{1,0:T(8,128)(2,1)S(1)}, u32[]{:S(2)}, u32[]{:S(2)}) collective-permute-start(bf16[32,2048]{1,0:T(8,128)(2,1)S(1)} %collective-permute-done.2.refs_3_), channel_id=1, source_target_pairs={{0,2},{2,0},{4,6},{6,4},{8,10},{10,8},{12,14},{14,12},{1,3},{3,1},... | collective-permute-start | bytes 393224 | tf_op jit(solution)/shard_map/ppermute | solution.py:304
  30.8 1.4 %collective-permute-start.7 = (bf16[4,32,512]{2,1,0:T(8,128)(2,1)S(1)}, bf16[4,32,512]{2,1,0:T(8,128)(2,1)S(1)}, u32[]{:S(2)}, u32[]{:S(2)}) collective-permute-start(bf16[4,32,512]{2,1,0:T(8,128)(2,1)S(1)} %get-tuple-element.32), channel_id=1, source_target_pairs={{0,2},{2,0},{4,6},{6,4},{8,10},{10,8},{12,14},{14,12},{1,3},{3,1},... | collective-permute-start | bytes 393224 | tf_op jit(solution)/shard_map/ppermute | solution.py:304
  32.2 6.2 %collective-permute-start.10 = (bf16[32,1024]{1,0:T(8,128)(2,1)S(1)}, bf16[32,1024]{1,0:T(8,128)(2,1)S(1)}, u32[]{:S(2)}, u32[]{:S(2)}) collective-permute-start(bf16[32,1024]{1,0:T(8,128)(2,1)S(1)} %get-tuple-element.35), channel_id=1, source_target_pairs={{0,8},{1,0},{2,10},{3,2},{4,12},{5,4},{6,14},{7,6},{8,9},{9,1},{10... | collective-permute-start | bytes 196616 | tf_op jit(solution)/shard_map/ppermute | solution.py:661
  35.4 6.2 %collective-permute-start.11 = (bf16[32,1024]{1,0:T(8,128)(2,1)S(1)}, bf16[32,1024]{1,0:T(8,128)(2,1)S(1)}, u32[]{:S(2)}, u32[]{:S(2)}) collective-permute-start(bf16[32,1024]{1,0:T(8,128)(2,1)S(1)} %get-tuple-element.36), channel_id=1, source_target_pairs={{0,12},{1,4},{2,14},{3,6},{4,8},{5,0},{6,10},{7,2},{8,13},{9,5},{1... | collective-permute-start | bytes 196616 | tf_op jit(solution)/shard_map/ppermute | solution.py:661
  36.3 5.3 %collective-permute-start.8 = (bf16[32,1024]{1,0:T(8,128)(2,1)S(1)}, bf16[32,1024]{1,0:T(8,128)(2,1)S(1)}, u32[]{:S(2)}, u32[]{:S(2)}) collective-permute-start(bf16[32,1024]{1,0:T(8,128)(2,1)S(1)} %get-tuple-element.33), channel_id=1, source_target_pairs={{0,0},{1,8},{2,2},{3,10},{4,4},{5,12},{6,6},{7,14},{8,1},{9,9},{10... | collective-permute-start | bytes 196616 | tf_op jit(solution)/shard_map/ppermute | solution.py:661
  37.2 4.5 %collective-permute-start.9 = (bf16[32,1024]{1,0:T(8,128)(2,1)S(1)}, bf16[32,1024]{1,0:T(8,128)(2,1)S(1)}, u32[]{:S(2)}, u32[]{:S(2)}) collective-permute-start(bf16[32,1024]{1,0:T(8,128)(2,1)S(1)} %get-tuple-element.34), channel_id=1, source_target_pairs={{0,4},{1,12},{2,6},{3,14},{4,0},{5,8},{6,2},{7,10},{8,5},{9,13},{1... | collective-permute-start | bytes 196616 | tf_op jit(solution)/shard_map/ppermute | solution.py:661
  42.4 8.9 %collective-permute-start.12 = (bf16[32,2176]{1,0:T(8,128)(2,1)S(1)}, bf16[32,2176]{1,0:T(8,128)(2,1)S(1)}, u32[]{:S(2)}, u32[]{:S(2)}) collective-permute-start(bf16[32,2176]{1,0:T(8,128)(2,1)S(1)} %get-tuple-element.38.refs_0_), channel_id=1, source_target_pairs={{0,4},{2,6},{4,0},{6,2},{8,12},{10,14},{12,8},{14,10},{1,5},{3,7},... | collective-permute-start | bytes 417800 | tf_op jit(solution)/shard_map/ppermute | solution.py:304
  43.5 14.7 %collective-permute-start.13 = (bf16[32,2176]{1,0:T(8,128)(2,1)S(1)}, bf16[32,2176]{1,0:T(8,128)(2,1)S(1)}, u32[]{:S(2)}, u32[]{:S(2)}) collective-permute-start(bf16[32,2176]{1,0:T(8,128)(2,1)S(1)} %get-tuple-element.38.refs_0_), channel_id=1, source_target_pairs={{0,12},{2,14},{4,8},{6,10},{8,4},{10,6},{12,0},{14,2},{1,13},{3,15... | collective-permute-start | bytes 417800 | tf_op jit(solution)/shard_map/ppermute | solution.py:304
  51.3 11.2 %collective-permute-start.21 = (bf16[32,2176]{1,0:T(8,128)(2,1)S(1)}, bf16[32,2176]{1,0:T(8,128)(2,1)S(1)}, u32[]{:S(2)}, u32[]{:S(2)}) collective-permute-start(bf16[32,2176]{1,0:T(8,128)(2,1)S(1)} %get-tuple-element.38.refs_0_), channel_id=1, source_target_pairs={{0,8},{2,10},{4,12},{6,14},{8,0},{10,2},{12,4},{14,6},{1,9},{3,11}... | collective-permute-start | bytes 417800 | tf_op jit(solution)/shard_map/ppermute | solution.py:304
  51.3 11.3 %collective-permute-start.14 = (bf16[32,2176]{1,0:T(8,128)(2,1)S(1)}, bf16[32,2176]{1,0:T(8,128)(2,1)S(1)}, u32[]{:S(2)}, u32[]{:S(2)}) collective-permute-start(bf16[32,2176]{1,0:T(8,128)(2,1)S(1)} %shard_map.121.refs_0_), channel_id=1, source_target_pairs={{0,2},{2,0},{4,6},{6,4},{8,10},{10,8},{12,14},{14,12},{1,3},{3,1},... | collective-permute-start | bytes 417800 | tf_op jit(solution)/shard_map/ppermute | solution.py:304
  58.2 4.5 %collective-permute-start.15 = (bf16[32,2176]{1,0:T(8,128)(2,1)S(1)}, bf16[32,2176]{1,0:T(8,128)(2,1)S(1)}, u32[]{:S(2)}, u32[]{:S(2)}) collective-permute-start(bf16[32,2176]{1,0:T(8,128)(2,1)S(1)} %collective-permute-done.13.refs_1_), channel_id=1, source_target_pairs={{0,2},{2,0},{4,6},{6,4},{8,10},{10,8},{12,14},{14,12},{1,3},{3,1},... | collective-permute-start | bytes 417800 | tf_op jit(solution)/shard_map/ppermute | solution.py:304
  58.2 8.1 %collective-permute-start.22 = (bf16[32,2176]{1,0:T(8,128)(2,1)S(1)}, bf16[32,2176]{1,0:T(8,128)(2,1)S(1)}, u32[]{:S(2)}, u32[]{:S(2)}) collective-permute-start(bf16[32,2176]{1,0:T(8,128)(2,1)S(1)} %get-tuple-element.38.refs_0_), channel_id=1, source_target_pairs={{0,2},{2,0},{4,6},{6,4},{8,10},{10,8},{12,14},{14,12},{1,3},{3,1},... | collective-permute-start | bytes 417800 | tf_op jit(solution)/shard_map/ppermute | solution.py:304
  62.6 3.7 %collective-permute-start.23 = (bf16[32,2176]{1,0:T(8,128)(2,1)S(1)}, bf16[32,2176]{1,0:T(8,128)(2,1)S(1)}, u32[]{:S(2)}, u32[]{:S(2)}) collective-permute-start(bf16[32,2176]{1,0:T(8,128)(2,1)S(1)} %shard_map.126.refs_1_), channel_id=1, source_target_pairs={{0,2},{2,0},{4,6},{6,4},{8,10},{10,8},{12,14},{14,12},{1,3},{3,1},... | collective-permute-start | bytes 417800 | tf_op jit(solution)/shard_map/ppermute | solution.py:304
  65.1 12.8 %collective-permute-start.16 = (bf16[128,1664]{1,0:T(8,128)(2,1)S(1)}, bf16[128,1664]{1,0:T(8,128)(2,1)S(1)}, u32[]{:S(2)}, u32[]{:S(2)}) collective-permute-start(bf16[128,1664]{1,0:T(8,128)(2,1)S(1)} %get-tuple-element.41), channel_id=1, source_target_pairs={{0,1},{1,0},{2,3},{3,2},{4,5},{5,4},{6,7},{7,6},{8,9},{9,8},{10,11... | collective-permute-start | bytes 1277960 | tf_op jit(solution)/shard_map/ppermute | solution.py:304
  68.7 18.3 %collective-permute-start.24 = (bf16[128,1664]{1,0:T(8,128)(2,1)S(1)}, bf16[128,1664]{1,0:T(8,128)(2,1)S(1)}, u32[]{:S(2)}, u32[]{:S(2)}) collective-permute-start(bf16[128,1664]{1,0:T(8,128)(2,1)S(1)} %get-tuple-element.49), channel_id=1, source_target_pairs={{0,1},{1,0},{2,3},{3,2},{4,5},{5,4},{6,7},{7,6},{8,9},{9,8},{10,11... | collective-permute-start | bytes 1277960 | tf_op jit(solution)/shard_map/ppermute | solution.py:304
  78.6 12.5 %collective-permute-start.17 = (bf16[128,768]{1,0:T(8,128)(2,1)S(1)}, bf16[128,768]{1,0:T(8,128)(2,1)S(1)}, u32[]{:S(2)}, u32[]{:S(2)}) collective-permute-start(bf16[128,768]{1,0:T(8,128)(2,1)S(1)} %shard_map.123.act_ref), channel_id=1, source_target_pairs={{0,1},{1,0},{2,3},{3,2},{4,5},{5,4},{6,7},{7,6},{8,9},{9,8},{10,11... | collective-permute-start | bytes 589832 | tf_op jit(solution)/shard_map/ppermute | solution.py:304
  87.8 7.1 %collective-permute-start.25 = (bf16[128,768]{1,0:T(8,128)(2,1)S(1)}, bf16[128,768]{1,0:T(8,128)(2,1)S(1)}, u32[]{:S(2)}, u32[]{:S(2)}) collective-permute-start(bf16[128,768]{1,0:T(8,128)(2,1)S(1)} %shard_map.128.act_ref), channel_id=1, source_target_pairs={{0,1},{1,0},{2,3},{3,2},{4,5},{5,4},{6,7},{7,6},{8,9},{9,8},{10,11... | collective-permute-start | bytes 589832 | tf_op jit(solution)/shard_map/ppermute | solution.py:304
  92.7 3.8 %collective-permute-start.18 = (bf16[64,2048]{1,0:T(8,128)(2,1)S(1)}, bf16[64,2048]{1,0:T(8,128)(2,1)S(1)}, u32[]{:S(2)}, u32[]{:S(2)}) collective-permute-start(bf16[64,2048]{1,0:T(8,128)(2,1)S(1)} %get-tuple-element.45), channel_id=1, source_target_pairs={{0,2},{2,0},{4,6},{6,4},{8,10},{10,8},{12,14},{14,12},{1,3},{3,1},... | collective-permute-start | bytes 786440 | tf_op jit(solution)/shard_map/ppermute | solution.py:304
  96.5 2.3 %collective-permute-start.26 = (bf16[64,2048]{1,0:T(8,128)(2,1)S(1)}, bf16[64,2048]{1,0:T(8,128)(2,1)S(1)}, u32[]{:S(2)}, u32[]{:S(2)}) collective-permute-start(bf16[64,2048]{1,0:T(8,128)(2,1)S(1)} %get-tuple-element.52), channel_id=1, source_target_pairs={{0,2},{2,0},{4,6},{6,4},{8,10},{10,8},{12,14},{14,12},{1,3},{3,1},... | collective-permute-start | bytes 786440 | tf_op jit(solution)/shard_map/ppermute | solution.py:304
  96.6 6.0 %collective-permute-start.19 = (bf16[32,2048]{1,0:T(8,128)(2,1)S(1)}, bf16[32,2048]{1,0:T(8,128)(2,1)S(1)}, u32[]{:S(2)}, u32[]{:S(2)}) collective-permute-start(bf16[32,2048]{1,0:T(8,128)(2,1)S(1)} %get-tuple-element.46), channel_id=1, source_target_pairs={{0,4},{2,6},{4,0},{6,2},{8,12},{10,14},{12,8},{14,10},{1,5},{3,7},... | collective-permute-start | bytes 393224 | tf_op jit(solution)/shard_map/ppermute | solution.py:304
  96.7 9.2 %collective-permute-start.20 = (bf16[32,2048]{1,0:T(8,128)(2,1)S(1)}, bf16[32,2048]{1,0:T(8,128)(2,1)S(1)}, u32[]{:S(2)}, u32[]{:S(2)}) collective-permute-start(bf16[32,2048]{1,0:T(8,128)(2,1)S(1)} %get-tuple-element.47), channel_id=1, source_target_pairs={{0,12},{2,14},{4,8},{6,10},{8,4},{10,6},{12,0},{14,2},{1,13},{3,15... | collective-permute-start | bytes 393224 | tf_op jit(solution)/shard_map/ppermute | solution.py:304
  98.8 13.4 %collective-permute-start.27 = (bf16[32,2048]{1,0:T(8,128)(2,1)S(1)}, bf16[32,2048]{1,0:T(8,128)(2,1)S(1)}, u32[]{:S(2)}, u32[]{:S(2)}) collective-permute-start(bf16[32,2048]{1,0:T(8,128)(2,1)S(1)} %get-tuple-element.54), channel_id=1, source_target_pairs={{0,8},{2,10},{4,12},{6,14},{8,0},{10,2},{12,4},{14,6},{1,9},{3,11}... | collective-permute-start | bytes 393224 | tf_op jit(solution)/shard_map/ppermute | solution.py:304
